TPU v7x, 768 devices: a whole 4x8x12 slice. The times are simulated.
768 devices in a mesh: dp: 12 (over z), fsdp: 64 (over y, x, core).
Axes of the slice: x: 4, y: 8, z: 12, core: 2. Of those that a mesh axis runs over, the one named last changes fastest.
Arguments:
- hidden: bfloat16 [196608, 4096], P(('dp', 'fsdp')), may hold values from -6 to 6
- queries: bfloat16 [196608, 2048], P(('dp', 'fsdp')), may hold values from -6 to 6
- keys: bfloat16 [196608, 512], P(('dp', 'fsdp')), may hold values from -6 to 6
- target: bfloat16 [196608, 2048], P(('dp', 'fsdp')), may hold values from -6 to 6
- lengths: int32 [768], P(('dp', 'fsdp')), may hold values from 64 to 256
- value_weight_frozen: bfloat16 [4096, 512], P('fsdp'), may hold values from -0.09375 to 0.09375
- adapter_down_map: float32 [4096, 64], P('fsdp'), may hold values from -0.09375 to 0.09375
- adapter_up_map: float32 [64, 512], replicated, may hold values from -0.75 to 0.75
- average_down_map: float32 [4096, 64], P('fsdp'), may hold values from -0.09375 to 0.09375
- average_up_map: float32 [64, 512], replicated, may hold values from -0.75 to 0.75
Outputs:
- down_map_gradient: float32 [4096, 64], P('fsdp')
- up_map_gradient: float32 [64, 512], replicated
- average_down_next: float32 [4096, 64], P('fsdp')
- average_up_next: float32 [64, 512], replicated
- loss: float32 [], replicated
Inputs may be any that keep to these rules, and one draw needn't show every extreme that they name: `lengths`: slots at or past a sequence's length are padding.
All inputs are finite; a program needn't handle non-finite values.
Results may differ from a plain program's by a relative error of at most 0.0049.
Values may be sent and summed in bfloat16 or wider, within the bound.
No kernel may reach another device: no remote copies, remote signals or barrier semaphores. Data moves between devices by JAX's collectives and lax.ppermute only.
A program may use at most 64 MiB of HBM per device.

v0:
```python
import math

import jax
import jax.numpy as jnp
from jax import lax
from jax.sharding import PartitionSpec as P

HEADS = 16
KEY_VALUE_HEADS = 4
HEAD_DIM = 128


adapter_scale = 2.0
average_decay = 0.9
learning_rate = 1.0
masked_score = -1e30


def side_by_side(arrays, axis, dim, along):
    both = jnp.concatenate(arrays, axis=along)
    filled, at, finished = (lax.all_gather(both, axis, axis=dim, tiled=True), 0, [])
    for a in arrays:
        finished.append(lax.slice_in_dim(filled, at, at + a.shape[along], axis=along))
        at += a.shape[along]
    return tuple(finished)


def split_up(shard, dim, length):
    before, after = (shard.shape[:dim], shard.shape[dim + 1 :])
    return jnp.moveaxis(shard.reshape(*before, length, -1, *after), dim, 0)


def summed_on_arrival(shard, axis, dim):
    blocks = split_up(shard, dim, lax.axis_size(axis))
    arrived = lax.all_to_all(blocks, axis, split_axis=0, concat_axis=0, tiled=True)
    return arrived.sum(axis=0)


def from_everyone(shard, axis):
    length = lax.axis_size(axis)
    return lax.all_to_all(
        jnp.broadcast_to(shard[None], (length, *shard.shape)), axis, 0, 0, tiled=True
    )


def over_copies(shard, axis):
    return from_everyone(shard, axis).sum(axis=0)


def together(arrays, axis):
    vector, at, finished = (jnp.concatenate([a.reshape(-1) for a in arrays]), 0, [])
    subtotal = lax.psum(vector, axis)
    for a in arrays:
        finished.append(subtotal[at : at + a.size].reshape(a.shape))
        at += a.size
    return tuple(finished)


def per_device(
    hidden,
    queries,
    keys,
    target,
    lengths,
    value_weight_frozen,
    adapter_down_map,
    adapter_up_map,
    average_down_map,
    average_up_map,
):
    tok_rows = hidden.shape[0]
    group_size = HEADS // KEY_VALUE_HEADS
    seq_length = lengths[0]
    down_factor_slice = adapter_down_map.astype(jnp.bfloat16)
    up_factor_slice = adapter_up_map.astype(jnp.bfloat16)
    pieces = side_by_side((value_weight_frozen, down_factor_slice), "fsdp", 0, 1)
    columns = hidden
    frozen_value_output = jnp.dot(columns, pieces[0], preferred_element_type=jnp.float32)
    adapter_hidden = jnp.dot(columns, pieces[1], preferred_element_type=jnp.float32)
    adapter_hidden = adapter_hidden.astype(jnp.bfloat16)
    value_outputs = (
        frozen_value_output
        + adapter_scale
        * jnp.dot(adapter_hidden, up_factor_slice, preferred_element_type=jnp.float32)
    ).astype(jnp.bfloat16)
    position = jnp.arange(tok_rows, dtype=jnp.int32)
    allowed = (position[None, :] <= position[:, None]) & (position[None, :] < seq_length)
    q_heads = queries.reshape(tok_rows, KEY_VALUE_HEADS, group_size, HEAD_DIM)
    k_heads = keys.reshape(tok_rows, KEY_VALUE_HEADS, HEAD_DIM)
    v_heads = value_outputs.reshape(tok_rows, KEY_VALUE_HEADS, HEAD_DIM)
    scores = jnp.einsum(
        "tkgd,skd->kgts", q_heads, k_heads, preferred_element_type=jnp.float32
    ) / math.sqrt(HEAD_DIM)
    scores = jnp.where(allowed, scores, masked_score)
    row_max = jnp.max(scores, axis=-1, keepdims=True)
    weights = jnp.exp(scores - row_max)
    attn_probs = (weights / jnp.sum(weights, axis=-1, keepdims=True)).astype(jnp.bfloat16)
    output = jnp.einsum(
        "kgts,skd->tkgd", attn_probs, v_heads, preferred_element_type=jnp.float32
    ).reshape(tok_rows, HEADS * HEAD_DIM)
    live_rows = (position < seq_length)[:, None]
    differ = jnp.where(live_rows, output - target.astype(jnp.float32), 0.0)
    loss_local = jnp.sum(differ * differ)
    cotangent = differ.astype(jnp.bfloat16).reshape(tok_rows, KEY_VALUE_HEADS, group_size, HEAD_DIM)
    value_grad = jnp.einsum(
        "kgts,tkgd->skd", attn_probs, cotangent, preferred_element_type=jnp.float32
    )
    value_grad = value_grad.reshape(tok_rows, KEY_VALUE_HEADS * HEAD_DIM).astype(jnp.bfloat16)
    latent_grad = lax.dot_general(
        value_grad, up_factor_slice, (((1,), (1,)), ((), ())), preferred_element_type=jnp.float32
    ).astype(jnp.bfloat16)
    up_term = lax.dot_general(
        adapter_hidden, value_grad, (((0,), (0,)), ((), ())), preferred_element_type=jnp.float32
    )
    count_local = seq_length.astype(jnp.float32)
    columns = hidden
    down_map_gradient = summed_on_arrival(
        adapter_scale
        * lax.dot_general(
            columns, latent_grad, (((0,), (0,)), ((), ())), preferred_element_type=jnp.float32
        ),
        "fsdp",
        0,
    )
    down_map_gradient = over_copies(down_map_gradient, "dp")
    up_map_gradient, loss_sum, token_grand_count = together(
        (adapter_scale * up_term, loss_local, count_local), ("dp", "fsdp")
    )
    up_map_gradient = up_map_gradient / token_grand_count
    down_map_gradient = down_map_gradient / token_grand_count
    loss = loss_sum / (2.0 * token_grand_count)
    average_down_next = average_decay * average_down_map + (1.0 - average_decay) * (
        adapter_down_map - learning_rate * down_map_gradient
    )
    average_up_next = average_decay * average_up_map + (1.0 - average_decay) * (
        adapter_up_map - learning_rate * up_map_gradient
    )
    return (down_map_gradient, up_map_gradient, average_down_next, average_up_next, loss)


def solution(mesh):
    placed = (
        P(("dp", "fsdp"), None),
        P(("dp", "fsdp"), None),
        P(("dp", "fsdp"), None),
        P(("dp", "fsdp"), None),
        P(("dp", "fsdp")),
        P("fsdp", None),
        P("fsdp", None),
        P(),
        P("fsdp", None),
        P(),
    )
    return jax.shard_map(
        per_device,
        mesh=mesh,
        in_specs=placed,
        out_specs=(P("fsdp", None), P(), P("fsdp", None), P(), P()),
        check_vma=False,
    )
```

profile of v0, /device:TPU:1, one launch (start us, length us, event | category | flops | bytes accessed | tf_op | source)
XLA Modules:
  0.0 656.6 jit_solution(2038996036068490343)
XLA Ops:
  8.1 1.5 pad_maximum_fusion
  10.3 1.8 reshape.62
  13.9 1.2 fusion.27
  15.2 1.8 divide_convert_fusion
  17.0 93.9 %all-gather.2.cloned.1.call-done = bf16[4096,576]{1,0:T(8,128)(2,1)} async-done(((bf16[64,576]{1,0:T(8,128)(2,1)}), bf16[4096,576]{1,0:T(8,128)(2,1)}) %all-gather.2.cloned.1.call-update) | async-done | bytes 4718608 | tf_op jit(solution)/shard_map/all_gather | solution.py:21
  110.9 2.0 convolution_convert_fusion.1
  112.9 3.6 fusion.9
  116.8 1.8 fusion.28
  118.6 3.0 copy.36
  121.6 3.6 multiply_reduce_fusion
  125.3 1.5 copy.50
  126.8 2.4 fusion.14
  129.8 2.1 reshape.65
  132.0 4.1 copy.58
  136.1 3.5 reshape.74
  139.6 6.0 all-to-all-start
  146.8 1.4 concatenate.7
  148.2 465.8 %all-reduce.2.cloned.1.call-done = f32[32770]{0:T(1024)} async-done(((f32[32770]{0:T(1024)}), f32[32770]{0:T(1024)}) %all-reduce.2.cloned.1.call-update) | async-done | bytes 131096 | tf_op jit(solution)/shard_map/psum | solution.py:52
  614.0 1.3 fusion.26
  616.8 4.4 reduce
  621.2 2.2 reshape.75
  623.3 1.8 bitcast_reduce_fusion
  626.2 6.8 %all-to-all-start.1 = ((f32[12,1,4096]{2,1,0:T(1,128)}), f32[12,1,4096]{2,1,0:T(1,128)S(1)}, u32[]{:S(2)}, u32[]{:S(2)}) async-start(f32[12,1,4096]{2,1,0:T(1,128)} %reshape.76), calls=%async_computation.1 | async-start | bytes 393216 | tf_op jit(solution)/shard_map/all_to_all | solution.py:41
  635.6 10.5 %all-to-all-done.1 = f32[12,1,4096]{2,1,0:T(1,128)S(1)} async-done(((f32[12,1,4096]{2,1,0:T(1,128)}), f32[12,1,4096]{2,1,0:T(1,128)S(1)}, u32[]{:S(2)}, u32[]{:S(2)}) %all-to-all-start.1) | async-done | bytes 196640 | tf_op jit(solution)/shard_map/all_to_all | solution.py:41
  (47 shorter events, 11.3 us)
Async XLA Ops:
  7.2 103.7 %copy-start = (bf16[256,4096]{1,0:T(8,128)(2,1)S(1)}, bf16[256,4096]{1,0:T(8,128)(2,1)}, u32[]{:S(2)}) copy-start(bf16[256,4096]{1,0:T(8,128)(2,1)} %param.10) | copy-start | bytes 6291460
  7.2 103.7 %all-gather.2.cloned.1.call-start = ((), (), s32[]{:S(2)}) async-start(), calls=%async_computation.2 | async-start | bytes 5324800 | tf_op jit(solution)/shard_map/all_gather | solution.py:21
  112.8 3.7 copy-start.6
  112.9 3.7 copy-start.3
  112.9 4.0 copy-start.1
  118.6 3.0 copy-start.4
  139.6 475.7 %all-to-all-start = ((f32[64,1,4096]{2,1,0:T(1,128)}), f32[64,1,4096]{2,1,0:T(1,128)S(1)}, u32[]{:S(2)}, u32[]{:S(2)}) async-start(f32[64,1,4096]{2,1,0:T(1,128)} %reshape.74), calls=%async_computation | async-start | bytes 2097152 | tf_op jit(solution)/shard_map/all_to_all | solution.py:35
  145.6 468.4 %all-reduce.2.cloned.1.call-start = ((), (), s32[]{:S(2)}) async-start(), calls=%async_computation.3 | async-start | bytes 270336 | tf_op jit(solution)/shard_map/psum | solution.py:52
  615.3 1.0 copy-start.2
  623.3 9.7 %copy-start.9 = (f32[32770]{0:T(1024)S(1)}, f32[32770]{0:T(1024)}, u32[]{:S(2)}) copy-start(f32[32770]{0:T(1024)} %all-reduce.2.cloned.1.call-done) | copy-start | bytes 393244
  623.3 11.6 %copy-start.8 = (f32[64,512]{1,0:T(8,128)S(1)}, f32[64,512]{1,0:T(8,128)}, u32[]{:S(2)}) copy-start(f32[64,512]{1,0:T(8,128)} %param.19) | copy-start | bytes 393220
  625.2 22.2 %copy-start.7 = (f32[64,64]{1,0:T(8,128)S(1)}, f32[64,64]{1,0:T(8,128)}, u32[]{:S(2)}) copy-start(f32[64,64]{1,0:T(8,128)} %param.16) | copy-start | bytes 49156
  625.2 22.2 %copy-start.10 = (f32[64,64]{1,0:T(8,128)S(1)}, f32[64,64]{1,0:T(8,128)}, u32[]{:S(2)}) copy-start(f32[64,64]{1,0:T(8,128)} %param.18) | copy-start | bytes 49156
  626.2 19.9 %all-to-all-start.1 = ((f32[12,1,4096]{2,1,0:T(1,128)}), f32[12,1,4096]{2,1,0:T(1,128)S(1)}, u32[]{:S(2)}, u32[]{:S(2)}) async-start(f32[12,1,4096]{2,1,0:T(1,128)} %reshape.76), calls=%async_computation.1 | async-start | bytes 393216 | tf_op jit(solution)/shard_map/all_to_all | solution.py:41
  634.2 14.4 %copy-start.5 = (f32[64,512]{1,0:T(8,128)}, f32[64,512]{1,0:T(8,128)S(1)}, u32[]{:S(2)}) copy-start(f32[64,512]{1,0:T(8,128)S(1)} %div.43) | copy-start | bytes 393220
Sparse Core Ops, SparseCore 0:
  12.5 98.3 all-gather.1
  151.8 462.1 all-reduce.1
where the time goes:
time: 657 us
  waiting for transfers between devices  570 us (87%)
  local copies, waits for them, and re-layouts  24.7 us (4%)
  other arithmetic  19 us (3%)
  between operations  17.3 us (3%)
  starting transfers between devices  13.1 us (2%)
  matrix products  12.4 us (2%)
    psum x1, waiting for transfers between devices, together(): subtotal = lax.psum(vector, axis)  466 us
    all_gather x1, waiting for transfers between devices, side_by_side(): lax.all_gather(both, axis, axis=dim, tiled=True)  93.9 us
  transfers between devices with their start and end apart: 4, of which 3 were waited for; matrix products, arithmetic and copies ran while one was open for 2% of the time, Pallas kernels for 0%

commit v1 on v0

v1 whole, which is shorter than its diff:
```python
import math

import jax
import jax.numpy as jnp
from jax import lax
from jax.experimental import pallas as pl
from jax.experimental.pallas import tpu as pltpu
from jax.sharding import PartitionSpec as P

HEADS = 16
KEY_VALUE_HEADS = 4
HEAD_DIM = 128
GROUP = HEADS // KEY_VALUE_HEADS
TOK = 256
MODEL = 4096
RANK = 64
KV_WIDTH = KEY_VALUE_HEADS * HEAD_DIM

adapter_scale = 2.0
average_decay = 0.9
learning_rate = 1.0
masked_score = -1e30

PIECE_ROWS = 40
CHUNKS = 8


def nt(a, b):
    return lax.dot_general(a, b, (((1,), (1,)), ((), ())), preferred_element_type=jnp.float32)


def nn(a, b):
    return lax.dot_general(a, b, (((1,), (0,)), ((), ())), preferred_element_type=jnp.float32)


def probs_kernel(length_ref, q_ref, k_ref, p_ref, pt_ref):
    length = length_ref[0]
    keys = k_ref[...]
    row = lax.broadcasted_iota(jnp.int32, (TOK, TOK), 0)
    col = lax.broadcasted_iota(jnp.int32, (TOK, TOK), 1)
    allowed = (col <= row) & (col < length)
    for g in range(GROUP):
        scores = nt(q_ref[:, g * HEAD_DIM : (g + 1) * HEAD_DIM], keys) * (1.0 / math.sqrt(HEAD_DIM))
        scores = jnp.where(allowed, scores, masked_score)
        weights = jnp.exp(scores - jnp.max(scores, axis=-1, keepdims=True))
        probs = weights * (1.0 / jnp.sum(weights, axis=-1, keepdims=True))
        p_ref[0, g * TOK : (g + 1) * TOK, :] = probs.astype(jnp.bfloat16)
        pt_ref[0, :, g * TOK : (g + 1) * TOK] = jnp.transpose(probs).astype(jnp.bfloat16)


def attention_probs(lengths, queries, keys):
    shape = jax.ShapeDtypeStruct
    return pl.pallas_call(
        probs_kernel,
        grid=(KEY_VALUE_HEADS,),
        in_specs=[
            pl.BlockSpec(memory_space=pltpu.SMEM),
            pl.BlockSpec((TOK, GROUP * HEAD_DIM), lambda h: (0, h)),
            pl.BlockSpec((TOK, HEAD_DIM), lambda h: (0, h)),
        ],
        out_specs=[
            pl.BlockSpec((1, GROUP * TOK, TOK), lambda h: (h, 0, 0)),
            pl.BlockSpec((1, TOK, GROUP * TOK), lambda h: (h, 0, 0)),
        ],
        out_shape=[
            shape((KEY_VALUE_HEADS, GROUP * TOK, TOK), jnp.bfloat16),
            shape((KEY_VALUE_HEADS, TOK, GROUP * TOK), jnp.bfloat16),
        ],
        compiler_params=pltpu.CompilerParams(vmem_limit_bytes=16 * 2**20),
        cost_estimate=pl.CostEstimate(flops=2**31, bytes_accessed=6 * 2**20, transcendentals=2**20),
        name="probs",
    )(lengths, queries, keys)


def grads_kernel(
    facts_ref, hidden, own_hbm, other_hbm, probs, probs_t, target, up_ref, out_ref,
    weight, cot, value_grad, sems,
):
    length, core = facts_ref[0], facts_ref[1]
    columns, rows = own_hbm.shape[0], own_hbm.shape[1]
    step = MODEL // rows
    loads = []
    for c in range(rows):
        copies = []
        for x in range(columns):
            base = c * step + x * 2 * RANK
            for i, (source, side) in enumerate(((own_hbm, core), (other_hbm, 1 - core))):
                place = pl.ds(pl.multiple_of(base + side * RANK, RANK), RANK)
                copies.append(pltpu.make_async_copy(source.at[x, c], weight.at[place, :], sems.at[c, 2 * x + i]))
        loads.append(copies)
    for copies in loads:
        for copy in copies:
            copy.start()

    up = up_ref[...].astype(jnp.bfloat16)
    total = None
    for c in range(rows):
        for copy in loads[c]:
            copy.wait()
        part = nn(hidden[:, c * step : (c + 1) * step], weight[c * step : (c + 1) * step, :])
        total = part if total is None else total + part
    latent = total[:, KV_WIDTH:].astype(jnp.bfloat16)
    values = (total[:, :KV_WIDTH] + adapter_scale * nn(latent, up)).astype(jnp.bfloat16)

    live = lax.broadcasted_iota(jnp.int32, (TOK, HEAD_DIM), 0) < length
    squares = jnp.zeros((TOK, HEAD_DIM), jnp.float32)
    for k in range(KEY_VALUE_HEADS):
        output = nn(probs[k], values[:, k * HEAD_DIM : (k + 1) * HEAD_DIM])
        for g in range(GROUP):
            h = k * GROUP + g
            aim = target[:, h * HEAD_DIM : (h + 1) * HEAD_DIM].astype(jnp.float32)
            differ = jnp.where(live, output[g * TOK : (g + 1) * TOK, :] - aim, 0.0)
            squares = squares + differ * differ
            cot[g * TOK : (g + 1) * TOK, :] = differ.astype(jnp.bfloat16)
        value_grad[:, k * HEAD_DIM : (k + 1) * HEAD_DIM] = nn(probs_t[k], cot[...]).astype(jnp.bfloat16)

    grad = value_grad[...]
    latent_grad_t = nt(up, grad).astype(jnp.bfloat16)
    up_term = lax.dot_general(latent, grad, (((0,), (0,)), ((), ())), preferred_element_type=jnp.float32)

    lane = lax.broadcasted_iota(jnp.int32, (RANK // 2, HEAD_DIM), 1) < RANK
    for m in range(MODEL // 512):
        term = nn(latent_grad_t, hidden[:, m * 512 : (m + 1) * 512])
        for i in range(4):
            a = term[: RANK // 2, i * 128 : (i + 1) * 128]
            b = term[RANK // 2 :, i * 128 : (i + 1) * 128]
            even = jnp.where(lane, a, pltpu.roll(b, RANK, 1))
            odd = jnp.where(lane, pltpu.roll(a, RANK, 1), b)
            out_ref[m * 8 + 2 * i, :32, :] = even.astype(jnp.bfloat16)
            out_ref[m * 8 + 2 * i + 1, :32, :] = odd.astype(jnp.bfloat16)

    loss = jnp.sum(jnp.sum(squares, axis=0, keepdims=True), axis=1, keepdims=True)
    high = loss.astype(jnp.bfloat16).astype(jnp.float32)
    sub8 = lax.broadcasted_iota(jnp.int32, (8, HEAD_DIM), 0)
    lane8 = lax.broadcasted_iota(jnp.int32, (8, HEAD_DIM), 1)
    count = jnp.full((8, HEAD_DIM), length, jnp.int32).astype(jnp.float32)
    facts = jnp.where(lane8 == 0, high, jnp.where(lane8 == 1, loss - high, jnp.where(lane8 == 2, count, 0.0)))
    for q in range(8):
        for b in range(4):
            tile = up_term[8 * q : 8 * q + 8, b * 128 : (b + 1) * 128]
            out_ref[8 * q + b, 32:, :] = jnp.where(sub8 < 4, tile, facts).astype(jnp.bfloat16)
            out_ref[8 * q + 4 + b, 32:, :] = jnp.where(sub8 < 4, pltpu.roll(tile, 4, 0), facts).astype(jnp.bfloat16)


def gradient_pieces(facts, hidden, own, other, probs, probs_t, target, up_map):
    vmem = pl.BlockSpec(memory_space=pltpu.VMEM)
    hbm = pl.BlockSpec(memory_space=pltpu.HBM)
    width = own.shape[-1]
    return pl.pallas_call(
        grads_kernel,
        in_specs=[pl.BlockSpec(memory_space=pltpu.SMEM), vmem, hbm, hbm, vmem, vmem, vmem, vmem],
        out_specs=vmem,
        out_shape=jax.ShapeDtypeStruct((MODEL // RANK, PIECE_ROWS, HEAD_DIM), jnp.bfloat16),
        scratch_shapes=[
            pltpu.VMEM((MODEL, width), jnp.bfloat16),
            pltpu.VMEM((GROUP * TOK, HEAD_DIM), jnp.bfloat16),
            pltpu.VMEM((TOK, KV_WIDTH), jnp.bfloat16),
            pltpu.SemaphoreType.DMA((own.shape[1], 2 * own.shape[0])),
        ],
        compiler_params=pltpu.CompilerParams(vmem_limit_bytes=32 * 2**20),
        cost_estimate=pl.CostEstimate(flops=2**32, bytes_accessed=14 * 2**20, transcendentals=0),
        name="grads",
    )(facts, hidden, own, other, probs, probs_t, target, up_map)


def fold_kernel(pieces_ref, out_ref):
    total = jnp.sum(pieces_ref[...].astype(jnp.float32), axis=0)
    for d in range(out_ref.shape[0]):
        out_ref[d] = total


def fold(pieces, copies):
    return pl.pallas_call(
        fold_kernel,
        out_shape=jax.ShapeDtypeStruct((copies, PIECE_ROWS, HEAD_DIM), jnp.float32),
        name="fold",
    )(pieces)


def owner_kernel(pieces_ref, down_ref, average_ref, grad_ref, next_ref, up_ref, loss_ref):
    total = jnp.sum(pieces_ref[...], axis=0)
    count = total[36:37, 2:3]
    loss_ref[...] = (total[36:37, 0:1] + total[36:37, 1:2]) / (2.0 * count)
    factor = adapter_scale / count
    rows = jnp.concatenate([total[:32, :RANK], total[:32, RANK:]], axis=0)
    grad = jnp.transpose(rows) * factor
    grad_ref[...] = grad
    next_ref[...] = average_decay * average_ref[...] + (1.0 - average_decay) * (down_ref[...] - learning_rate * grad)
    up_ref[0] = total[32:36, :] * factor


def owner_update(pieces, down_map, average_down_map):
    shape = jax.ShapeDtypeStruct
    return pl.pallas_call(
        owner_kernel,
        out_shape=[
            shape((RANK, RANK), jnp.float32),
            shape((RANK, RANK), jnp.float32),
            shape((1, 4, HEAD_DIM), jnp.float32),
            shape((1, 1), jnp.float32),
        ],
        name="owner",
    )(pieces, down_map, average_down_map)


def second_kernel(pieces_ref, up_ref, average_ref, grad_ref, next_ref):
    for j in range(MODEL // RANK):
        q, b = divmod(j, 4)
        grad_ref[4 * q : 4 * q + 4, b * 128 : (b + 1) * 128] = pieces_ref[j]
    next_ref[...] = average_decay * average_ref[...] + (1.0 - average_decay) * (
        up_ref[...] - learning_rate * grad_ref[...]
    )


def second_update(pieces, up_map, average_up_map):
    shape = jax.ShapeDtypeStruct((RANK, KV_WIDTH), jnp.float32)
    return pl.pallas_call(second_kernel, out_shape=[shape, shape], name="second")(pieces, up_map, average_up_map)


def exchange(pieces, axis):
    return lax.all_to_all(pieces, axis, 0, 0, tiled=True)


def along_y(owners):
    return [list(range(k, owners, 8)) for k in range(8)]


def along_x(owners):
    return [[y * 8 + x * 2 + core for x in range(4)] for y in range(owners // 8) for core in range(2)]


def gathered(shard, groups):
    copies = jnp.broadcast_to(shard[None], (len(groups[0]), *shard.shape))
    return lax.all_to_all(copies, "fsdp", 0, 0, tiled=True, axis_index_groups=groups)


def per_device(
    hidden,
    queries,
    keys,
    target,
    lengths,
    value_weight_frozen,
    adapter_down_map,
    adapter_up_map,
    average_down_map,
    average_up_map,
):
    owners, replicas = lax.axis_size("fsdp"), lax.axis_size("dp")
    core = lax.axis_index("fsdp").astype(jnp.int32) % 2
    facts = jnp.stack([lengths[0], core])
    both = jnp.concatenate([value_weight_frozen, adapter_down_map.astype(jnp.bfloat16)], axis=1)
    own = gathered(gathered(both, along_y(owners)), along_x(owners))
    other = lax.ppermute(own, "fsdp", [(i, i ^ 1) for i in range(owners)])
    probs, probs_t = attention_probs(lengths, queries, keys)
    pieces = gradient_pieces(facts, hidden, own, other, probs, probs_t, target, adapter_up_map)
    summed = fold(exchange(pieces, "fsdp"), replicas)
    down_grad, average_down_next, up_piece, loss = owner_update(
        exchange(summed, "dp"), adapter_down_map, average_down_map
    )
    up_pieces = exchange(jnp.broadcast_to(up_piece, (owners, 4, HEAD_DIM)), "fsdp")
    up_grad, average_up_next = second_update(up_pieces, adapter_up_map, average_up_map)
    return (down_grad, up_grad, average_down_next, average_up_next, loss.reshape(()))


def solution(mesh):
    placed = (
        P(("dp", "fsdp"), None),
        P(("dp", "fsdp"), None),
        P(("dp", "fsdp"), None),
        P(("dp", "fsdp"), None),
        P(("dp", "fsdp")),
        P("fsdp", None),
        P("fsdp", None),
        P(),
        P("fsdp", None),
        P(),
    )
    return jax.shard_map(
        per_device,
        mesh=mesh,
        in_specs=placed,
        out_specs=(P("fsdp", None), P(), P("fsdp", None), P(), P()),
        check_vma=False,
    )
```

time: 657 us -> 162 us (0.25)
  waiting for transfers between devices: 570 us -> 0.01 us
  blocking collectives: 0 us -> 132 us
  local copies, waits for them, and re-layouts: 24.7 us -> 2.34 us
  Pallas kernels: 0 us -> 18.5 us
  other arithmetic: 19 us -> 1.69 us
  between operations: 17.3 us -> 1.38 us
  matrix products: 12.4 us -> 0 us
  starting transfers between devices: 13.1 us -> 5.12 us
    psum x1 -> x0, waiting for transfers between devices: 466 us -> none  [together(): subtotal = lax.psum(vector, axis)]
    all_to_all x0 -> x5, blocking collectives: none -> 132 us  [the longest x3 71.8 us: exchange(): return lax.all_to_all(pieces, axis, 0, 0, tiled=True)]
    all_gather x1 -> x0, waiting for transfers between devices: 93.9 us -> none  [side_by_side(): lax.all_gather(both, axis, axis=dim, tiled=True)]
    pallas_call x0 -> x5, Pallas kernels: none -> 18.5 us  [the longest x1 10.1 us: gradient_pieces(): pl.pallas_call(grads_kernel, in_specs=[pl.BlockSpec(memory_space=pltpu.SM...]
    reshape x6 -> x0, local copies, waits for them, and re-layouts: 13.6 us -> none  [the longest x2 6.29 us: split_up(): return jnp.moveaxis(shard.reshape(*before, length, -1, *after), dim, 0)]
    all_to_all x2 -> x0, starting transfers between devices: 12.8 us -> none  [the longest x1 6.85 us: from_everyone(): lax.all_to_all(jnp.broadcast_to(shard[None], (length, *shard.shape)), axi...]
    dot_general x8 -> x0, matrix products: 12.4 us -> none  [the longest x1 3.64 us: per_device(): jnp.dot(columns, pieces[0], preferred_element_type=jnp.float32)]
    all_to_all x2 -> x0, waiting for transfers between devices: 10.5 us -> none  [the longest x1 10.5 us: from_everyone(): lax.all_to_all(jnp.broadcast_to(shard[None], (length, *shard.shape)), axi...]
  transfers between devices with their start and end apart: 4 -> 1, of which waited for: 3 -> 0; matrix products, arithmetic and copies ran while one was open for 2% -> 0% of each run, Pallas kernels for 0% -> 2%
where the time goes in v1:
time: 162 us; the launch traced here: 161 us
  blocking collectives  132 us (81%)
  Pallas kernels  18.5 us (11%)
  starting transfers between devices  5.12 us (3%)
  local copies, waits for them, and re-layouts  2.34 us (1%)
  other arithmetic  1.69 us (1%)
    all_to_all x3, blocking collectives, exchange(): return lax.all_to_all(pieces, axis, 0, 0, tiled=True)  71.8 us
    all_to_all x2, blocking collectives, gathered(): lax.all_to_all(copies, 'fsdp', 0, 0, tiled=True, axis_index_groups=groups)  60.3 us
    pallas_call x1, Pallas kernels, gradient_pieces(): pl.pallas_call(grads_kernel, in_specs=[pl.BlockSpec(memory_space=pltpu.SM...  10.1 us
    ppermute x1, starting transfers between devices, per_device(): other = lax.ppermute(own, 'fsdp', [(i, i ^ 1) for i in range(owners)])  5.12 us
  transfers between devices with their start and end apart: 1, of which 0 were waited for; matrix products, arithmetic and copies ran while one was open for 0% of the time, Pallas kernels for 2%

profile of v1, /device:TPU:1, one launch (start us, length us, event | category | flops | bytes accessed | tf_op | source)
XLA Modules:
  0.0 161.1 jit_solution(13823706789556215057)
XLA Ops:
  0.6 0.8 convert_element_type.3
  1.4 0.8 pad_maximum_fusion
  2.2 0.1 broadcast_in_dim.8
  2.3 21.7 %all_to_all.25 = bf16[8,64,576]{2,1,0:T(8,128)(2,1)S(1)} all-to-all(bf16[8,64,576]{2,1,0:T(8,128)(2,1)S(1)} %broadcast_in_dim.8), channel_id=1, replica_groups={{0,8,16,24,32,40,48,56},{1,9,17,25,33,41,49,57},{2,10,18,26,34,42,50,58..., dimensions={0} | all-to-all | bytes 1179648 | tf_op jit(solution)/shard_map/all_to_all | solution.py:234
  24.0 0.4 broadcast_in_dim.9
  24.3 0.0 copy-start.4
  24.3 38.6 %all_to_all.26.own_hbm = bf16[4,8,64,576]{3,2,1,0:T(8,128)(2,1)S(1)} all-to-all(bf16[4,8,64,576]{3,2,1,0:T(8,128)(2,1)S(1)} %broadcast_in_dim.9), channel_id=1, replica_groups={{0,2,4,6},{1,3,5,7},{8,10,12,14},{9,11,13,15},{16,18,20,22},{17,19,21,2..., dimensions={0} | all-to-all | bytes 4718592 | tf_op jit(solution)/shard_map/all_to_all | solution.py:234
  62.9 5.1 %collective-permute-start = (bf16[4,8,64,576]{3,2,1,0:T(8,128)(2,1)S(1)}, bf16[4,8,64,576]{3,2,1,0:T(8,128)(2,1)}, u32[]{:S(2)}, u32[]{:S(2)}) collective-permute-start(bf16[4,8,64,576]{3,2,1,0:T(8,128)(2,1)S(1)} %all_to_all.26.own_hbm), channel_id=1, source_target_pairs={{0,1},{1,0},{2,3},{3,2},{4,5},{5,4},{6,7},{7,6},{8,9},{9,8},{10,11... | collective-permute-start | bytes 7077896 | tf_op jit(solution)/shard_map/ppermute | solution.py:254
  68.7 0.1 pad_add_fusion.facts_ref
  68.8 0.0 copy-done.4
  68.8 1.2 copy-done.2
  70.0 3.0 %probs.1 = (bf16[4,1024,256]{2,1,0:T(8,128)(2,1)S(1)}, bf16[4,256,1024]{2,1,0:T(8,128)(2,1)S(1)}) custom-call(s32[1]{0:T(128)S(6)} %copy.15.length_ref, bf16[256,2048]{1,0:T(8,128)(2,1)S(1)} %copy-done.2, bf16[256,512]{1,0:T(8,128)(2,1)S(1)} %copy-done.4), custom_call_target="tpu_custom_call" | custom-call | flops 2147483648 | bytes 6291456 | tf_op jit(solution)/shard_map/probs/pallas_call | solution.py:53
  73.0 0.0 collective-permute-done.other_hbm
  73.0 0.0 copy-done
  73.0 0.0 copy-done.1
  73.0 0.0 copy-done.3
  73.0 10.1 %grads.1 = bf16[64,40,128]{2,1,0:T(8,128)(2,1)S(1)} custom-call(s32[2]{0:T(128)S(1)} %pad_add_fusion.facts_ref, bf16[256,4096]{1,0:T(8,128)(2,1)S(1)} %copy-done.1, bf16[4,8,64,576]{3,2,1,0:T(8,128)(2,1)S(1)} %all_to_all.26.own_hbm, bf16[4,8,64,576]{3,2,1,0:T(8,128)(2,1)} %collective-permute-done.other_hbm, ...), custom_call_target="tpu_custom_call" | custom-call | flops 4294967296 | bytes 14680064 | tf_op jit(solution)/shard_map/grads/pallas_call | solution.py:149
  83.2 24.5 %all_to_all.27.pieces_ref = bf16[64,40,128]{2,1,0:T(8,128)(2,1)} all-to-all(bf16[64,40,128]{2,1,0:T(8,128)(2,1)S(1)} %grads.1), channel_id=1, replica_groups=mesh['dp'=12,'fsdp'=64] {'fsdp'}, dimensions={0} | all-to-all | bytes 1310720 | tf_op jit(solution)/shard_map/all_to_all | solution.py:221
  107.6 1.9 %fold.1 = f32[12,40,128]{2,1,0:T(8,128)} custom-call(bf16[64,40,128]{2,1,0:T(8,128)(2,1)} %all_to_all.27.pieces_ref), custom_call_target="tpu_custom_call" | custom-call | tf_op jit(solution)/shard_map/fold/pallas_call | solution.py:173
  109.6 28.9 %all_to_all.28.pieces_ref = f32[12,40,128]{2,1,0:T(8,128)} all-to-all(f32[12,40,128]{2,1,0:T(8,128)} %fold.1), channel_id=1, replica_groups=mesh['dp'=12,'fsdp'=64] {'dp'}, dimensions={0} | all-to-all | bytes 491520 | tf_op jit(solution)/shard_map/all_to_all | solution.py:221
  138.5 1.7 %owner.1 = (f32[64,64]{1,0:T(8,128)}, f32[64,64]{1,0:T(8,128)}, f32[1,4,128]{2,1,0:T(4,128)}, f32[1,1]{1,0:T(1,128)}) custom-call(f32[12,40,128]{2,1,0:T(8,128)} %all_to_all.28.pieces_ref, f32[64,64]{1,0:T(8,128)} %down_ref.1, f32[64,64]{1,0:T(8,128)} %average_ref.2), custom_call_target="tpu_custom_call" | custom-call | tf_op jit(solution)/shard_map/owner/pallas_call | solution.py:194
  140.2 0.7 broadcast_in_dim.22
  140.9 18.4 %all_to_all.29.pieces_ref = f32[64,4,128]{2,1,0:T(4,128)} all-to-all(f32[64,4,128]{2,1,0:T(4,128)S(1)} %broadcast_in_dim.22), channel_id=1, replica_groups=mesh['dp'=12,'fsdp'=64] {'fsdp'}, dimensions={0} | all-to-all | bytes 262144 | tf_op jit(solution)/shard_map/all_to_all | solution.py:221
  159.4 1.8 %second.1 = (f32[64,512]{1,0:T(8,128)}, f32[64,512]{1,0:T(8,128)}) custom-call(f32[64,4,128]{2,1,0:T(4,128)} %all_to_all.29.pieces_ref, f32[64,512]{1,0:T(8,128)} %up_ref.3, f32[64,512]{1,0:T(8,128)} %average_ref.3), custom_call_target="tpu_custom_call" | custom-call | tf_op jit(solution)/shard_map/second/pallas_call | solution.py:217
  (4 shorter events, 0.0 us)
Async XLA Ops:
  24.3 44.5 %copy-start.4 = (bf16[256,512]{1,0:T(8,128)(2,1)S(1)}, bf16[256,512]{1,0:T(8,128)(2,1)}, u32[]{:S(2)}) copy-start(bf16[256,512]{1,0:T(8,128)(2,1)} %k_ref.1) | copy-start | bytes 786436
  62.9 10.1 %collective-permute-start = (bf16[4,8,64,576]{3,2,1,0:T(8,128)(2,1)S(1)}, bf16[4,8,64,576]{3,2,1,0:T(8,128)(2,1)}, u32[]{:S(2)}, u32[]{:S(2)}) collective-permute-start(bf16[4,8,64,576]{3,2,1,0:T(8,128)(2,1)S(1)} %all_to_all.26.own_hbm), channel_id=1, source_target_pairs={{0,1},{1,0},{2,3},{3,2},{4,5},{5,4},{6,7},{7,6},{8,9},{9,8},{10,11... | collective-permute-start | bytes 7077896 | tf_op jit(solution)/shard_map/ppermute | solution.py:254
  68.8 1.2 copy-start.2
  70.0 3.0 %copy-start = (f32[64,512]{1,0:T(8,128)S(1)}, f32[64,512]{1,0:T(8,128)}, u32[]{:S(2)}) copy-start(f32[64,512]{1,0:T(8,128)} %up_ref.3) | copy-start | bytes 393220
  70.0 3.0 %copy-start.1 = (bf16[256,4096]{1,0:T(8,128)(2,1)S(1)}, bf16[256,4096]{1,0:T(8,128)(2,1)}, u32[]{:S(2)}) copy-start(bf16[256,4096]{1,0:T(8,128)(2,1)} %hidden.1) | copy-start | bytes 6291460
  70.0 3.0 %copy-start.3 = (bf16[256,2048]{1,0:T(8,128)(2,1)S(1)}, bf16[256,2048]{1,0:T(8,128)(2,1)}, u32[]{:S(2)}) copy-start(bf16[256,2048]{1,0:T(8,128)(2,1)} %target.1) | copy-start | bytes 3145732

commit v2 on v1

--- a/solution.py
+++ b/solution.py
@@ -1,3 +1,4 @@
+import functools
 import math
 
 import jax
@@ -6,6 +7,7 @@
 from jax.experimental import pallas as pl
 from jax.experimental.pallas import tpu as pltpu
 from jax.sharding import PartitionSpec as P
+
 
 HEADS = 16
 KEY_VALUE_HEADS = 4
@@ -15,6 +17,7 @@
 MODEL = 4096
 RANK = 64
 KV_WIDTH = KEY_VALUE_HEADS * HEAD_DIM
+WIDTH = KV_WIDTH + RANK
 
 adapter_scale = 2.0
 average_decay = 0.9
@@ -22,7 +25,7 @@
 masked_score = -1e30
 
 PIECE_ROWS = 40
-CHUNKS = 8
+SMALL = pltpu.CompilerParams(vmem_limit_bytes=4 * 2**20)
 
 
 def nt(a, b):
@@ -72,33 +75,73 @@
     )(lengths, queries, keys)
 
 
+def pack_kernel(value_ref, down_ref, out_ref):
+    down = down_ref[...].astype(jnp.bfloat16)
+    for d in range(out_ref.shape[0]):
+        out_ref[d, :, :KV_WIDTH] = value_ref[...]
+        out_ref[d, :, KV_WIDTH:] = down
+
+
+def packed_shard(value_rows, down_rows, copies):
+    return pl.pallas_call(
+        pack_kernel,
+        out_shape=jax.ShapeDtypeStruct((copies, RANK, WIDTH), jnp.bfloat16),
+        compiler_params=SMALL,
+        name="pack",
+    )(value_rows, down_rows)
+
+
+def block_product(facts_ref, which, hidden, first, second, out):
+    x = lax.rem(facts_ref[2] + (4 - which), 4)
+    total = None
+    for y in range(0, first.shape[0], 2):
+        left, right = [], []
+        for i in (y, y + 1):
+            left.append(hidden[:, pl.ds(pl.multiple_of(i * 512 + x * 128, 128), 128)])
+            right += [first[i], second[i]]
+        part = nn(jnp.concatenate(left, axis=1), jnp.concatenate(right, axis=0))
+        total = part if total is None else total + part
+    out[...] = total
+
+
+def in_core_order(facts_ref, own, other, run):
+    @pl.when(facts_ref[1] == 0)
+    def _():
+        run(own, other)
+
+    @pl.when(facts_ref[1] != 0)
+    def _():
+        run(other, own)
+
+
+def partial_kernel(which, facts_ref, hidden, own, other, *rest):
+    out = rest[-1]
+    in_core_order(facts_ref, own, other, lambda a, b: block_product(facts_ref, which, hidden, a, b, out))
+    if len(rest) > 1:
+        out[...] += rest[0][...]
+
+
+def partial_values(facts, hidden, own, other, which, before=None):
+    vmem = pl.BlockSpec(memory_space=pltpu.VMEM)
+    given = () if before is None else (before,)
+    return pl.pallas_call(
+        functools.partial(partial_kernel, which),
+        in_specs=[pl.BlockSpec(memory_space=pltpu.SMEM)] + [vmem] * (3 + len(given)),
+        out_specs=vmem,
+        out_shape=jax.ShapeDtypeStruct((TOK, WIDTH), jnp.float32),
+        compiler_params=pltpu.CompilerParams(vmem_limit_bytes=8 * 2**20),
+        cost_estimate=pl.CostEstimate(flops=2**29, bytes_accessed=2**21, transcendentals=0),
+        name="partial",
+    )(facts, hidden, own, other, *given)
+
+
 def grads_kernel(
-    facts_ref, hidden, own_hbm, other_hbm, probs, probs_t, target, up_ref, out_ref,
-    weight, cot, value_grad, sems,
+    facts_ref, hidden, own, other, before, probs, probs_t, target, up_ref, out_ref, last, cot, value_grad,
 ):
-    length, core = facts_ref[0], facts_ref[1]
-    columns, rows = own_hbm.shape[0], own_hbm.shape[1]
-    step = MODEL // rows
-    loads = []
-    for c in range(rows):
-        copies = []
-        for x in range(columns):
-            base = c * step + x * 2 * RANK
-            for i, (source, side) in enumerate(((own_hbm, core), (other_hbm, 1 - core))):
-                place = pl.ds(pl.multiple_of(base + side * RANK, RANK), RANK)
-                copies.append(pltpu.make_async_copy(source.at[x, c], weight.at[place, :], sems.at[c, 2 * x + i]))
-        loads.append(copies)
-    for copies in loads:
-        for copy in copies:
-            copy.start()
-
+    length = facts_ref[0]
     up = up_ref[...].astype(jnp.bfloat16)
-    total = None
-    for c in range(rows):
-        for copy in loads[c]:
-            copy.wait()
-        part = nn(hidden[:, c * step : (c + 1) * step], weight[c * step : (c + 1) * step, :])
-        total = part if total is None else total + part
+    in_core_order(facts_ref, own, other, lambda a, b: block_product(facts_ref, 2, hidden, a, b, last))
+    total = last[...] + before[...]
     latent = total[:, KV_WIDTH:].astype(jnp.bfloat16)
     values = (total[:, :KV_WIDTH] + adapter_scale * nn(latent, up)).astype(jnp.bfloat16)
 
@@ -142,25 +185,22 @@
             out_ref[8 * q + 4 + b, 32:, :] = jnp.where(sub8 < 4, pltpu.roll(tile, 4, 0), facts).astype(jnp.bfloat16)
 
 
-def gradient_pieces(facts, hidden, own, other, probs, probs_t, target, up_map):
+def gradient_pieces(facts, hidden, own, other, before, probs, probs_t, target, up_map):
     vmem = pl.BlockSpec(memory_space=pltpu.VMEM)
-    hbm = pl.BlockSpec(memory_space=pltpu.HBM)
-    width = own.shape[-1]
     return pl.pallas_call(
         grads_kernel,
-        in_specs=[pl.BlockSpec(memory_space=pltpu.SMEM), vmem, hbm, hbm, vmem, vmem, vmem, vmem],
+        in_specs=[pl.BlockSpec(memory_space=pltpu.SMEM)] + [vmem] * 8,
         out_specs=vmem,
         out_shape=jax.ShapeDtypeStruct((MODEL // RANK, PIECE_ROWS, HEAD_DIM), jnp.bfloat16),
         scratch_shapes=[
-            pltpu.VMEM((MODEL, width), jnp.bfloat16),
+            pltpu.VMEM((TOK, WIDTH), jnp.float32),
             pltpu.VMEM((GROUP * TOK, HEAD_DIM), jnp.bfloat16),
             pltpu.VMEM((TOK, KV_WIDTH), jnp.bfloat16),
-            pltpu.SemaphoreType.DMA((own.shape[1], 2 * own.shape[0])),
-        ],
-        compiler_params=pltpu.CompilerParams(vmem_limit_bytes=32 * 2**20),
-        cost_estimate=pl.CostEstimate(flops=2**32, bytes_accessed=14 * 2**20, transcendentals=0),
+        ],
+        compiler_params=pltpu.CompilerParams(vmem_limit_bytes=24 * 2**20),
+        cost_estimate=pl.CostEstimate(flops=2**32, bytes_accessed=10 * 2**20, transcendentals=0),
         name="grads",
-    )(facts, hidden, own, other, probs, probs_t, target, up_map)
+    )(facts, hidden, own, other, before, probs, probs_t, target, up_map)
 
 
 def fold_kernel(pieces_ref, out_ref):
@@ -173,6 +213,7 @@
     return pl.pallas_call(
         fold_kernel,
         out_shape=jax.ShapeDtypeStruct((copies, PIECE_ROWS, HEAD_DIM), jnp.float32),
+        compiler_params=SMALL,
         name="fold",
     )(pieces)
 
@@ -186,19 +227,22 @@
     grad = jnp.transpose(rows) * factor
     grad_ref[...] = grad
     next_ref[...] = average_decay * average_ref[...] + (1.0 - average_decay) * (down_ref[...] - learning_rate * grad)
-    up_ref[0] = total[32:36, :] * factor
-
-
-def owner_update(pieces, down_map, average_down_map):
+    piece = total[32:36, :] * factor
+    for d in range(up_ref.shape[0]):
+        up_ref[d] = piece
+
+
+def owner_update(pieces, down_map, average_down_map, copies):
     shape = jax.ShapeDtypeStruct
     return pl.pallas_call(
         owner_kernel,
         out_shape=[
             shape((RANK, RANK), jnp.float32),
             shape((RANK, RANK), jnp.float32),
-            shape((1, 4, HEAD_DIM), jnp.float32),
+            shape((copies, 4, HEAD_DIM), jnp.float32),
             shape((1, 1), jnp.float32),
         ],
+        compiler_params=SMALL,
         name="owner",
     )(pieces, down_map, average_down_map)
 
@@ -214,7 +258,9 @@
 
 def second_update(pieces, up_map, average_up_map):
     shape = jax.ShapeDtypeStruct((RANK, KV_WIDTH), jnp.float32)
-    return pl.pallas_call(second_kernel, out_shape=[shape, shape], name="second")(pieces, up_map, average_up_map)
+    return pl.pallas_call(second_kernel, out_shape=[shape, shape], compiler_params=SMALL, name="second")(
+        pieces, up_map, average_up_map
+    )
 
 
 def exchange(pieces, axis):
@@ -225,13 +271,13 @@
     return [list(range(k, owners, 8)) for k in range(8)]
 
 
-def along_x(owners):
-    return [[y * 8 + x * 2 + core for x in range(4)] for y in range(owners // 8) for core in range(2)]
-
-
-def gathered(shard, groups):
-    copies = jnp.broadcast_to(shard[None], (len(groups[0]), *shard.shape))
-    return lax.all_to_all(copies, "fsdp", 0, 0, tiled=True, axis_index_groups=groups)
+def along_x(block, owners, shift):
+    moved = [(i, i // 8 * 8 + (i + 2 * shift) % 8) for i in range(owners)]
+    return lax.ppermute(block, "fsdp", moved)
+
+
+def from_other_core(block, owners):
+    return lax.ppermute(block, "fsdp", [(i, i ^ 1) for i in range(owners)])
 
 
 def per_device(
@@ -247,19 +293,26 @@
     average_up_map,
 ):
     owners, replicas = lax.axis_size("fsdp"), lax.axis_size("dp")
-    core = lax.axis_index("fsdp").astype(jnp.int32) % 2
-    facts = jnp.stack([lengths[0], core])
-    both = jnp.concatenate([value_weight_frozen, adapter_down_map.astype(jnp.bfloat16)], axis=1)
-    own = gathered(gathered(both, along_y(owners)), along_x(owners))
-    other = lax.ppermute(own, "fsdp", [(i, i ^ 1) for i in range(owners)])
+    place = lax.axis_index("fsdp").astype(jnp.int32)
+    facts = jnp.stack([lengths[0], place & 1, (place >> 1) & 3])
+    shards = packed_shard(value_weight_frozen, adapter_down_map, owners // 8)
+    own = lax.all_to_all(shards, "fsdp", 0, 0, tiled=True, axis_index_groups=along_y(owners))
+    blocks, others, total = [own], [], None
+    for shift in (1, 2, 3):
+        blocks.append(along_x(own, owners, shift))
+    for shift in range(4):
+        others.append(from_other_core(blocks[shift], owners))
     probs, probs_t = attention_probs(lengths, queries, keys)
-    pieces = gradient_pieces(facts, hidden, own, other, probs, probs_t, target, adapter_up_map)
+    for shift in (0, 1, 3):
+        total = partial_values(facts, hidden, blocks[shift], others[shift], shift, total)
+    pieces = gradient_pieces(
+        facts, hidden, blocks[2], others[2], total, probs, probs_t, target, adapter_up_map
+    )
     summed = fold(exchange(pieces, "fsdp"), replicas)
     down_grad, average_down_next, up_piece, loss = owner_update(
-        exchange(summed, "dp"), adapter_down_map, average_down_map
-    )
-    up_pieces = exchange(jnp.broadcast_to(up_piece, (owners, 4, HEAD_DIM)), "fsdp")
-    up_grad, average_up_next = second_update(up_pieces, adapter_up_map, average_up_map)
+        exchange(summed, "dp"), adapter_down_map, average_down_map, owners
+    )
+    up_grad, average_up_next = second_update(exchange(up_piece, "fsdp"), adapter_up_map, average_up_map)
     return (down_grad, up_grad, average_down_next, average_up_next, loss.reshape(()))
 
 

time: 162 us -> 160 us (0.988)
  blocking collectives: 132 us -> 97.9 us
  starting transfers between devices: 5.12 us -> 34.4 us
  waiting for transfers between devices: 0.01 us -> 7.83 us
  Pallas kernels: 18.5 us -> 13.3 us
    all_to_all x2 -> x1, blocking collectives: 60.3 us -> 21.7 us  [per_device(): lax.all_to_all(shards, 'fsdp', 0, 0, tiled=True, axis_index_groups=along_...]
    ppermute x1 -> x7, starting transfers between devices: 5.12 us -> 34.4 us  [the longest x4 19.5 us: from_other_core(): return lax.ppermute(block, 'fsdp', [(i, i ^ 1) for i in range(owners)])]
    ppermute x1 -> x7, waiting for transfers between devices: 0.01 us -> 7.83 us  [the longest x3 7.82 us: along_x(): return lax.ppermute(block, 'fsdp', moved)]
    pallas_call x1, Pallas kernels: 10.1 us -> 4.48 us  [gradient_pieces(): pl.pallas_call(grads_kernel, in_specs=[pl.BlockSpec(memory_space=pltpu.SM...]
    all_to_all x3, blocking collectives: 71.8 us -> 76.3 us  [exchange(): return lax.all_to_all(pieces, axis, 0, 0, tiled=True)]
    pallas_call x1 -> x5, Pallas kernels: 1.76 us -> 4.98 us  [the longest x3 4.19 us: partial_values(): pl.pallas_call(functools.partial(partial_kernel, which), in_specs=[pl.Blo...]
    unnamed x10 -> x20, local copies, waits for them, and re-layouts: 1.24 us -> 3.8 us
    pallas_call x1, Pallas kernels: 1.93 us -> 0.13 us  [fold(): pl.pallas_call(fold_kernel, out_shape=jax.ShapeDtypeStruct((copies, PIECE...]
  transfers between devices with their start and end apart: 1 -> 7, of which waited for: 0 -> 2; matrix products, arithmetic and copies ran while one was open for 0% -> 0% of each run, Pallas kernels for 2% -> 5%
where the time goes in v2:
time: 160 us; the launch traced here: 159 us
  blocking collectives  97.9 us (61%)
  starting transfers between devices  34.4 us (22%)
  Pallas kernels  13.3 us (8%)
  waiting for transfers between devices  7.83 us (5%)
  local copies, waits for them, and re-layouts  3.8 us (2%)
    all_to_all x3, blocking collectives, exchange(): return lax.all_to_all(pieces, axis, 0, 0, tiled=True)  76.3 us
    all_to_all x1, blocking collectives, per_device(): lax.all_to_all(shards, 'fsdp', 0, 0, tiled=True, axis_index_groups=along_...  21.7 us
    ppermute x4, starting transfers between devices, from_other_core(): return lax.ppermute(block, 'fsdp', [(i, i ^ 1) for i in range(owners)])  19.5 us
    ppermute x3, starting transfers between devices, along_x(): return lax.ppermute(block, 'fsdp', moved)  14.9 us
    ppermute x3, waiting for transfers between devices, along_x(): return lax.ppermute(block, 'fsdp', moved)  7.82 us
    pallas_call x1, Pallas kernels, gradient_pieces(): pl.pallas_call(grads_kernel, in_specs=[pl.BlockSpec(memory_space=pltpu.SM...  4.48 us
    pallas_call x3, Pallas kernels, partial_values(): pl.pallas_call(functools.partial(partial_kernel, which), in_specs=[pl.Blo...  4.19 us
    unnamed x20, local copies, waits for them, and re-layouts  3.8 us
  transfers between devices with their start and end apart: 7, of which 2 were waited for; matrix products, arithmetic and copies ran while one was open for 0% of the time, Pallas kernels for 5%

profile of v2, /device:TPU:1, one launch (start us, length us, event | category | flops | bytes accessed | tf_op | source)
XLA Modules:
  0.0 158.9 jit_solution(6972402362624929886)
XLA Ops:
  0.6 0.7 copy-done.3
  1.4 0.8 copy-done.5
  2.3 21.7 %all_to_all.20.own = bf16[8,64,576]{2,1,0:T(8,128)(2,1)S(1)} all-to-all(bf16[8,64,576]{2,1,0:T(8,128)(2,1)S(1)} %pack.1), channel_id=1, replica_groups={{0,8,16,24,32,40,48,56},{1,9,17,25,33,41,49,57},{2,10,18,26,34,42,50,58..., dimensions={0} | all-to-all | bytes 1179648 | tf_op jit(solution)/shard_map/all_to_all | solution.py:299
  23.9 8.1 %collective-permute-start.4 = (bf16[8,64,576]{2,1,0:T(8,128)(2,1)S(1)}, bf16[8,64,576]{2,1,0:T(8,128)(2,1)S(1)}, u32[]{:S(2)}, u32[]{:S(2)}) collective-permute-start(bf16[8,64,576]{2,1,0:T(8,128)(2,1)S(1)} %all_to_all.20.own), channel_id=1, source_target_pairs={{0,2},{1,3},{2,4},{3,5},{4,6},{5,7},{6,0},{7,1},{8,10},{9,11},{10,... | collective-permute-start | bytes 1769480 | tf_op jit(solution)/shard_map/ppermute | solution.py:276
  32.0 3.2 %collective-permute-start.2 = (bf16[8,64,576]{2,1,0:T(8,128)(2,1)S(1)}, bf16[8,64,576]{2,1,0:T(8,128)(2,1)S(1)}, u32[]{:S(2)}, u32[]{:S(2)}) collective-permute-start(bf16[8,64,576]{2,1,0:T(8,128)(2,1)S(1)} %all_to_all.20.own), channel_id=1, source_target_pairs={{0,6},{1,7},{2,0},{3,1},{4,2},{5,3},{6,4},{7,5},{8,14},{9,15},{10,... | collective-permute-start | bytes 1769480 | tf_op jit(solution)/shard_map/ppermute | solution.py:276
  35.2 3.6 %collective-permute-start = (bf16[8,64,576]{2,1,0:T(8,128)(2,1)S(1)}, bf16[8,64,576]{2,1,0:T(8,128)(2,1)}, u32[]{:S(2)}, u32[]{:S(2)}) collective-permute-start(bf16[8,64,576]{2,1,0:T(8,128)(2,1)S(1)} %all_to_all.20.own), channel_id=1, source_target_pairs={{0,4},{1,5},{2,6},{3,7},{4,0},{5,1},{6,2},{7,3},{8,12},{9,13},{10,... | collective-permute-start | bytes 1769480 | tf_op jit(solution)/shard_map/ppermute | solution.py:276
  38.9 4.8 %collective-permute-start.6 = (bf16[8,64,576]{2,1,0:T(8,128)(2,1)S(1)}, bf16[8,64,576]{2,1,0:T(8,128)(2,1)S(1)}, u32[]{:S(2)}, u32[]{:S(2)}) collective-permute-start(bf16[8,64,576]{2,1,0:T(8,128)(2,1)S(1)} %all_to_all.20.own), channel_id=1, source_target_pairs={{0,1},{1,0},{2,3},{3,2},{4,5},{5,4},{6,7},{7,6},{8,9},{9,8},{10,11... | collective-permute-start | bytes 1769480 | tf_op jit(solution)/shard_map/ppermute | solution.py:280
  43.7 2.2 %collective-permute-done.4.own = bf16[8,64,576]{2,1,0:T(8,128)(2,1)S(1)} collective-permute-done((bf16[8,64,576]{2,1,0:T(8,128)(2,1)S(1)}, bf16[8,64,576]{2,1,0:T(8,128)(2,1)S(1)}, u32[]{:S(2)}, u32[]{:S(2)}) %collective-permute-start.4) | collective-permute-done | bytes 589856 | tf_op jit(solution)/shard_map/ppermute | solution.py:276
  45.9 6.3 %collective-permute-start.5 = (bf16[8,64,576]{2,1,0:T(8,128)(2,1)S(1)}, bf16[8,64,576]{2,1,0:T(8,128)(2,1)S(1)}, u32[]{:S(2)}, u32[]{:S(2)}) collective-permute-start(bf16[8,64,576]{2,1,0:T(8,128)(2,1)S(1)} %collective-permute-done.4.own), channel_id=1, source_target_pairs={{0,1},{1,0},{2,3},{3,2},{4,5},{5,4},{6,7},{7,6},{8,9},{9,8},{10,11... | collective-permute-start | bytes 1769480 | tf_op jit(solution)/shard_map/ppermute | solution.py:280
  52.2 3.5 %collective-permute-start.3 = (bf16[8,64,576]{2,1,0:T(8,128)(2,1)S(1)}, bf16[8,64,576]{2,1,0:T(8,128)(2,1)}, u32[]{:S(2)}, u32[]{:S(2)}) collective-permute-start(bf16[8,64,576]{2,1,0:T(8,128)(2,1)S(1)} %collective-permute-done.2.own), channel_id=1, source_target_pairs={{0,1},{1,0},{2,3},{3,2},{4,5},{5,4},{6,7},{7,6},{8,9},{9,8},{10,11... | collective-permute-start | bytes 1769480 | tf_op jit(solution)/shard_map/ppermute | solution.py:280
  55.8 5.6 %collective-permute-done.own = bf16[8,64,576]{2,1,0:T(8,128)(2,1)} collective-permute-done((bf16[8,64,576]{2,1,0:T(8,128)(2,1)S(1)}, bf16[8,64,576]{2,1,0:T(8,128)(2,1)}, u32[]{:S(2)}, u32[]{:S(2)}) %collective-permute-start) | collective-permute-done | bytes 589856 | tf_op jit(solution)/shard_map/ppermute | solution.py:276
  61.4 4.8 %collective-permute-start.1 = (bf16[8,64,576]{2,1,0:T(8,128)(2,1)}, bf16[8,64,576]{2,1,0:T(8,128)(2,1)}, u32[]{:S(2)}, u32[]{:S(2)}) collective-permute-start(bf16[8,64,576]{2,1,0:T(8,128)(2,1)} %collective-permute-done.own), channel_id=1, source_target_pairs={{0,1},{1,0},{2,3},{3,2},{4,5},{5,4},{6,7},{7,6},{8,9},{9,8},{10,11... | collective-permute-start | bytes 1769480 | tf_op jit(solution)/shard_map/ppermute | solution.py:280
  66.9 1.2 copy-done.7
  68.2 0.9 copy-done.9
  69.1 3.0 %probs.1 = (bf16[4,1024,256]{2,1,0:T(8,128)(2,1)S(1)}, bf16[4,256,1024]{2,1,0:T(8,128)(2,1)S(1)}) custom-call(s32[1]{0:T(128)S(6)} %copy.15.length_ref, bf16[256,2048]{1,0:T(8,128)(2,1)S(1)} %copy-done.7, bf16[256,512]{1,0:T(8,128)(2,1)S(1)} %copy-done.9), custom_call_target="tpu_custom_call" | custom-call | flops 2147483648 | bytes 6291456 | tf_op jit(solution)/shard_map/probs/pallas_call | solution.py:56
  72.1 1.1 partial.3.rest_0_
  73.3 1.2 partial.4.rest_0_
  74.5 1.9 %partial.5.before = f32[256,576]{1,0:T(8,128)S(1)} custom-call(s32[3]{0:T(128)S(1)} %pad_add_fusion.facts_ref, bf16[256,4096]{1,0:T(8,128)(2,1)S(1)} %copy-done, bf16[8,64,576]{2,1,0:T(8,128)(2,1)S(1)} %collective-permute-done.2.own, bf16[8,64,576]{2,1,0:T(8,128)(2,1)} %collective-permute-done.3.other, f32[256,576]{1,0:T(8,128)S(1)} %partial.4.rest_0_), custom_call_target="tpu_custom_call" | custom-call | flops 536870912 | bytes 2097152 | tf_op jit(solution)/shard_map/partial/pallas_call | solution.py:127
  76.4 4.5 %grads.1 = bf16[64,40,128]{2,1,0:T(8,128)(2,1)S(1)} custom-call(s32[3]{0:T(128)S(1)} %pad_add_fusion.facts_ref, bf16[256,4096]{1,0:T(8,128)(2,1)S(1)} %copy-done, bf16[8,64,576]{2,1,0:T(8,128)(2,1)} %collective-permute-done.own, bf16[8,64,576]{2,1,0:T(8,128)(2,1)} %collective-permute-done.1.other, f32[256,576]{1,0:T(8,128)S(1)} %partial.5.before, ...), custom_call_target="tpu_custom_call" | custom-call | flops 4294967296 | bytes 10485760 | tf_op jit(solution)/shard_map/grads/pallas_call | solution.py:190
  80.9 27.0 %all_to_all.21.pieces_ref = bf16[64,40,128]{2,1,0:T(8,128)(2,1)S(1)} all-to-all(bf16[64,40,128]{2,1,0:T(8,128)(2,1)S(1)} %grads.1), channel_id=1, replica_groups=mesh['dp'=12,'fsdp'=64] {'fsdp'}, dimensions={0} | all-to-all | bytes 1310720 | tf_op jit(solution)/shard_map/all_to_all | solution.py:267
  108.0 31.0 %all_to_all.22.pieces_ref = f32[12,40,128]{2,1,0:T(8,128)S(1)} all-to-all(f32[12,40,128]{2,1,0:T(8,128)S(1)} %fold.1), channel_id=1, replica_groups=mesh['dp'=12,'fsdp'=64] {'dp'}, dimensions={0} | all-to-all | bytes 491520 | tf_op jit(solution)/shard_map/all_to_all | solution.py:267
  139.0 0.8 owner.1
  139.8 18.4 %all_to_all.23.pieces_ref = f32[64,4,128]{2,1,0:T(4,128)S(1)} all-to-all(f32[64,4,128]{2,1,0:T(4,128)S(1)} %get-tuple-element.16), channel_id=1, replica_groups=mesh['dp'=12,'fsdp'=64] {'fsdp'}, dimensions={0} | all-to-all | bytes 262144 | tf_op jit(solution)/shard_map/all_to_all | solution.py:267
  158.2 0.7 second.1
  (24 shorter events, 0.3 us)
Async XLA Ops:
  0.6 0.8 copy-start.3
  1.4 0.8 copy-start.5
  23.9 22.0 %collective-permute-start.4 = (bf16[8,64,576]{2,1,0:T(8,128)(2,1)S(1)}, bf16[8,64,576]{2,1,0:T(8,128)(2,1)S(1)}, u32[]{:S(2)}, u32[]{:S(2)}) collective-permute-start(bf16[8,64,576]{2,1,0:T(8,128)(2,1)S(1)} %all_to_all.20.own), channel_id=1, source_target_pairs={{0,2},{1,3},{2,4},{3,5},{4,6},{5,7},{6,0},{7,1},{8,10},{9,11},{10,... | collective-permute-start | bytes 1769480 | tf_op jit(solution)/shard_map/ppermute | solution.py:276
  32.0 20.2 %collective-permute-start.2 = (bf16[8,64,576]{2,1,0:T(8,128)(2,1)S(1)}, bf16[8,64,576]{2,1,0:T(8,128)(2,1)S(1)}, u32[]{:S(2)}, u32[]{:S(2)}) collective-permute-start(bf16[8,64,576]{2,1,0:T(8,128)(2,1)S(1)} %all_to_all.20.own), channel_id=1, source_target_pairs={{0,6},{1,7},{2,0},{3,1},{4,2},{5,3},{6,4},{7,5},{8,14},{9,15},{10,... | collective-permute-start | bytes 1769480 | tf_op jit(solution)/shard_map/ppermute | solution.py:276
  35.2 26.2 %collective-permute-start = (bf16[8,64,576]{2,1,0:T(8,128)(2,1)S(1)}, bf16[8,64,576]{2,1,0:T(8,128)(2,1)}, u32[]{:S(2)}, u32[]{:S(2)}) collective-permute-start(bf16[8,64,576]{2,1,0:T(8,128)(2,1)S(1)} %all_to_all.20.own), channel_id=1, source_target_pairs={{0,4},{1,5},{2,6},{3,7},{4,0},{5,1},{6,2},{7,3},{8,12},{9,13},{10,... | collective-permute-start | bytes 1769480 | tf_op jit(solution)/shard_map/ppermute | solution.py:276
  38.9 33.2 %collective-permute-start.6 = (bf16[8,64,576]{2,1,0:T(8,128)(2,1)S(1)}, bf16[8,64,576]{2,1,0:T(8,128)(2,1)S(1)}, u32[]{:S(2)}, u32[]{:S(2)}) collective-permute-start(bf16[8,64,576]{2,1,0:T(8,128)(2,1)S(1)} %all_to_all.20.own), channel_id=1, source_target_pairs={{0,1},{1,0},{2,3},{3,2},{4,5},{5,4},{6,7},{7,6},{8,9},{9,8},{10,11... | collective-permute-start | bytes 1769480 | tf_op jit(solution)/shard_map/ppermute | solution.py:280
  45.9 27.4 %collective-permute-start.5 = (bf16[8,64,576]{2,1,0:T(8,128)(2,1)S(1)}, bf16[8,64,576]{2,1,0:T(8,128)(2,1)S(1)}, u32[]{:S(2)}, u32[]{:S(2)}) collective-permute-start(bf16[8,64,576]{2,1,0:T(8,128)(2,1)S(1)} %collective-permute-done.4.own), channel_id=1, source_target_pairs={{0,1},{1,0},{2,3},{3,2},{4,5},{5,4},{6,7},{7,6},{8,9},{9,8},{10,11... | collective-permute-start | bytes 1769480 | tf_op jit(solution)/shard_map/ppermute | solution.py:280
  52.2 22.3 %collective-permute-start.3 = (bf16[8,64,576]{2,1,0:T(8,128)(2,1)S(1)}, bf16[8,64,576]{2,1,0:T(8,128)(2,1)}, u32[]{:S(2)}, u32[]{:S(2)}) collective-permute-start(bf16[8,64,576]{2,1,0:T(8,128)(2,1)S(1)} %collective-permute-done.2.own), channel_id=1, source_target_pairs={{0,1},{1,0},{2,3},{3,2},{4,5},{5,4},{6,7},{7,6},{8,9},{9,8},{10,11... | collective-permute-start | bytes 1769480 | tf_op jit(solution)/shard_map/ppermute | solution.py:280
  61.4 15.0 %collective-permute-start.1 = (bf16[8,64,576]{2,1,0:T(8,128)(2,1)}, bf16[8,64,576]{2,1,0:T(8,128)(2,1)}, u32[]{:S(2)}, u32[]{:S(2)}) collective-permute-start(bf16[8,64,576]{2,1,0:T(8,128)(2,1)} %collective-permute-done.own), channel_id=1, source_target_pairs={{0,1},{1,0},{2,3},{3,2},{4,5},{5,4},{6,7},{7,6},{8,9},{9,8},{10,11... | collective-permute-start | bytes 1769480 | tf_op jit(solution)/shard_map/ppermute | solution.py:280
  66.9 1.2 copy-start.7
  68.2 0.9 copy-start.9
  69.1 3.0 %copy-start = (bf16[256,4096]{1,0:T(8,128)(2,1)S(1)}, bf16[256,4096]{1,0:T(8,128)(2,1)}, u32[]{:S(2)}) copy-start(bf16[256,4096]{1,0:T(8,128)(2,1)} %hidden.7) | copy-start | bytes 6291460
  74.5 1.9 %copy-start.1 = (f32[64,512]{1,0:T(8,128)S(1)}, f32[64,512]{1,0:T(8,128)}, u32[]{:S(2)}) copy-start(f32[64,512]{1,0:T(8,128)} %up_ref.3) | copy-start | bytes 393220
  74.5 1.9 %copy-start.8 = (bf16[256,2048]{1,0:T(8,128)(2,1)S(1)}, bf16[256,2048]{1,0:T(8,128)(2,1)}, u32[]{:S(2)}) copy-start(bf16[256,2048]{1,0:T(8,128)(2,1)} %target.1) | copy-start | bytes 3145732
  80.9 58.1 %copy-start.4 = (f32[64,64]{1,0:T(8,128)S(1)}, f32[64,64]{1,0:T(8,128)}, u32[]{:S(2)}) copy-start(f32[64,64]{1,0:T(8,128)} %down_ref.3) | copy-start | bytes 49156
  80.9 58.1 %copy-start.6 = (f32[64,64]{1,0:T(8,128)S(1)}, f32[64,64]{1,0:T(8,128)}, u32[]{:S(2)}) copy-start(f32[64,64]{1,0:T(8,128)} %average_ref.2) | copy-start | bytes 49156
  80.9 77.2 %copy-start.2 = (f32[64,512]{1,0:T(8,128)S(1)}, f32[64,512]{1,0:T(8,128)}, u32[]{:S(2)}) copy-start(f32[64,512]{1,0:T(8,128)} %average_ref.3) | copy-start | bytes 393220

commit v3 on v2

--- a/solution.py
+++ b/solution.py
@@ -18,6 +18,7 @@
 RANK = 64
 KV_WIDTH = KEY_VALUE_HEADS * HEAD_DIM
 WIDTH = KV_WIDTH + RANK
+PADDED = KV_WIDTH + HEAD_DIM
 
 adapter_scale = 2.0
 average_decay = 0.9
@@ -91,58 +92,90 @@
     )(value_rows, down_rows)
 
 
-def block_product(facts_ref, which, hidden, first, second, out):
-    x = lax.rem(facts_ref[2] + (4 - which), 4)
-    total = None
-    for y in range(0, first.shape[0], 2):
-        left, right = [], []
-        for i in (y, y + 1):
-            left.append(hidden[:, pl.ds(pl.multiple_of(i * 512 + x * 128, 128), 128)])
-            right += [first[i], second[i]]
-        part = nn(jnp.concatenate(left, axis=1), jnp.concatenate(right, axis=0))
-        total = part if total is None else total + part
-    out[...] = total
-
-
-def in_core_order(facts_ref, own, other, run):
-    @pl.when(facts_ref[1] == 0)
-    def _():
-        run(own, other)
-
-    @pl.when(facts_ref[1] != 0)
-    def _():
-        run(other, own)
-
-
-def partial_kernel(which, facts_ref, hidden, own, other, *rest):
-    out = rest[-1]
-    in_core_order(facts_ref, own, other, lambda a, b: block_product(facts_ref, which, hidden, a, b, out))
-    if len(rest) > 1:
-        out[...] += rest[0][...]
-
-
-def partial_values(facts, hidden, own, other, which, before=None):
+def split_kernel(facts_ref, hidden, keep, send):
+    first = lax.broadcasted_iota(jnp.int32, (TOK, HEAD_DIM), 1) < RANK
+    mine = facts_ref[1] == 0
+    for x in range(4):
+        for y in range(0, 8, 2):
+            a = hidden[:, y * 512 + x * 128 : y * 512 + (x + 1) * 128].astype(jnp.float32)
+            b = hidden[:, (y + 1) * 512 + x * 128 : (y + 1) * 512 + (x + 1) * 128].astype(jnp.float32)
+            even = jnp.where(first, a, pltpu.roll(b, RANK, 1))
+            odd = jnp.where(first, pltpu.roll(a, RANK, 1), b)
+            to = pl.ds(x * 512 + y * 64, 128)
+            keep[:, to] = jnp.where(mine, even, odd).astype(jnp.bfloat16)
+            send[:, to] = jnp.where(mine, odd, even).astype(jnp.bfloat16)
+
+
+def split_hidden(facts, hidden):
     vmem = pl.BlockSpec(memory_space=pltpu.VMEM)
-    given = () if before is None else (before,)
-    return pl.pallas_call(
-        functools.partial(partial_kernel, which),
-        in_specs=[pl.BlockSpec(memory_space=pltpu.SMEM)] + [vmem] * (3 + len(given)),
-        out_specs=vmem,
-        out_shape=jax.ShapeDtypeStruct((TOK, WIDTH), jnp.float32),
-        compiler_params=pltpu.CompilerParams(vmem_limit_bytes=8 * 2**20),
+    shape = jax.ShapeDtypeStruct((TOK, MODEL // 2), jnp.bfloat16)
+    return pl.pallas_call(
+        split_kernel,
+        in_specs=[pl.BlockSpec(memory_space=pltpu.SMEM), vmem],
+        out_specs=[vmem, vmem],
+        out_shape=[shape, shape],
+        compiler_params=pltpu.CompilerParams(vmem_limit_bytes=12 * 2**20),
+        cost_estimate=pl.CostEstimate(flops=2**30, bytes_accessed=2**22, transcendentals=0),
+        name="split",
+    )(facts, hidden)
+
+
+def partial_kernel(which, facts_ref, mine, theirs, *rest):
+    *blocks, before, out = rest
+    column = lax.rem(facts_ref[2] + (4 - which), 4) * 512
+    half = facts_ref[3] * 256
+    for i, tokens in enumerate((mine, theirs)):
+        if len(blocks) == 1:
+            part = nn(
+                tokens[:, pl.ds(pl.multiple_of(column, 512), 512)], blocks[0][...].reshape(512, WIDTH)
+            )
+        else:
+            part = nn(
+                tokens[:, pl.ds(pl.multiple_of(column + half, 256), 256)], blocks[0][...].reshape(256, WIDTH)
+            )
+            rows = jnp.concatenate([blocks[1][...].reshape(128, WIDTH), blocks[2][...].reshape(128, WIDTH)], axis=0)
+            part += nn(tokens[:, pl.ds(pl.multiple_of(column + (256 - half), 256), 256)], rows)
+        out[i] = part if before is None else part + before[i]
+
+
+def first_partial_kernel(which, facts_ref, mine, theirs, block, out):
+    partial_kernel(which, facts_ref, mine, theirs, block, None, out)
+
+
+def last_partial_kernel(which, facts_ref, mine, theirs, half, low, high, before, own, other):
+    class Outs:
+        def __setitem__(self, i, value):
+            (own, other)[i][:, :WIDTH] = value
+
+    partial_kernel(which, facts_ref, mine, theirs, half, low, high, before, Outs())
+    for out in (own, other):
+        out[:, WIDTH:] = jnp.zeros((TOK, PADDED - WIDTH), jnp.float32)
+
+
+def partial_values(facts, mine, theirs, blocks, which, before=None):
+    vmem = pl.BlockSpec(memory_space=pltpu.VMEM)
+    given = tuple(blocks) + (() if before is None else (before,))
+    last = len(blocks) > 1
+    body = last_partial_kernel if last else first_partial_kernel if before is None else partial_kernel
+    shape = jax.ShapeDtypeStruct((TOK, PADDED), jnp.float32)
+    return pl.pallas_call(
+        functools.partial(body, which),
+        in_specs=[pl.BlockSpec(memory_space=pltpu.SMEM)] + [vmem] * (2 + len(given)),
+        out_specs=[vmem, vmem] if last else vmem,
+        out_shape=[shape, shape] if last else jax.ShapeDtypeStruct((2, TOK, WIDTH), jnp.float32),
+        compiler_params=pltpu.CompilerParams(vmem_limit_bytes=12 * 2**20),
         cost_estimate=pl.CostEstimate(flops=2**29, bytes_accessed=2**21, transcendentals=0),
         name="partial",
-    )(facts, hidden, own, other, *given)
+    )(facts, mine, theirs, *given)
 
 
 def grads_kernel(
-    facts_ref, hidden, own, other, before, probs, probs_t, target, up_ref, out_ref, last, cot, value_grad,
+    facts_ref, hidden, before, swapped, probs, probs_t, target, up_ref, out_ref, cot, value_grad,
 ):
     length = facts_ref[0]
     up = up_ref[...].astype(jnp.bfloat16)
-    in_core_order(facts_ref, own, other, lambda a, b: block_product(facts_ref, 2, hidden, a, b, last))
-    total = last[...] + before[...]
-    latent = total[:, KV_WIDTH:].astype(jnp.bfloat16)
+    total = before[...] + swapped[...]
+    latent = total[:, KV_WIDTH:WIDTH].astype(jnp.bfloat16)
     values = (total[:, :KV_WIDTH] + adapter_scale * nn(latent, up)).astype(jnp.bfloat16)
 
     live = lax.broadcasted_iota(jnp.int32, (TOK, HEAD_DIM), 0) < length
@@ -185,22 +218,21 @@
             out_ref[8 * q + 4 + b, 32:, :] = jnp.where(sub8 < 4, pltpu.roll(tile, 4, 0), facts).astype(jnp.bfloat16)
 
 
-def gradient_pieces(facts, hidden, own, other, before, probs, probs_t, target, up_map):
+def gradient_pieces(facts, hidden, before, swapped, probs, probs_t, target, up_map):
     vmem = pl.BlockSpec(memory_space=pltpu.VMEM)
     return pl.pallas_call(
         grads_kernel,
-        in_specs=[pl.BlockSpec(memory_space=pltpu.SMEM)] + [vmem] * 8,
+        in_specs=[pl.BlockSpec(memory_space=pltpu.SMEM)] + [vmem] * 7,
         out_specs=vmem,
         out_shape=jax.ShapeDtypeStruct((MODEL // RANK, PIECE_ROWS, HEAD_DIM), jnp.bfloat16),
         scratch_shapes=[
-            pltpu.VMEM((TOK, WIDTH), jnp.float32),
             pltpu.VMEM((GROUP * TOK, HEAD_DIM), jnp.bfloat16),
             pltpu.VMEM((TOK, KV_WIDTH), jnp.bfloat16),
         ],
         compiler_params=pltpu.CompilerParams(vmem_limit_bytes=24 * 2**20),
         cost_estimate=pl.CostEstimate(flops=2**32, bytes_accessed=10 * 2**20, transcendentals=0),
         name="grads",
-    )(facts, hidden, own, other, before, probs, probs_t, target, up_map)
+    )(facts, hidden, before, swapped, probs, probs_t, target, up_map)
 
 
 def fold_kernel(pieces_ref, out_ref):
@@ -294,20 +326,24 @@
 ):
     owners, replicas = lax.axis_size("fsdp"), lax.axis_size("dp")
     place = lax.axis_index("fsdp").astype(jnp.int32)
-    facts = jnp.stack([lengths[0], place & 1, (place >> 1) & 3])
+    parity = lax.axis_index("dp").astype(jnp.int32) & 1
+    facts = jnp.stack([lengths[0], place & 1, (place >> 1) & 3, parity])
     shards = packed_shard(value_weight_frozen, adapter_down_map, owners // 8)
     own = lax.all_to_all(shards, "fsdp", 0, 0, tiled=True, axis_index_groups=along_y(owners))
-    blocks, others, total = [own], [], None
-    for shift in (1, 2, 3):
-        blocks.append(along_x(own, owners, shift))
-    for shift in range(4):
-        others.append(from_other_core(blocks[shift], owners))
+    mine, send = split_hidden(facts, hidden)
+    theirs = from_other_core(send, owners)
     probs, probs_t = attention_probs(lengths, queries, keys)
-    for shift in (0, 1, 3):
-        total = partial_values(facts, hidden, blocks[shift], others[shift], shift, total)
-    pieces = gradient_pieces(
-        facts, hidden, blocks[2], others[2], total, probs, probs_t, target, adapter_up_map
-    )
+    half = along_x(lax.dynamic_slice_in_dim(own, parity * 4, 4, axis=0), owners, 2)
+    near = along_x(own, owners, 1)
+    far = along_x(own, owners, 3)
+    low = lax.ppermute(half[:2], "dp", [(i, (i + 1) % replicas) for i in range(replicas)])
+    high = lax.ppermute(half[2:], "dp", [(i, (i - 1) % replicas) for i in range(replicas)])
+    total = None
+    for shift, block in ((0, own), (1, near), (3, far)):
+        total = partial_values(facts, mine, theirs, (block,), shift, total)
+    total, other = partial_values(facts, mine, theirs, (half, low, high), 2, total)
+    swapped = from_other_core(other, owners)
+    pieces = gradient_pieces(facts, hidden, total, swapped, probs, probs_t, target, adapter_up_map)
     summed = fold(exchange(pieces, "fsdp"), replicas)
     down_grad, average_down_next, up_piece, loss = owner_update(
         exchange(summed, "dp"), adapter_down_map, average_down_map, owners

time: 160 us -> 154 us (0.963)
  blocking collectives: 97.9 us -> 62.6 us
  starting transfers between devices: 34.4 us -> 53.9 us
  waiting for transfers between devices: 7.83 us -> 16.3 us
  Pallas kernels: 13.3 us -> 15.8 us
    all_to_all x1 -> x0, blocking collectives: 21.7 us -> none  [per_device(): lax.all_to_all(shards, 'fsdp', 0, 0, tiled=True, axis_index_groups=along_...]
    ppermute x0 -> x2, starting transfers between devices: none -> 16.2 us  [the longest x1 12.2 us: per_device(): lax.ppermute(half[2:], 'dp', [(i, (i - 1) % replicas) for i in range(repl...]
    all_to_all x3, blocking collectives: 76.3 us -> 62.6 us  [exchange(): return lax.all_to_all(pieces, axis, 0, 0, tiled=True)]
    ppermute x3, waiting for transfers between devices: 7.82 us -> 16.3 us  [along_x(): return lax.ppermute(block, 'fsdp', moved)]
    all_to_all x0 -> x1, starting transfers between devices: none -> 7.64 us  [per_device(): lax.all_to_all(shards, 'fsdp', 0, 0, tiled=True, axis_index_groups=along_...]
    ppermute x4 -> x2, starting transfers between devices: 19.5 us -> 12.1 us  [from_other_core(): return lax.ppermute(block, 'fsdp', [(i, i ^ 1) for i in range(owners)])]
    ppermute x3, starting transfers between devices: 14.9 us -> 18 us  [along_x(): return lax.ppermute(block, 'fsdp', moved)]
    pallas_call x3 -> x5, Pallas kernels: 4.19 us -> 7.19 us  [the longest x4 4.49 us: partial_values(): pl.pallas_call(functools.partial(body, which), in_specs=[pl.BlockSpec(mem...]
  transfers between devices with their start and end apart: 7 -> 8, of which waited for: 2 -> 1; matrix products, arithmetic and copies ran while one was open for 0% -> 0% of each run, Pallas kernels for 5% -> 6%
where the time goes in v3:
time: 154 us
  blocking collectives  62.6 us (41%)
  starting transfers between devices  53.9 us (35%)
  waiting for transfers between devices  16.3 us (11%)
  Pallas kernels  15.8 us (10%)
  local copies, waits for them, and re-layouts  3.3 us (2%)
  between operations  1.57 us (1%)
    all_to_all x3, blocking collectives, exchange(): return lax.all_to_all(pieces, axis, 0, 0, tiled=True)  62.6 us
    ppermute x3, starting transfers between devices, along_x(): return lax.ppermute(block, 'fsdp', moved)  18 us
    ppermute x3, waiting for transfers between devices, along_x(): return lax.ppermute(block, 'fsdp', moved)  16.3 us
    ppermute x1, starting transfers between devices, per_device(): lax.ppermute(half[2:], 'dp', [(i, (i - 1) % replicas) for i in range(repl...  12.2 us
    ppermute x2, starting transfers between devices, from_other_core(): return lax.ppermute(block, 'fsdp', [(i, i ^ 1) for i in range(owners)])  12.1 us
    all_to_all x1, starting transfers between devices, per_device(): lax.all_to_all(shards, 'fsdp', 0, 0, tiled=True, axis_index_groups=along_...  7.64 us
    pallas_call x4, Pallas kernels, partial_values(): pl.pallas_call(functools.partial(body, which), in_specs=[pl.BlockSpec(mem...  4.49 us
    ppermute x1, starting transfers between devices, per_device(): lax.ppermute(half[:2], 'dp', [(i, (i + 1) % replicas) for i in range(repl...  4 us
  transfers between devices with their start and end apart: 8, of which 1 were waited for; matrix products, arithmetic and copies ran while one was open for 0% of the time, Pallas kernels for 6%

profile of v3, /device:TPU:1, one launch (start us, length us, event | category | flops | bytes accessed | tf_op | source)
XLA Modules:
  0.0 153.6 jit_solution(14759965904034806504)
XLA Ops:
  0.6 0.7 copy-done.2
  1.4 0.8 copy-done.4
  2.2 0.9 pack.1
  3.1 7.6 %all-to-all-start = ((bf16[8,64,576]{2,1,0:T(8,128)(2,1)}), bf16[8,64,576]{2,1,0:T(8,128)(2,1)S(1)}, u32[]{:S(2)}, u32[]{:S(2)}) async-start(bf16[8,64,576]{2,1,0:T(8,128)(2,1)} %pack.1), calls=%async_computation | async-start | bytes 1310720 | tf_op jit(solution)/shard_map/all_to_all | solution.py:332
  11.5 1.6 %copy-done.6 = bf16[256,4096]{1,0:T(8,128)(2,1)S(1)} copy-done((bf16[256,4096]{1,0:T(8,128)(2,1)S(1)}, bf16[256,4096]{1,0:T(8,128)(2,1)}, u32[]{:S(2)}) %copy-start.6) | copy-done | bytes 2097176
  13.1 2.7 %split.1 = (bf16[256,2048]{1,0:T(8,128)(2,1)S(1)}, bf16[256,2048]{1,0:T(8,128)(2,1)}) custom-call(s32[4]{0:T(128)S(1)} %pad_add_fusion.facts_ref, bf16[256,4096]{1,0:T(8,128)(2,1)S(1)} %copy-done.6), custom_call_target="tpu_custom_call" | custom-call | flops 1073741824 | bytes 4194304 | tf_op jit(solution)/shard_map/split/pallas_call | solution.py:112
  15.8 8.3 %collective-permute-start = (bf16[256,2048]{1,0:T(8,128)(2,1)}, bf16[256,2048]{1,0:T(8,128)(2,1)S(1)}, u32[]{:S(2)}, u32[]{:S(2)}) collective-permute-start(bf16[256,2048]{1,0:T(8,128)(2,1)} %get-tuple-element.18), channel_id=1, source_target_pairs={{0,1},{1,0},{2,3},{3,2},{4,5},{5,4},{6,7},{7,6},{8,9},{9,8},{10,11... | collective-permute-start | bytes 3145736 | tf_op jit(solution)/shard_map/ppermute | solution.py:312
  24.1 10.5 %collective-permute-start.5 = (bf16[8,64,576]{2,1,0:T(8,128)(2,1)S(1)}, bf16[8,64,576]{2,1,0:T(8,128)(2,1)S(1)}, u32[]{:S(2)}, u32[]{:S(2)}) collective-permute-start(bf16[8,64,576]{2,1,0:T(8,128)(2,1)S(1)} %all-to-all-done.block), channel_id=1, source_target_pairs={{0,2},{1,3},{2,4},{3,5},{4,6},{5,7},{6,0},{7,1},{8,10},{9,11},{10,... | collective-permute-start | bytes 1769480 | tf_op jit(solution)/shard_map/ppermute | solution.py:308
  34.7 4.4 %collective-permute-start.1 = (bf16[4,64,576]{2,1,0:T(8,128)(2,1)S(1)}, bf16[4,64,576]{2,1,0:T(8,128)(2,1)S(1)}, u32[]{:S(2)}, u32[]{:S(2)}) collective-permute-start(bf16[4,64,576]{2,1,0:T(8,128)(2,1)S(1)} %constant_dynamic-slice_fusion), channel_id=1, source_target_pairs={{0,4},{1,5},{2,6},{3,7},{4,0},{5,1},{6,2},{7,3},{8,12},{9,13},{10,... | collective-permute-start | bytes 884744 | tf_op jit(solution)/shard_map/ppermute | solution.py:308
  39.1 3.1 %collective-permute-start.4 = (bf16[8,64,576]{2,1,0:T(8,128)(2,1)S(1)}, bf16[8,64,576]{2,1,0:T(8,128)(2,1)S(1)}, u32[]{:S(2)}, u32[]{:S(2)}) collective-permute-start(bf16[8,64,576]{2,1,0:T(8,128)(2,1)S(1)} %all-to-all-done.block), channel_id=1, source_target_pairs={{0,6},{1,7},{2,0},{3,1},{4,2},{5,3},{6,4},{7,5},{8,14},{9,15},{10,... | collective-permute-start | bytes 1769480 | tf_op jit(solution)/shard_map/ppermute | solution.py:308
  42.1 16.3 %collective-permute-done.1.half = bf16[4,64,576]{2,1,0:T(8,128)(2,1)S(1)} collective-permute-done((bf16[4,64,576]{2,1,0:T(8,128)(2,1)S(1)}, bf16[4,64,576]{2,1,0:T(8,128)(2,1)S(1)}, u32[]{:S(2)}, u32[]{:S(2)}) %collective-permute-start.1) | collective-permute-done | bytes 294944 | tf_op jit(solution)/shard_map/ppermute | solution.py:308
  58.5 4.0 %collective-permute-start.2 = (bf16[2,64,576]{2,1,0:T(8,128)(2,1)S(1)}, bf16[2,64,576]{2,1,0:T(8,128)(2,1)S(1)}, u32[]{:S(2)}, u32[]{:S(2)}) collective-permute-start(bf16[2,64,576]{2,1,0:T(8,128)(2,1)S(1)} %get-tuple-element.30), channel_id=1, source_target_pairs={{0,64},{64,128},{128,192},{192,256},{256,320},{320,384},{384,448},... | collective-permute-start | bytes 442376 | tf_op jit(solution)/shard_map/ppermute | solution.py:339
  62.5 12.2 %collective-permute-start.3 = (bf16[2,64,576]{2,1,0:T(8,128)(2,1)S(1)}, bf16[2,64,576]{2,1,0:T(8,128)(2,1)S(1)}, u32[]{:S(2)}, u32[]{:S(2)}) collective-permute-start(bf16[2,64,576]{2,1,0:T(8,128)(2,1)S(1)} %get-tuple-element.29), channel_id=1, source_target_pairs={{0,704},{64,0},{128,64},{192,128},{256,192},{320,256},{384,320},{4... | collective-permute-start | bytes 442376 | tf_op jit(solution)/shard_map/ppermute | solution.py:340
  74.7 1.1 partial.4.rest_1_
  75.9 1.1 partial.5.rest_1_
  77.0 1.1 partial.6.before
  78.2 1.1 partial.7
  79.4 3.8 %collective-permute-start.6 = (f32[256,640]{1,0:T(8,128)S(1)}, f32[256,640]{1,0:T(8,128)S(1)}, u32[]{:S(2)}, u32[]{:S(2)}) collective-permute-start(f32[256,640]{1,0:T(8,128)S(1)} %get-tuple-element.20), channel_id=1, source_target_pairs={{0,1},{1,0},{2,3},{3,2},{4,5},{5,4},{6,7},{7,6},{8,9},{9,8},{10,11... | collective-permute-start | bytes 1966088 | tf_op jit(solution)/shard_map/ppermute | solution.py:312
  83.2 3.0 %probs.1 = (bf16[4,1024,256]{2,1,0:T(8,128)(2,1)S(1)}, bf16[4,256,1024]{2,1,0:T(8,128)(2,1)S(1)}) custom-call(s32[1]{0:T(128)S(6)} %copy.15.length_ref, bf16[256,2048]{1,0:T(8,128)(2,1)S(1)} %copy-done.8, bf16[256,512]{1,0:T(8,128)(2,1)S(1)} %copy-done.10), custom_call_target="tpu_custom_call" | custom-call | flops 2147483648 | bytes 6291456 | tf_op jit(solution)/shard_map/probs/pallas_call | solution.py:57
  86.2 3.1 %grads.1 = bf16[64,40,128]{2,1,0:T(8,128)(2,1)S(1)} custom-call(s32[4]{0:T(128)S(1)} %pad_add_fusion.facts_ref, bf16[256,4096]{1,0:T(8,128)(2,1)S(1)} %copy-done.7, f32[256,640]{1,0:T(8,128)S(1)} %get-tuple-element.19.before, f32[256,640]{1,0:T(8,128)S(1)} %collective-permute-done.6.swapped, bf16[4,1024,256]{2,1,0:T(8,128)(2,1)S(1)} %get-tuple-element.21.probs, ...), custom_call_target="tpu_custom_call" | custom-call | flops 4294967296 | bytes 10485760 | tf_op jit(solution)/shard_map/grads/pallas_call | solution.py:223
  89.3 23.9 %all_to_all.20.pieces_ref = bf16[64,40,128]{2,1,0:T(8,128)(2,1)S(1)} all-to-all(bf16[64,40,128]{2,1,0:T(8,128)(2,1)S(1)} %grads.1), channel_id=1, replica_groups=mesh['dp'=12,'fsdp'=64] {'fsdp'}, dimensions={0} | all-to-all | bytes 1310720 | tf_op jit(solution)/shard_map/all_to_all | solution.py:299
  113.4 20.7 %all_to_all.21.pieces_ref = f32[12,40,128]{2,1,0:T(8,128)S(1)} all-to-all(f32[12,40,128]{2,1,0:T(8,128)S(1)} %fold.1), channel_id=1, replica_groups=mesh['dp'=12,'fsdp'=64] {'dp'}, dimensions={0} | all-to-all | bytes 491520 | tf_op jit(solution)/shard_map/all_to_all | solution.py:299
  134.1 0.8 owner.1
  134.9 18.0 %all_to_all.22.pieces_ref = f32[64,4,128]{2,1,0:T(4,128)S(1)} all-to-all(f32[64,4,128]{2,1,0:T(4,128)S(1)} %get-tuple-element.24), channel_id=1, replica_groups=mesh['dp'=12,'fsdp'=64] {'fsdp'}, dimensions={0} | all-to-all | bytes 262144 | tf_op jit(solution)/shard_map/all_to_all | solution.py:299
  (31 shorter events, 1.1 us)
Async XLA Ops:
  0.6 0.8 copy-start.2
  1.4 0.8 copy-start.4
  3.1 21.0 %all-to-all-start = ((bf16[8,64,576]{2,1,0:T(8,128)(2,1)}), bf16[8,64,576]{2,1,0:T(8,128)(2,1)S(1)}, u32[]{:S(2)}, u32[]{:S(2)}) async-start(bf16[8,64,576]{2,1,0:T(8,128)(2,1)} %pack.1), calls=%async_computation | async-start | bytes 1310720 | tf_op jit(solution)/shard_map/all_to_all | solution.py:332
  11.5 1.6 %copy-start.6 = (bf16[256,4096]{1,0:T(8,128)(2,1)S(1)}, bf16[256,4096]{1,0:T(8,128)(2,1)}, u32[]{:S(2)}) copy-start(bf16[256,4096]{1,0:T(8,128)(2,1)} %hidden.3) | copy-start | bytes 6291460
  15.8 58.9 %collective-permute-start = (bf16[256,2048]{1,0:T(8,128)(2,1)}, bf16[256,2048]{1,0:T(8,128)(2,1)S(1)}, u32[]{:S(2)}, u32[]{:S(2)}) collective-permute-start(bf16[256,2048]{1,0:T(8,128)(2,1)} %get-tuple-element.18), channel_id=1, source_target_pairs={{0,1},{1,0},{2,3},{3,2},{4,5},{5,4},{6,7},{7,6},{8,9},{9,8},{10,11... | collective-permute-start | bytes 3145736 | tf_op jit(solution)/shard_map/ppermute | solution.py:312
  24.1 51.7 %collective-permute-start.5 = (bf16[8,64,576]{2,1,0:T(8,128)(2,1)S(1)}, bf16[8,64,576]{2,1,0:T(8,128)(2,1)S(1)}, u32[]{:S(2)}, u32[]{:S(2)}) collective-permute-start(bf16[8,64,576]{2,1,0:T(8,128)(2,1)S(1)} %all-to-all-done.block), channel_id=1, source_target_pairs={{0,2},{1,3},{2,4},{3,5},{4,6},{5,7},{6,0},{7,1},{8,10},{9,11},{10,... | collective-permute-start | bytes 1769480 | tf_op jit(solution)/shard_map/ppermute | solution.py:308
  34.7 23.7 %collective-permute-start.1 = (bf16[4,64,576]{2,1,0:T(8,128)(2,1)S(1)}, bf16[4,64,576]{2,1,0:T(8,128)(2,1)S(1)}, u32[]{:S(2)}, u32[]{:S(2)}) collective-permute-start(bf16[4,64,576]{2,1,0:T(8,128)(2,1)S(1)} %constant_dynamic-slice_fusion), channel_id=1, source_target_pairs={{0,4},{1,5},{2,6},{3,7},{4,0},{5,1},{6,2},{7,3},{8,12},{9,13},{10,... | collective-permute-start | bytes 884744 | tf_op jit(solution)/shard_map/ppermute | solution.py:308
  39.1 37.9 %collective-permute-start.4 = (bf16[8,64,576]{2,1,0:T(8,128)(2,1)S(1)}, bf16[8,64,576]{2,1,0:T(8,128)(2,1)S(1)}, u32[]{:S(2)}, u32[]{:S(2)}) collective-permute-start(bf16[8,64,576]{2,1,0:T(8,128)(2,1)S(1)} %all-to-all-done.block), channel_id=1, source_target_pairs={{0,6},{1,7},{2,0},{3,1},{4,2},{5,3},{6,4},{7,5},{8,14},{9,15},{10,... | collective-permute-start | bytes 1769480 | tf_op jit(solution)/shard_map/ppermute | solution.py:308
  58.5 19.7 %collective-permute-start.2 = (bf16[2,64,576]{2,1,0:T(8,128)(2,1)S(1)}, bf16[2,64,576]{2,1,0:T(8,128)(2,1)S(1)}, u32[]{:S(2)}, u32[]{:S(2)}) collective-permute-start(bf16[2,64,576]{2,1,0:T(8,128)(2,1)S(1)} %get-tuple-element.30), channel_id=1, source_target_pairs={{0,64},{64,128},{128,192},{192,256},{256,320},{320,384},{384,448},... | collective-permute-start | bytes 442376 | tf_op jit(solution)/shard_map/ppermute | solution.py:339
  62.5 15.7 %collective-permute-start.3 = (bf16[2,64,576]{2,1,0:T(8,128)(2,1)S(1)}, bf16[2,64,576]{2,1,0:T(8,128)(2,1)S(1)}, u32[]{:S(2)}, u32[]{:S(2)}) collective-permute-start(bf16[2,64,576]{2,1,0:T(8,128)(2,1)S(1)} %get-tuple-element.29), channel_id=1, source_target_pairs={{0,704},{64,0},{128,64},{192,128},{256,192},{320,256},{384,320},{4... | collective-permute-start | bytes 442376 | tf_op jit(solution)/shard_map/ppermute | solution.py:340
  78.1 5.0 %copy-start.8 = (bf16[256,2048]{1,0:T(8,128)(2,1)S(1)}, bf16[256,2048]{1,0:T(8,128)(2,1)}, u32[]{:S(2)}) copy-start(bf16[256,2048]{1,0:T(8,128)(2,1)} %q_ref.1) | copy-start | bytes 3145732
  78.2 5.0 %copy-start.10 = (bf16[256,512]{1,0:T(8,128)(2,1)S(1)}, bf16[256,512]{1,0:T(8,128)(2,1)}, u32[]{:S(2)}) copy-start(bf16[256,512]{1,0:T(8,128)(2,1)} %k_ref.1) | copy-start | bytes 786436
  79.3 6.9 %copy-start = (f32[64,512]{1,0:T(8,128)S(1)}, f32[64,512]{1,0:T(8,128)}, u32[]{:S(2)}) copy-start(f32[64,512]{1,0:T(8,128)} %up_ref.3) | copy-start | bytes 393220
  79.3 6.9 %copy-start.7 = (bf16[256,4096]{1,0:T(8,128)(2,1)S(1)}, bf16[256,4096]{1,0:T(8,128)(2,1)}, u32[]{:S(2)}) copy-start(bf16[256,4096]{1,0:T(8,128)(2,1)} %hidden.3) | copy-start | bytes 6291460
  79.3 6.9 %copy-start.9 = (bf16[256,2048]{1,0:T(8,128)(2,1)S(1)}, bf16[256,2048]{1,0:T(8,128)(2,1)}, u32[]{:S(2)}) copy-start(bf16[256,2048]{1,0:T(8,128)(2,1)} %target.1) | copy-start | bytes 3145732
  79.4 6.8 %collective-permute-start.6 = (f32[256,640]{1,0:T(8,128)S(1)}, f32[256,640]{1,0:T(8,128)S(1)}, u32[]{:S(2)}, u32[]{:S(2)}) collective-permute-start(f32[256,640]{1,0:T(8,128)S(1)} %get-tuple-element.20), channel_id=1, source_target_pairs={{0,1},{1,0},{2,3},{3,2},{4,5},{5,4},{6,7},{7,6},{8,9},{9,8},{10,11... | collective-permute-start | bytes 1966088 | tf_op jit(solution)/shard_map/ppermute | solution.py:312
  89.3 44.8 %copy-start.3 = (f32[64,64]{1,0:T(8,128)S(1)}, f32[64,64]{1,0:T(8,128)}, u32[]{:S(2)}) copy-start(f32[64,64]{1,0:T(8,128)} %down_ref.3) | copy-start | bytes 49156
  89.3 44.7 %copy-start.5 = (f32[64,64]{1,0:T(8,128)S(1)}, f32[64,64]{1,0:T(8,128)}, u32[]{:S(2)}) copy-start(f32[64,64]{1,0:T(8,128)} %average_ref.2) | copy-start | bytes 49156
  89.3 63.6 %copy-start.1 = (f32[64,512]{1,0:T(8,128)S(1)}, f32[64,512]{1,0:T(8,128)}, u32[]{:S(2)}) copy-start(f32[64,512]{1,0:T(8,128)} %average_ref.3) | copy-start | bytes 393220

commit v4 on v3

--- a/solution.py
+++ b/solution.py
@@ -123,18 +123,19 @@
 def partial_kernel(which, facts_ref, mine, theirs, *rest):
     *blocks, before, out = rest
     column = lax.rem(facts_ref[2] + (4 - which), 4) * 512
-    half = facts_ref[3] * 256
     for i, tokens in enumerate((mine, theirs)):
         if len(blocks) == 1:
-            part = nn(
-                tokens[:, pl.ds(pl.multiple_of(column, 512), 512)], blocks[0][...].reshape(512, WIDTH)
-            )
+            part = nn(tokens[:, pl.ds(pl.multiple_of(column, 512), 512)], blocks[0][...].reshape(512, WIDTH))
         else:
-            part = nn(
-                tokens[:, pl.ds(pl.multiple_of(column + half, 256), 256)], blocks[0][...].reshape(256, WIDTH)
-            )
-            rows = jnp.concatenate([blocks[1][...].reshape(128, WIDTH), blocks[2][...].reshape(128, WIDTH)], axis=0)
-            part += nn(tokens[:, pl.ds(pl.multiple_of(column + (256 - half), 256), 256)], rows)
+            part = None
+            for j in (0, 2):
+                left, right = [], []
+                for k in (j, j + 1):
+                    quarter = facts_ref[3] ^ k
+                    left.append(tokens[:, pl.ds(pl.multiple_of(column + quarter * 128, 128), 128)])
+                    right.append(blocks[k][...].reshape(128, WIDTH))
+                more = nn(jnp.concatenate(left, axis=1), jnp.concatenate(right, axis=0))
+                part = more if part is None else part + more
         out[i] = part if before is None else part + before[i]
 
 
@@ -142,20 +143,19 @@
     partial_kernel(which, facts_ref, mine, theirs, block, None, out)
 
 
-def last_partial_kernel(which, facts_ref, mine, theirs, half, low, high, before, own, other):
+def last_partial_kernel(which, facts_ref, mine, theirs, block, before, own, other):
     class Outs:
         def __setitem__(self, i, value):
             (own, other)[i][:, :WIDTH] = value
 
-    partial_kernel(which, facts_ref, mine, theirs, half, low, high, before, Outs())
+    partial_kernel(which, facts_ref, mine, theirs, block, before, Outs())
     for out in (own, other):
         out[:, WIDTH:] = jnp.zeros((TOK, PADDED - WIDTH), jnp.float32)
 
 
-def partial_values(facts, mine, theirs, blocks, which, before=None):
+def partial_values(facts, mine, theirs, blocks, which, before=None, last=False):
     vmem = pl.BlockSpec(memory_space=pltpu.VMEM)
     given = tuple(blocks) + (() if before is None else (before,))
-    last = len(blocks) > 1
     body = last_partial_kernel if last else first_partial_kernel if before is None else partial_kernel
     shape = jax.ShapeDtypeStruct((TOK, PADDED), jnp.float32)
     return pl.pallas_call(
@@ -306,6 +306,15 @@
 def along_x(block, owners, shift):
     moved = [(i, i // 8 * 8 + (i + 2 * shift) % 8) for i in range(owners)]
     return lax.ppermute(block, "fsdp", moved)
+
+
+def from_neighbour(part, owners, replicas, y, z):
+    moved = [
+        ((d + z) % replicas * owners + (i + 8 * y) % owners, d * owners + i)
+        for d in range(replicas)
+        for i in range(owners)
+    ]
+    return lax.ppermute(part, ("dp", "fsdp"), moved)
 
 
 def from_other_core(block, owners):
@@ -326,22 +335,24 @@
 ):
     owners, replicas = lax.axis_size("fsdp"), lax.axis_size("dp")
     place = lax.axis_index("fsdp").astype(jnp.int32)
-    parity = lax.axis_index("dp").astype(jnp.int32) & 1
-    facts = jnp.stack([lengths[0], place & 1, (place >> 1) & 3, parity])
+    plane = lax.axis_index("dp").astype(jnp.int32)
+    quarter = (plane & 1) * 2 + ((place >> 3) & 1)
+    facts = jnp.stack([lengths[0], place & 1, (place >> 1) & 3, quarter])
     shards = packed_shard(value_weight_frozen, adapter_down_map, owners // 8)
     own = lax.all_to_all(shards, "fsdp", 0, 0, tiled=True, axis_index_groups=along_y(owners))
     mine, send = split_hidden(facts, hidden)
     theirs = from_other_core(send, owners)
     probs, probs_t = attention_probs(lengths, queries, keys)
-    half = along_x(lax.dynamic_slice_in_dim(own, parity * 4, 4, axis=0), owners, 2)
+    part = along_x(lax.dynamic_slice_in_dim(own, quarter * 2, 2, axis=0), owners, 2)
     near = along_x(own, owners, 1)
     far = along_x(own, owners, 3)
-    low = lax.ppermute(half[:2], "dp", [(i, (i + 1) % replicas) for i in range(replicas)])
-    high = lax.ppermute(half[2:], "dp", [(i, (i - 1) % replicas) for i in range(replicas)])
+    beside = from_neighbour(part, owners, replicas, 1, 0)
+    behind = from_neighbour(part, owners, replicas, 0, 1)
+    corner = from_neighbour(part, owners, replicas, 1, 1)
     total = None
-    for shift, block in ((0, own), (1, near), (3, far)):
-        total = partial_values(facts, mine, theirs, (block,), shift, total)
-    total, other = partial_values(facts, mine, theirs, (half, low, high), 2, total)
+    for shift, given in ((0, (own,)), (3, (far,)), (2, (part, beside, behind, corner))):
+        total = partial_values(facts, mine, theirs, given, shift, total)
+    total, other = partial_values(facts, mine, theirs, (near,), 1, total, last=True)
     swapped = from_other_core(other, owners)
     pieces = gradient_pieces(facts, hidden, total, swapped, probs, probs_t, target, adapter_up_map)
     summed = fold(exchange(pieces, "fsdp"), replicas)

time: 154 us -> 158 us (1.026)
  starting transfers between devices: 53.9 us -> 56.7 us
    ppermute x2 -> x3, waiting for transfers between devices: 0.01 us -> 2.19 us  [from_neighbour(): return lax.ppermute(part, ('dp', 'fsdp'), moved)]
    ppermute x2 -> x3, starting transfers between devices: 16.2 us -> 18.1 us  [from_neighbour(): return lax.ppermute(part, ('dp', 'fsdp'), moved)]
  transfers between devices with their start and end apart: 8 -> 9, of which waited for: 1 -> 2; matrix products, arithmetic and copies ran while one was open for 0% -> 0% of each run, Pallas kernels for 6% -> 6%
where the time goes in v4:
time: 158 us
  blocking collectives  61.9 us (39%)
  starting transfers between devices  56.7 us (36%)
  waiting for transfers between devices  17.8 us (11%)
  Pallas kernels  16.4 us (10%)
  local copies, waits for them, and re-layouts  3.26 us (2%)
    all_to_all x3, blocking collectives, exchange(): return lax.all_to_all(pieces, axis, 0, 0, tiled=True)  61.9 us
    ppermute x3, starting transfers between devices, from_neighbour(): return lax.ppermute(part, ('dp', 'fsdp'), moved)  18.1 us
    ppermute x3, starting transfers between devices, along_x(): return lax.ppermute(block, 'fsdp', moved)  17.4 us
    ppermute x3, waiting for transfers between devices, along_x(): return lax.ppermute(block, 'fsdp', moved)  15.6 us
    ppermute x2, starting transfers between devices, from_other_core(): return lax.ppermute(block, 'fsdp', [(i, i ^ 1) for i in range(owners)])  13.6 us
    all_to_all x1, starting transfers between devices, per_device(): lax.all_to_all(shards, 'fsdp', 0, 0, tiled=True, axis_index_groups=along_...  7.64 us
    pallas_call x4, Pallas kernels, partial_values(): pl.pallas_call(functools.partial(body, which), in_specs=[pl.BlockSpec(mem...  5.07 us
    unnamed x22, local copies, waits for them, and re-layouts  3.24 us
  transfers between devices with their start and end apart: 9, of which 2 were waited for; matrix products, arithmetic and copies ran while one was open for 0% of the time, Pallas kernels for 6%

profile of v4, /device:TPU:1, one launch (start us, length us, event | category | flops | bytes accessed | tf_op | source)
XLA Modules:
  0.0 157.8 jit_solution(5517025510166749784)
XLA Ops:
  1.4 0.8 copy-done.4
  2.2 0.9 pack.1
  3.1 7.6 %all-to-all-start = ((bf16[8,64,576]{2,1,0:T(8,128)(2,1)}), bf16[8,64,576]{2,1,0:T(8,128)(2,1)S(1)}, u32[]{:S(2)}, u32[]{:S(2)}) async-start(bf16[8,64,576]{2,1,0:T(8,128)(2,1)} %pack.1), calls=%async_computation | async-start | bytes 1310720 | tf_op jit(solution)/shard_map/all_to_all | solution.py:342
  11.5 1.6 %copy-done.6 = bf16[256,4096]{1,0:T(8,128)(2,1)S(1)} copy-done((bf16[256,4096]{1,0:T(8,128)(2,1)S(1)}, bf16[256,4096]{1,0:T(8,128)(2,1)}, u32[]{:S(2)}) %copy-start.6) | copy-done | bytes 2097176
  13.1 2.7 %split.1 = (bf16[256,2048]{1,0:T(8,128)(2,1)S(1)}, bf16[256,2048]{1,0:T(8,128)(2,1)}) custom-call(s32[4]{0:T(128)S(1)} %pad_add_fusion.facts_ref, bf16[256,4096]{1,0:T(8,128)(2,1)S(1)} %copy-done.6), custom_call_target="tpu_custom_call" | custom-call | flops 1073741824 | bytes 4194304 | tf_op jit(solution)/shard_map/split/pallas_call | solution.py:112
  15.8 8.3 %collective-permute-start = (bf16[256,2048]{1,0:T(8,128)(2,1)}, bf16[256,2048]{1,0:T(8,128)(2,1)S(1)}, u32[]{:S(2)}, u32[]{:S(2)}) collective-permute-start(bf16[256,2048]{1,0:T(8,128)(2,1)} %get-tuple-element.18), channel_id=1, source_target_pairs={{0,1},{1,0},{2,3},{3,2},{4,5},{5,4},{6,7},{7,6},{8,9},{9,8},{10,11... | collective-permute-start | bytes 3145736 | tf_op jit(solution)/shard_map/ppermute | solution.py:321
  24.1 11.8 %collective-permute-start.6 = (bf16[8,64,576]{2,1,0:T(8,128)(2,1)S(1)}, bf16[8,64,576]{2,1,0:T(8,128)(2,1)}, u32[]{:S(2)}, u32[]{:S(2)}) collective-permute-start(bf16[8,64,576]{2,1,0:T(8,128)(2,1)S(1)} %all-to-all-done.block), channel_id=1, source_target_pairs={{0,6},{1,7},{2,0},{3,1},{4,2},{5,3},{6,4},{7,5},{8,14},{9,15},{10,... | collective-permute-start | bytes 1769480 | tf_op jit(solution)/shard_map/ppermute | solution.py:308
  35.9 1.9 %collective-permute-start.1 = (bf16[8,64,576]{2,1,0:T(8,128)(2,1)S(1)}, bf16[8,64,576]{2,1,0:T(8,128)(2,1)S(1)}, u32[]{:S(2)}, u32[]{:S(2)}) collective-permute-start(bf16[8,64,576]{2,1,0:T(8,128)(2,1)S(1)} %all-to-all-done.block), channel_id=1, source_target_pairs={{0,2},{1,3},{2,4},{3,5},{4,6},{5,7},{6,0},{7,1},{8,10},{9,11},{10,... | collective-permute-start | bytes 1769480 | tf_op jit(solution)/shard_map/ppermute | solution.py:308
  37.9 3.6 %collective-permute-start.2 = (bf16[2,64,576]{2,1,0:T(8,128)(2,1)S(1)}, bf16[2,64,576]{2,1,0:T(8,128)(2,1)S(1)}, u32[]{:S(2)}, u32[]{:S(2)}) collective-permute-start(bf16[2,64,576]{2,1,0:T(8,128)(2,1)S(1)} %constant_dynamic-slice_fusion), channel_id=1, source_target_pairs={{0,4},{1,5},{2,6},{3,7},{4,0},{5,1},{6,2},{7,3},{8,12},{9,13},{10,... | collective-permute-start | bytes 442376 | tf_op jit(solution)/shard_map/ppermute | solution.py:308
  41.5 15.6 %collective-permute-done.2.rest_0_ = bf16[2,64,576]{2,1,0:T(8,128)(2,1)S(1)} collective-permute-done((bf16[2,64,576]{2,1,0:T(8,128)(2,1)S(1)}, bf16[2,64,576]{2,1,0:T(8,128)(2,1)S(1)}, u32[]{:S(2)}, u32[]{:S(2)}) %collective-permute-start.2) | collective-permute-done | bytes 147488 | tf_op jit(solution)/shard_map/ppermute | solution.py:308
  57.2 1.9 %collective-permute-start.3 = (bf16[2,64,576]{2,1,0:T(8,128)(2,1)S(1)}, bf16[2,64,576]{2,1,0:T(8,128)(2,1)S(1)}, u32[]{:S(2)}, u32[]{:S(2)}) collective-permute-start(bf16[2,64,576]{2,1,0:T(8,128)(2,1)S(1)} %collective-permute-done.2.rest_0_), channel_id=1, source_target_pairs={{8,0},{9,1},{10,2},{11,3},{12,4},{13,5},{14,6},{15,7},{16,8},{17,9... | collective-permute-start | bytes 442376 | tf_op jit(solution)/shard_map/ppermute | solution.py:317
  59.1 14.3 %collective-permute-start.4 = (bf16[2,64,576]{2,1,0:T(8,128)(2,1)S(1)}, bf16[2,64,576]{2,1,0:T(8,128)(2,1)S(1)}, u32[]{:S(2)}, u32[]{:S(2)}) collective-permute-start(bf16[2,64,576]{2,1,0:T(8,128)(2,1)S(1)} %collective-permute-done.2.rest_0_), channel_id=1, source_target_pairs={{64,0},{65,1},{66,2},{67,3},{68,4},{69,5},{70,6},{71,7},{72,8},{73... | collective-permute-start | bytes 442376 | tf_op jit(solution)/shard_map/ppermute | solution.py:317
  73.4 1.9 %collective-permute-start.5 = (bf16[2,64,576]{2,1,0:T(8,128)(2,1)S(1)}, bf16[2,64,576]{2,1,0:T(8,128)(2,1)S(1)}, u32[]{:S(2)}, u32[]{:S(2)}) collective-permute-start(bf16[2,64,576]{2,1,0:T(8,128)(2,1)S(1)} %collective-permute-done.2.rest_0_), channel_id=1, source_target_pairs={{72,0},{73,1},{74,2},{75,3},{76,4},{77,5},{78,6},{79,7},{80,8},{81... | collective-permute-start | bytes 442376 | tf_op jit(solution)/shard_map/ppermute | solution.py:317
  75.3 1.1 partial.4.rest_1_
  76.5 1.7 %partial.5.rest_4_ = f32[2,256,576]{2,1,0:T(8,128)S(1)} custom-call(s32[4]{0:T(128)S(1)} %pad_add_fusion.facts_ref, bf16[256,2048]{1,0:T(8,128)(2,1)S(1)} %get-tuple-element.17.mine, bf16[256,2048]{1,0:T(8,128)(2,1)S(1)} %collective-permute-done.theirs, bf16[8,64,576]{2,1,0:T(8,128)(2,1)} %collective-permute-done.6.rest_0_, f32[2,256,576]{2,1,0:T(8,128)S(1)} %partial.4.rest_1_), custom_call_target="tpu_custom_call" | custom-call | flops 536870912 | bytes 2097152 | tf_op jit(solution)/shard_map/partial/pallas_call | solution.py:161
  78.2 2.2 %collective-permute-done.5.rest_3_ = bf16[2,64,576]{2,1,0:T(8,128)(2,1)S(1)} collective-permute-done((bf16[2,64,576]{2,1,0:T(8,128)(2,1)S(1)}, bf16[2,64,576]{2,1,0:T(8,128)(2,1)S(1)}, u32[]{:S(2)}, u32[]{:S(2)}) %collective-permute-start.5) | collective-permute-done | bytes 147488 | tf_op jit(solution)/shard_map/ppermute | solution.py:317
  80.4 1.1 partial.6.before
  81.5 1.1 partial.7
  82.7 5.3 %collective-permute-start.7 = (f32[256,640]{1,0:T(8,128)S(1)}, f32[256,640]{1,0:T(8,128)S(1)}, u32[]{:S(2)}, u32[]{:S(2)}) collective-permute-start(f32[256,640]{1,0:T(8,128)S(1)} %get-tuple-element.20), channel_id=1, source_target_pairs={{0,1},{1,0},{2,3},{3,2},{4,5},{5,4},{6,7},{7,6},{8,9},{9,8},{10,11... | collective-permute-start | bytes 1966088 | tf_op jit(solution)/shard_map/ppermute | solution.py:321
  88.0 3.0 %probs.1 = (bf16[4,1024,256]{2,1,0:T(8,128)(2,1)S(1)}, bf16[4,256,1024]{2,1,0:T(8,128)(2,1)S(1)}) custom-call(s32[1]{0:T(128)S(6)} %copy.15.length_ref, bf16[256,2048]{1,0:T(8,128)(2,1)S(1)} %copy-done.8, bf16[256,512]{1,0:T(8,128)(2,1)S(1)} %copy-done.10), custom_call_target="tpu_custom_call" | custom-call | flops 2147483648 | bytes 6291456 | tf_op jit(solution)/shard_map/probs/pallas_call | solution.py:57
  91.1 3.1 %grads.1 = bf16[64,40,128]{2,1,0:T(8,128)(2,1)S(1)} custom-call(s32[4]{0:T(128)S(1)} %pad_add_fusion.facts_ref, bf16[256,4096]{1,0:T(8,128)(2,1)S(1)} %copy-done.7, f32[256,640]{1,0:T(8,128)S(1)} %get-tuple-element.19.before, f32[256,640]{1,0:T(8,128)S(1)} %collective-permute-done.7.swapped, bf16[4,1024,256]{2,1,0:T(8,128)(2,1)S(1)} %get-tuple-element.21.probs, ...), custom_call_target="tpu_custom_call" | custom-call | flops 4294967296 | bytes 10485760 | tf_op jit(solution)/shard_map/grads/pallas_call | solution.py:223
  94.2 25.1 %all_to_all.20.pieces_ref = bf16[64,40,128]{2,1,0:T(8,128)(2,1)S(1)} all-to-all(bf16[64,40,128]{2,1,0:T(8,128)(2,1)S(1)} %grads.1), channel_id=1, replica_groups=mesh['dp'=12,'fsdp'=64] {'fsdp'}, dimensions={0} | all-to-all | bytes 1310720 | tf_op jit(solution)/shard_map/all_to_all | solution.py:299
  119.4 18.5 %all_to_all.21.pieces_ref = f32[12,40,128]{2,1,0:T(8,128)S(1)} all-to-all(f32[12,40,128]{2,1,0:T(8,128)S(1)} %fold.1), channel_id=1, replica_groups=mesh['dp'=12,'fsdp'=64] {'dp'}, dimensions={0} | all-to-all | bytes 491520 | tf_op jit(solution)/shard_map/all_to_all | solution.py:299
  138.7 18.4 %all_to_all.22.pieces_ref = f32[64,4,128]{2,1,0:T(4,128)S(1)} all-to-all(f32[64,4,128]{2,1,0:T(4,128)S(1)} %get-tuple-element.24), channel_id=1, replica_groups=mesh['dp'=12,'fsdp'=64] {'fsdp'}, dimensions={0} | all-to-all | bytes 262144 | tf_op jit(solution)/shard_map/all_to_all | solution.py:299
  (32 shorter events, 2.6 us)
Async XLA Ops:
  0.6 0.8 copy-start.2
  1.4 0.8 copy-start.4
  3.1 21.0 %all-to-all-start = ((bf16[8,64,576]{2,1,0:T(8,128)(2,1)}), bf16[8,64,576]{2,1,0:T(8,128)(2,1)S(1)}, u32[]{:S(2)}, u32[]{:S(2)}) async-start(bf16[8,64,576]{2,1,0:T(8,128)(2,1)} %pack.1), calls=%async_computation | async-start | bytes 1310720 | tf_op jit(solution)/shard_map/all_to_all | solution.py:342
  11.5 1.6 %copy-start.6 = (bf16[256,4096]{1,0:T(8,128)(2,1)S(1)}, bf16[256,4096]{1,0:T(8,128)(2,1)}, u32[]{:S(2)}) copy-start(bf16[256,4096]{1,0:T(8,128)(2,1)} %hidden.3) | copy-start | bytes 6291460
  15.8 57.6 %collective-permute-start = (bf16[256,2048]{1,0:T(8,128)(2,1)}, bf16[256,2048]{1,0:T(8,128)(2,1)S(1)}, u32[]{:S(2)}, u32[]{:S(2)}) collective-permute-start(bf16[256,2048]{1,0:T(8,128)(2,1)} %get-tuple-element.18), channel_id=1, source_target_pairs={{0,1},{1,0},{2,3},{3,2},{4,5},{5,4},{6,7},{7,6},{8,9},{9,8},{10,11... | collective-permute-start | bytes 3145736 | tf_op jit(solution)/shard_map/ppermute | solution.py:321
  24.1 52.3 %collective-permute-start.6 = (bf16[8,64,576]{2,1,0:T(8,128)(2,1)S(1)}, bf16[8,64,576]{2,1,0:T(8,128)(2,1)}, u32[]{:S(2)}, u32[]{:S(2)}) collective-permute-start(bf16[8,64,576]{2,1,0:T(8,128)(2,1)S(1)} %all-to-all-done.block), channel_id=1, source_target_pairs={{0,6},{1,7},{2,0},{3,1},{4,2},{5,3},{6,4},{7,5},{8,14},{9,15},{10,... | collective-permute-start | bytes 1769480 | tf_op jit(solution)/shard_map/ppermute | solution.py:308
  35.9 45.6 %collective-permute-start.1 = (bf16[8,64,576]{2,1,0:T(8,128)(2,1)S(1)}, bf16[8,64,576]{2,1,0:T(8,128)(2,1)S(1)}, u32[]{:S(2)}, u32[]{:S(2)}) collective-permute-start(bf16[8,64,576]{2,1,0:T(8,128)(2,1)S(1)} %all-to-all-done.block), channel_id=1, source_target_pairs={{0,2},{1,3},{2,4},{3,5},{4,6},{5,7},{6,0},{7,1},{8,10},{9,11},{10,... | collective-permute-start | bytes 1769480 | tf_op jit(solution)/shard_map/ppermute | solution.py:308
  37.9 19.3 %collective-permute-start.2 = (bf16[2,64,576]{2,1,0:T(8,128)(2,1)S(1)}, bf16[2,64,576]{2,1,0:T(8,128)(2,1)S(1)}, u32[]{:S(2)}, u32[]{:S(2)}) collective-permute-start(bf16[2,64,576]{2,1,0:T(8,128)(2,1)S(1)} %constant_dynamic-slice_fusion), channel_id=1, source_target_pairs={{0,4},{1,5},{2,6},{3,7},{4,0},{5,1},{6,2},{7,3},{8,12},{9,13},{10,... | collective-permute-start | bytes 442376 | tf_op jit(solution)/shard_map/ppermute | solution.py:308
  57.2 21.0 %collective-permute-start.3 = (bf16[2,64,576]{2,1,0:T(8,128)(2,1)S(1)}, bf16[2,64,576]{2,1,0:T(8,128)(2,1)S(1)}, u32[]{:S(2)}, u32[]{:S(2)}) collective-permute-start(bf16[2,64,576]{2,1,0:T(8,128)(2,1)S(1)} %collective-permute-done.2.rest_0_), channel_id=1, source_target_pairs={{8,0},{9,1},{10,2},{11,3},{12,4},{13,5},{14,6},{15,7},{16,8},{17,9... | collective-permute-start | bytes 442376 | tf_op jit(solution)/shard_map/ppermute | solution.py:317
  59.1 19.1 %collective-permute-start.4 = (bf16[2,64,576]{2,1,0:T(8,128)(2,1)S(1)}, bf16[2,64,576]{2,1,0:T(8,128)(2,1)S(1)}, u32[]{:S(2)}, u32[]{:S(2)}) collective-permute-start(bf16[2,64,576]{2,1,0:T(8,128)(2,1)S(1)} %collective-permute-done.2.rest_0_), channel_id=1, source_target_pairs={{64,0},{65,1},{66,2},{67,3},{68,4},{69,5},{70,6},{71,7},{72,8},{73... | collective-permute-start | bytes 442376 | tf_op jit(solution)/shard_map/ppermute | solution.py:317
  73.4 7.0 %collective-permute-start.5 = (bf16[2,64,576]{2,1,0:T(8,128)(2,1)S(1)}, bf16[2,64,576]{2,1,0:T(8,128)(2,1)S(1)}, u32[]{:S(2)}, u32[]{:S(2)}) collective-permute-start(bf16[2,64,576]{2,1,0:T(8,128)(2,1)S(1)} %collective-permute-done.2.rest_0_), channel_id=1, source_target_pairs={{72,0},{73,1},{74,2},{75,3},{76,4},{77,5},{78,6},{79,7},{80,8},{81... | collective-permute-start | bytes 442376 | tf_op jit(solution)/shard_map/ppermute | solution.py:317
  81.5 6.5 %copy-start.8 = (bf16[256,2048]{1,0:T(8,128)(2,1)S(1)}, bf16[256,2048]{1,0:T(8,128)(2,1)}, u32[]{:S(2)}) copy-start(bf16[256,2048]{1,0:T(8,128)(2,1)} %q_ref.1) | copy-start | bytes 3145732
  81.5 6.5 %copy-start.10 = (bf16[256,512]{1,0:T(8,128)(2,1)S(1)}, bf16[256,512]{1,0:T(8,128)(2,1)}, u32[]{:S(2)}) copy-start(bf16[256,512]{1,0:T(8,128)(2,1)} %k_ref.1) | copy-start | bytes 786436
  82.7 8.3 %copy-start = (f32[64,512]{1,0:T(8,128)S(1)}, f32[64,512]{1,0:T(8,128)}, u32[]{:S(2)}) copy-start(f32[64,512]{1,0:T(8,128)} %up_ref.3) | copy-start | bytes 393220
  82.7 8.3 %copy-start.7 = (bf16[256,4096]{1,0:T(8,128)(2,1)S(1)}, bf16[256,4096]{1,0:T(8,128)(2,1)}, u32[]{:S(2)}) copy-start(bf16[256,4096]{1,0:T(8,128)(2,1)} %hidden.3) | copy-start | bytes 6291460
  82.7 8.3 %copy-start.9 = (bf16[256,2048]{1,0:T(8,128)(2,1)S(1)}, bf16[256,2048]{1,0:T(8,128)(2,1)}, u32[]{:S(2)}) copy-start(bf16[256,2048]{1,0:T(8,128)(2,1)} %target.1) | copy-start | bytes 3145732
  82.7 8.3 %collective-permute-start.7 = (f32[256,640]{1,0:T(8,128)S(1)}, f32[256,640]{1,0:T(8,128)S(1)}, u32[]{:S(2)}, u32[]{:S(2)}) collective-permute-start(f32[256,640]{1,0:T(8,128)S(1)} %get-tuple-element.20), channel_id=1, source_target_pairs={{0,1},{1,0},{2,3},{3,2},{4,5},{5,4},{6,7},{7,6},{8,9},{9,8},{10,11... | collective-permute-start | bytes 1966088 | tf_op jit(solution)/shard_map/ppermute | solution.py:321
  94.2 43.7 %copy-start.3 = (f32[64,64]{1,0:T(8,128)S(1)}, f32[64,64]{1,0:T(8,128)}, u32[]{:S(2)}) copy-start(f32[64,64]{1,0:T(8,128)} %down_ref.3) | copy-start | bytes 49156
  94.2 43.7 %copy-start.5 = (f32[64,64]{1,0:T(8,128)S(1)}, f32[64,64]{1,0:T(8,128)}, u32[]{:S(2)}) copy-start(f32[64,64]{1,0:T(8,128)} %average_ref.2) | copy-start | bytes 49156
  94.2 62.9 %copy-start.1 = (f32[64,512]{1,0:T(8,128)S(1)}, f32[64,512]{1,0:T(8,128)}, u32[]{:S(2)}) copy-start(f32[64,512]{1,0:T(8,128)} %average_ref.3) | copy-start | bytes 393220

commit v5 on v4

--- a/solution.py
+++ b/solution.py
@@ -70,7 +70,7 @@
             shape((KEY_VALUE_HEADS, GROUP * TOK, TOK), jnp.bfloat16),
             shape((KEY_VALUE_HEADS, TOK, GROUP * TOK), jnp.bfloat16),
         ],
-        compiler_params=pltpu.CompilerParams(vmem_limit_bytes=16 * 2**20),
+        compiler_params=pltpu.CompilerParams(vmem_limit_bytes=60 * 2**20),
         cost_estimate=pl.CostEstimate(flops=2**31, bytes_accessed=6 * 2**20, transcendentals=2**20),
         name="probs",
     )(lengths, queries, keys)
@@ -169,8 +169,26 @@
     )(facts, mine, theirs, *given)
 
 
+def store_pieces(out_ref, latent_grad_t, hidden, up_term, facts, core):
+    lane = lax.broadcasted_iota(jnp.int32, (RANK // 2, HEAD_DIM), 1) < RANK
+    for x in range(4):
+        term = nn(latent_grad_t, hidden[:, x * 512 : (x + 1) * 512])
+        for i in range(4):
+            a = term[: RANK // 2, i * 128 : (i + 1) * 128]
+            b = term[RANK // 2 :, i * 128 : (i + 1) * 128]
+            out_ref[8 * i + x, :32, :] = jnp.where(lane, a, pltpu.roll(b, RANK, 1))
+            out_ref[8 * i + 4 + x, :32, :] = jnp.where(lane, pltpu.roll(a, RANK, 1), b)
+    sub = lax.broadcasted_iota(jnp.int32, (8, HEAD_DIM), 0)
+    for q in range(8):
+        for b in range(4):
+            tile = up_term[8 * q : 8 * q + 8, b * 128 : (b + 1) * 128]
+            rows = jnp.where(core == 0, tile, pltpu.roll(tile, 4, 0))
+            out_ref[4 * q + b, 32:, :] = jnp.where(sub < 4, rows, facts)
+
+
 def grads_kernel(
-    facts_ref, hidden, before, swapped, probs, probs_t, target, up_ref, out_ref, cot, value_grad,
+    facts_ref, hidden, before, swapped, probs, probs_t, target, up_ref,
+    out_ref, latent_grad_ref, up_term_ref, sums_ref, cot, value_grad,
 ):
     length = facts_ref[0]
     up = up_ref[...].astype(jnp.bfloat16)
@@ -194,37 +212,34 @@
     latent_grad_t = nt(up, grad).astype(jnp.bfloat16)
     up_term = lax.dot_general(latent, grad, (((0,), (0,)), ((), ())), preferred_element_type=jnp.float32)
 
-    lane = lax.broadcasted_iota(jnp.int32, (RANK // 2, HEAD_DIM), 1) < RANK
-    for m in range(MODEL // 512):
-        term = nn(latent_grad_t, hidden[:, m * 512 : (m + 1) * 512])
-        for i in range(4):
-            a = term[: RANK // 2, i * 128 : (i + 1) * 128]
-            b = term[RANK // 2 :, i * 128 : (i + 1) * 128]
-            even = jnp.where(lane, a, pltpu.roll(b, RANK, 1))
-            odd = jnp.where(lane, pltpu.roll(a, RANK, 1), b)
-            out_ref[m * 8 + 2 * i, :32, :] = even.astype(jnp.bfloat16)
-            out_ref[m * 8 + 2 * i + 1, :32, :] = odd.astype(jnp.bfloat16)
-
     loss = jnp.sum(jnp.sum(squares, axis=0, keepdims=True), axis=1, keepdims=True)
-    high = loss.astype(jnp.bfloat16).astype(jnp.float32)
-    sub8 = lax.broadcasted_iota(jnp.int32, (8, HEAD_DIM), 0)
-    lane8 = lax.broadcasted_iota(jnp.int32, (8, HEAD_DIM), 1)
+    lane = lax.broadcasted_iota(jnp.int32, (8, HEAD_DIM), 1)
+    row = lax.broadcasted_iota(jnp.int32, (8, HEAD_DIM), 0)
     count = jnp.full((8, HEAD_DIM), length, jnp.int32).astype(jnp.float32)
-    facts = jnp.where(lane8 == 0, high, jnp.where(lane8 == 1, loss - high, jnp.where(lane8 == 2, count, 0.0)))
-    for q in range(8):
-        for b in range(4):
-            tile = up_term[8 * q : 8 * q + 8, b * 128 : (b + 1) * 128]
-            out_ref[8 * q + b, 32:, :] = jnp.where(sub8 < 4, tile, facts).astype(jnp.bfloat16)
-            out_ref[8 * q + 4 + b, 32:, :] = jnp.where(sub8 < 4, pltpu.roll(tile, 4, 0), facts).astype(jnp.bfloat16)
-
-
-def gradient_pieces(facts, hidden, before, swapped, probs, probs_t, target, up_map):
+    sums = jnp.where(lane == 0, loss, jnp.where(lane == 1, count, 0.0))
+    sums = jnp.where(row == 4, sums, 0.0)
+    latent_grad_ref[...] = latent_grad_t
+    up_term_ref[...] = up_term
+    sums_ref[...] = sums
+    store_pieces(out_ref, latent_grad_t, hidden, up_term, sums, 1 - facts_ref[1])
+
+
+PIECES = jax.ShapeDtypeStruct((MODEL // RANK // 2, PIECE_ROWS, HEAD_DIM), jnp.float32)
+
+
+def gradients(facts, hidden, before, swapped, probs, probs_t, target, up_map):
     vmem = pl.BlockSpec(memory_space=pltpu.VMEM)
+    shape = jax.ShapeDtypeStruct
     return pl.pallas_call(
         grads_kernel,
         in_specs=[pl.BlockSpec(memory_space=pltpu.SMEM)] + [vmem] * 7,
-        out_specs=vmem,
-        out_shape=jax.ShapeDtypeStruct((MODEL // RANK, PIECE_ROWS, HEAD_DIM), jnp.bfloat16),
+        out_specs=[vmem] * 4,
+        out_shape=[
+            PIECES,
+            shape((RANK, TOK), jnp.bfloat16),
+            shape((RANK, KV_WIDTH), jnp.float32),
+            shape((8, HEAD_DIM), jnp.float32),
+        ],
         scratch_shapes=[
             pltpu.VMEM((GROUP * TOK, HEAD_DIM), jnp.bfloat16),
             pltpu.VMEM((TOK, KV_WIDTH), jnp.bfloat16),
@@ -235,31 +250,77 @@
     )(facts, hidden, before, swapped, probs, probs_t, target, up_map)
 
 
+def keep_kernel(facts_ref, hidden, latent_grad_ref, up_term_ref, sums_ref, out_ref):
+    store_pieces(out_ref, latent_grad_ref[...], hidden, up_term_ref[...], sums_ref[...], facts_ref[1])
+
+
+def kept_pieces(facts, hidden, latent_grad_t, up_term, sums):
+    vmem = pl.BlockSpec(memory_space=pltpu.VMEM)
+    return pl.pallas_call(
+        keep_kernel,
+        in_specs=[pl.BlockSpec(memory_space=pltpu.SMEM)] + [vmem] * 4,
+        out_specs=vmem,
+        out_shape=PIECES,
+        compiler_params=pltpu.CompilerParams(vmem_limit_bytes=8 * 2**20),
+        cost_estimate=pl.CostEstimate(flops=2**28, bytes_accessed=2**21, transcendentals=0),
+        name="keep",
+    )(facts, hidden, latent_grad_t, up_term, sums)
+
+
+def halved(wide):
+    high = wide.astype(jnp.bfloat16)
+    return high, (wide - high.astype(jnp.float32)).astype(jnp.bfloat16)
+
+
+def merge_kernel(kept, came, out_ref):
+    row = lax.broadcasted_iota(jnp.int32, (8, HEAD_DIM), 0)
+    for r in range(out_ref.shape[0]):
+        out_ref[r, :32, :] = (kept[r, :32, :] + came[r, :32, :]).astype(jnp.bfloat16)
+        rows = kept[r, 32:, :] + came[r, 32:, :]
+        rest = rows - rows.astype(jnp.bfloat16).astype(jnp.float32)
+        out_ref[r, 32:, :] = jnp.where(row == 5, pltpu.roll(rest, 1, 0), rows).astype(jnp.bfloat16)
+
+
+def merged(kept, came):
+    return pl.pallas_call(
+        merge_kernel,
+        out_shape=jax.ShapeDtypeStruct(PIECES.shape, jnp.bfloat16),
+        compiler_params=SMALL,
+        name="merge",
+    )(kept, came)
+
+
 def fold_kernel(pieces_ref, out_ref):
     total = jnp.sum(pieces_ref[...].astype(jnp.float32), axis=0)
+    row = lax.broadcasted_iota(jnp.int32, (8, HEAD_DIM), 0)
+    tail = total[32:, :]
+    tail = jnp.where(row == 4, tail + pltpu.roll(tail, 7, 0), tail)
+    high, low = halved(tail)
+    rows = jnp.concatenate([total[:32, :].astype(jnp.bfloat16), jnp.concatenate([high, low], axis=0)], axis=0)
     for d in range(out_ref.shape[0]):
-        out_ref[d] = total
+        out_ref[d] = rows
 
 
 def fold(pieces, copies):
     return pl.pallas_call(
         fold_kernel,
-        out_shape=jax.ShapeDtypeStruct((copies, PIECE_ROWS, HEAD_DIM), jnp.float32),
+        out_shape=jax.ShapeDtypeStruct((copies, PIECE_ROWS + 8, HEAD_DIM), jnp.bfloat16),
         compiler_params=SMALL,
         name="fold",
     )(pieces)
 
 
 def owner_kernel(pieces_ref, down_ref, average_ref, grad_ref, next_ref, up_ref, loss_ref):
-    total = jnp.sum(pieces_ref[...], axis=0)
-    count = total[36:37, 2:3]
-    loss_ref[...] = (total[36:37, 0:1] + total[36:37, 1:2]) / (2.0 * count)
+    total = jnp.sum(pieces_ref[...].astype(jnp.float32), axis=0)
+    tail = total[32:40, :] + total[40:48, :]
+    count = tail[4:5, 1:2]
+    loss_ref[...] = tail[4:5, 0:1] / (2.0 * count)
     factor = adapter_scale / count
     rows = jnp.concatenate([total[:32, :RANK], total[:32, RANK:]], axis=0)
     grad = jnp.transpose(rows) * factor
     grad_ref[...] = grad
     next_ref[...] = average_decay * average_ref[...] + (1.0 - average_decay) * (down_ref[...] - learning_rate * grad)
-    piece = total[32:36, :] * factor
+    piece = tail[:4, :] * factor
     for d in range(up_ref.shape[0]):
         up_ref[d] = piece
 
@@ -281,8 +342,9 @@
 
 def second_kernel(pieces_ref, up_ref, average_ref, grad_ref, next_ref):
     for j in range(MODEL // RANK):
-        q, b = divmod(j, 4)
-        grad_ref[4 * q : 4 * q + 4, b * 128 : (b + 1) * 128] = pieces_ref[j]
+        q, b = divmod(j // 2, 4)
+        top = 8 * q + 4 * (j % 2)
+        grad_ref[top : top + 4, b * 128 : (b + 1) * 128] = pieces_ref[j]
     next_ref[...] = average_decay * average_ref[...] + (1.0 - average_decay) * (
         up_ref[...] - learning_rate * grad_ref[...]
     )
@@ -301,6 +363,10 @@
 
 def along_y(owners):
     return [list(range(k, owners, 8)) for k in range(8)]
+
+
+def same_core(owners):
+    return [list(range(core, owners, 2)) for core in range(2)]
 
 
 def along_x(block, owners, shift):
@@ -354,8 +420,15 @@
         total = partial_values(facts, mine, theirs, given, shift, total)
     total, other = partial_values(facts, mine, theirs, (near,), 1, total, last=True)
     swapped = from_other_core(other, owners)
-    pieces = gradient_pieces(facts, hidden, total, swapped, probs, probs_t, target, adapter_up_map)
-    summed = fold(exchange(pieces, "fsdp"), replicas)
+    pieces, latent_grad_t, up_term, sums = gradients(
+        facts, send, total, swapped, probs, probs_t, target, adapter_up_map
+    )
+    came = from_other_core(pieces, owners)
+    kept = kept_pieces(facts, mine, latent_grad_t, up_term, sums)
+    arrived = lax.all_to_all(
+        merged(kept, came), "fsdp", 0, 0, tiled=True, axis_index_groups=same_core(owners)
+    )
+    summed = fold(arrived, replicas)
     down_grad, average_down_next, up_piece, loss = owner_update(
         exchange(summed, "dp"), adapter_down_map, average_down_map, owners
     )

time: 158 us -> 155 us (0.981)
  blocking collectives: 61.9 us -> 49.1 us
  Pallas kernels: 16.4 us -> 20.9 us
  local copies, waits for them, and re-layouts: 3.26 us -> 6.41 us
  starting transfers between devices: 56.7 us -> 58.5 us
    all_to_all x3 -> x2, blocking collectives: 61.9 us -> 32.1 us  [exchange(): return lax.all_to_all(pieces, axis, 0, 0, tiled=True)]
    all_to_all x0 -> x1, blocking collectives: none -> 17 us  [per_device(): lax.all_to_all(merged(kept, came), 'fsdp', 0, 0, tiled=True, axis_index_g...]
    unnamed x22 -> x20, local copies, waits for them, and re-layouts: 3.24 us -> 6.39 us
    pallas_call x1, Pallas kernels: 2.98 us -> 5.1 us  [attention_probs(): pl.pallas_call(probs_kernel, grid=(KEY_VALUE_HEADS,), in_specs=[pl.BlockS...]
    ppermute x2 -> x3, starting transfers between devices: 13.6 us -> 15.4 us  [from_other_core(): return lax.ppermute(block, 'fsdp', [(i, i ^ 1) for i in range(owners)])]
    pallas_call x1 -> x3, Pallas kernels: 3.09 us -> 4.67 us  [the longest x1 3.61 us: gradients(): pl.pallas_call(grads_kernel, in_specs=[pl.BlockSpec(memory_space=pltpu.SM...]
  transfers between devices with their start and end apart: 9 -> 10, of which waited for: 2 -> 3; matrix products, arithmetic and copies ran while one was open for 0% -> 0% of each run, Pallas kernels for 6% -> 8%
where the time goes in v5:
time: 155 us
  starting transfers between devices  58.5 us (38%)
  blocking collectives  49.1 us (32%)
  Pallas kernels  20.9 us (13%)
  waiting for transfers between devices  18 us (12%)
  local copies, waits for them, and re-layouts  6.41 us (4%)
    all_to_all x2, blocking collectives, exchange(): return lax.all_to_all(pieces, axis, 0, 0, tiled=True)  32.1 us
    ppermute x3, starting transfers between devices, from_neighbour(): return lax.ppermute(part, ('dp', 'fsdp'), moved)  18.1 us
    ppermute x3, starting transfers between devices, along_x(): return lax.ppermute(block, 'fsdp', moved)  17.4 us
    all_to_all x1, blocking collectives, per_device(): lax.all_to_all(merged(kept, came), 'fsdp', 0, 0, tiled=True, axis_index_g...  17 us
    ppermute x3, waiting for transfers between devices, along_x(): return lax.ppermute(block, 'fsdp', moved)  15.6 us
    ppermute x3, starting transfers between devices, from_other_core(): return lax.ppermute(block, 'fsdp', [(i, i ^ 1) for i in range(owners)])  15.4 us
    all_to_all x1, starting transfers between devices, per_device(): lax.all_to_all(shards, 'fsdp', 0, 0, tiled=True, axis_index_groups=along_...  7.64 us
    unnamed x20, local copies, waits for them, and re-layouts  6.39 us
  transfers between devices with their start and end apart: 10, of which 3 were waited for; matrix products, arithmetic and copies ran while one was open for 0% of the time, Pallas kernels for 8%

profile of v5, /device:TPU:1, one launch (start us, length us, event | category | flops | bytes accessed | tf_op | source)
XLA Modules:
  0.0 154.5 jit_solution(15168500041521396353)
XLA Ops:
  3.1 7.6 %all-to-all-start = ((bf16[8,64,576]{2,1,0:T(8,128)(2,1)}), bf16[8,64,576]{2,1,0:T(8,128)(2,1)S(1)}, u32[]{:S(2)}, u32[]{:S(2)}) async-start(bf16[8,64,576]{2,1,0:T(8,128)(2,1)} %pack.1), calls=%async_computation | async-start | bytes 1310720 | tf_op jit(solution)/shard_map/all_to_all | solution.py:408
  11.5 1.6 %copy-done.6 = bf16[256,4096]{1,0:T(8,128)(2,1)S(1)} copy-done((bf16[256,4096]{1,0:T(8,128)(2,1)S(1)}, bf16[256,4096]{1,0:T(8,128)(2,1)}, u32[]{:S(2)}) %copy-start.6) | copy-done | bytes 2097176
  13.1 2.7 %split.1 = (bf16[256,2048]{1,0:T(8,128)(2,1)S(1)}, bf16[256,2048]{1,0:T(8,128)(2,1)}) custom-call(s32[4]{0:T(128)S(1)} %pad_add_fusion.facts_ref, bf16[256,4096]{1,0:T(8,128)(2,1)S(1)} %copy-done.6), custom_call_target="tpu_custom_call" | custom-call | flops 1073741824 | bytes 4194304 | tf_op jit(solution)/shard_map/split/pallas_call | solution.py:112
  15.8 8.3 %collective-permute-start = (bf16[256,2048]{1,0:T(8,128)(2,1)}, bf16[256,2048]{1,0:T(8,128)(2,1)S(1)}, u32[]{:S(2)}, u32[]{:S(2)}) collective-permute-start(bf16[256,2048]{1,0:T(8,128)(2,1)} %get-tuple-element.22.hidden), channel_id=1, source_target_pairs={{0,1},{1,0},{2,3},{3,2},{4,5},{5,4},{6,7},{7,6},{8,9},{9,8},{10,11... | collective-permute-start | bytes 3145736 | tf_op jit(solution)/shard_map/ppermute | solution.py:387
  24.1 11.8 %collective-permute-start.6 = (bf16[8,64,576]{2,1,0:T(8,128)(2,1)S(1)}, bf16[8,64,576]{2,1,0:T(8,128)(2,1)}, u32[]{:S(2)}, u32[]{:S(2)}) collective-permute-start(bf16[8,64,576]{2,1,0:T(8,128)(2,1)S(1)} %all-to-all-done.block), channel_id=1, source_target_pairs={{0,6},{1,7},{2,0},{3,1},{4,2},{5,3},{6,4},{7,5},{8,14},{9,15},{10,... | collective-permute-start | bytes 1769480 | tf_op jit(solution)/shard_map/ppermute | solution.py:374
  35.9 1.9 %collective-permute-start.1 = (bf16[8,64,576]{2,1,0:T(8,128)(2,1)S(1)}, bf16[8,64,576]{2,1,0:T(8,128)(2,1)S(1)}, u32[]{:S(2)}, u32[]{:S(2)}) collective-permute-start(bf16[8,64,576]{2,1,0:T(8,128)(2,1)S(1)} %all-to-all-done.block), channel_id=1, source_target_pairs={{0,2},{1,3},{2,4},{3,5},{4,6},{5,7},{6,0},{7,1},{8,10},{9,11},{10,... | collective-permute-start | bytes 1769480 | tf_op jit(solution)/shard_map/ppermute | solution.py:374
  37.9 3.6 %collective-permute-start.2 = (bf16[2,64,576]{2,1,0:T(8,128)(2,1)S(1)}, bf16[2,64,576]{2,1,0:T(8,128)(2,1)S(1)}, u32[]{:S(2)}, u32[]{:S(2)}) collective-permute-start(bf16[2,64,576]{2,1,0:T(8,128)(2,1)S(1)} %constant_dynamic-slice_fusion), channel_id=1, source_target_pairs={{0,4},{1,5},{2,6},{3,7},{4,0},{5,1},{6,2},{7,3},{8,12},{9,13},{10,... | collective-permute-start | bytes 442376 | tf_op jit(solution)/shard_map/ppermute | solution.py:374
  41.5 15.6 %collective-permute-done.2.rest_0_ = bf16[2,64,576]{2,1,0:T(8,128)(2,1)S(1)} collective-permute-done((bf16[2,64,576]{2,1,0:T(8,128)(2,1)S(1)}, bf16[2,64,576]{2,1,0:T(8,128)(2,1)S(1)}, u32[]{:S(2)}, u32[]{:S(2)}) %collective-permute-start.2) | collective-permute-done | bytes 147488 | tf_op jit(solution)/shard_map/ppermute | solution.py:374
  57.2 2.8 %collective-permute-start.5 = (bf16[2,64,576]{2,1,0:T(8,128)(2,1)S(1)}, bf16[2,64,576]{2,1,0:T(8,128)(2,1)S(1)}, u32[]{:S(2)}, u32[]{:S(2)}) collective-permute-start(bf16[2,64,576]{2,1,0:T(8,128)(2,1)S(1)} %collective-permute-done.2.rest_0_), channel_id=1, source_target_pairs={{72,0},{73,1},{74,2},{75,3},{76,4},{77,5},{78,6},{79,7},{80,8},{81... | collective-permute-start | bytes 442376 | tf_op jit(solution)/shard_map/ppermute | solution.py:383
  60.0 13.4 %collective-permute-start.4 = (bf16[2,64,576]{2,1,0:T(8,128)(2,1)S(1)}, bf16[2,64,576]{2,1,0:T(8,128)(2,1)S(1)}, u32[]{:S(2)}, u32[]{:S(2)}) collective-permute-start(bf16[2,64,576]{2,1,0:T(8,128)(2,1)S(1)} %collective-permute-done.2.rest_0_), channel_id=1, source_target_pairs={{64,0},{65,1},{66,2},{67,3},{68,4},{69,5},{70,6},{71,7},{72,8},{73... | collective-permute-start | bytes 442376 | tf_op jit(solution)/shard_map/ppermute | solution.py:383
  73.4 1.9 %collective-permute-start.3 = (bf16[2,64,576]{2,1,0:T(8,128)(2,1)S(1)}, bf16[2,64,576]{2,1,0:T(8,128)(2,1)S(1)}, u32[]{:S(2)}, u32[]{:S(2)}) collective-permute-start(bf16[2,64,576]{2,1,0:T(8,128)(2,1)S(1)} %collective-permute-done.2.rest_0_), channel_id=1, source_target_pairs={{8,0},{9,1},{10,2},{11,3},{12,4},{13,5},{14,6},{15,7},{16,8},{17,9... | collective-permute-start | bytes 442376 | tf_op jit(solution)/shard_map/ppermute | solution.py:383
  76.5 1.7 %partial.5.rest_4_ = f32[2,256,576]{2,1,0:T(8,128)S(1)} custom-call(s32[4]{0:T(128)S(1)} %pad_add_fusion.facts_ref, bf16[256,2048]{1,0:T(8,128)(2,1)S(1)} %get-tuple-element.21.mine.hidden, bf16[256,2048]{1,0:T(8,128)(2,1)S(1)} %collective-permute-done.theirs, bf16[8,64,576]{2,1,0:T(8,128)(2,1)} %collective-permute-done.6.rest_0_, ...), custom_call_target="tpu_custom_call" | custom-call | flops 536870912 | bytes 2097152 | tf_op jit(solution)/shard_map/partial/pallas_call | solution.py:161
  78.2 1.3 collective-permute-done.3.rest_1_
  79.5 1.1 partial.6.before
  80.6 2.0 %partial.7 = (f32[256,640]{1,0:T(8,128)S(1)}, f32[256,640]{1,0:T(8,128)}) custom-call(s32[4]{0:T(128)S(1)} %pad_add_fusion.facts_ref, bf16[256,2048]{1,0:T(8,128)(2,1)S(1)} %get-tuple-element.21.mine.hidden, bf16[256,2048]{1,0:T(8,128)(2,1)S(1)} %collective-permute-done.theirs, bf16[8,64,576]{2,1,0:T(8,128)(2,1)S(1)} %collective-permute-done.1.block, ...), custom_call_target="tpu_custom_call" | custom-call | flops 536870912 | bytes 2097152 | tf_op jit(solution)/shard_map/partial/pallas_call | solution.py:161
  82.6 5.1 %collective-permute-start.7 = (f32[256,640]{1,0:T(8,128)}, f32[256,640]{1,0:T(8,128)S(1)}, u32[]{:S(2)}, u32[]{:S(2)}) collective-permute-start(f32[256,640]{1,0:T(8,128)} %get-tuple-element.24), channel_id=1, source_target_pairs={{0,1},{1,0},{2,3},{3,2},{4,5},{5,4},{6,7},{7,6},{8,9},{9,8},{10,11... | collective-permute-start | bytes 1966088 | tf_op jit(solution)/shard_map/ppermute | solution.py:387
  87.8 5.1 %probs.1 = (bf16[4,1024,256]{2,1,0:T(8,128)(2,1)}, bf16[4,256,1024]{2,1,0:T(8,128)(2,1)}) custom-call(s32[1]{0:T(128)S(6)} %copy.15.length_ref, bf16[256,2048]{1,0:T(8,128)(2,1)} %q_ref.1, bf16[256,512]{1,0:T(8,128)(2,1)} %k_ref.1), custom_call_target="tpu_custom_call" | custom-call | flops 2147483648 | bytes 6291456 | tf_op jit(solution)/shard_map/probs/pallas_call | solution.py:57
  92.9 1.6 %copy-done.8 = bf16[4,1024,256]{2,1,0:T(8,128)(2,1)S(1)} copy-done((bf16[4,1024,256]{2,1,0:T(8,128)(2,1)S(1)}, bf16[4,1024,256]{2,1,0:T(8,128)(2,1)}, u32[]{:S(2)}) %copy-start.8) | copy-done | bytes 2097176
  94.5 1.6 %copy-done.9 = bf16[4,256,1024]{2,1,0:T(8,128)(2,1)S(1)} copy-done((bf16[4,256,1024]{2,1,0:T(8,128)(2,1)S(1)}, bf16[4,256,1024]{2,1,0:T(8,128)(2,1)}, u32[]{:S(2)}) %copy-start.9) | copy-done | bytes 2097176
  96.1 3.6 %grads.1 = (f32[32,40,128]{2,1,0:T(8,128)S(1)}, bf16[64,256]{1,0:T(8,128)(2,1)S(1)}, f32[64,512]{1,0:T(8,128)S(1)}, f32[8,128]{1,0:T(8,128)S(1)}) custom-call(s32[4]{0:T(128)S(1)} %pad_add_fusion.facts_ref, bf16[256,2048]{1,0:T(8,128)(2,1)} %get-tuple-element.22.hidden, f32[256,640]{1,0:T(8,128)S(1)} %get-tuple-element.23.before, ...), custom_call_target="tpu_custom_call" | custom-call | flops 4294967296 | bytes 10485760 | tf_op jit(solution)/shard_map/grads/pallas_call | solution.py:233
  99.7 1.9 %collective-permute-start.8 = (f32[32,40,128]{2,1,0:T(8,128)S(1)}, f32[32,40,128]{2,1,0:T(8,128)S(1)}, u32[]{:S(2)}, u32[]{:S(2)}) collective-permute-start(f32[32,40,128]{2,1,0:T(8,128)S(1)} %get-tuple-element.30), channel_id=1, source_target_pairs={{0,1},{1,0},{2,3},{3,2},{4,5},{5,4},{6,7},{7,6},{8,9},{9,8},{10,11... | collective-permute-start | bytes 1966088 | tf_op jit(solution)/shard_map/ppermute | solution.py:387
  103.8 17.0 %all_to_all.20.pieces_ref = bf16[32,40,128]{2,1,0:T(8,128)(2,1)S(1)} all-to-all(bf16[32,40,128]{2,1,0:T(8,128)(2,1)S(1)} %merge.1), channel_id=1, replica_groups={{0,2,4,6,8,10,12,14,16,18,20,22,24,26,28,30,32,34,36,38,40,42,44,46,48,..., dimensions={0} | all-to-all | bytes 655360 | tf_op jit(solution)/shard_map/all_to_all | solution.py:428
  120.9 13.0 %all_to_all.21.pieces_ref = bf16[12,48,128]{2,1,0:T(8,128)(2,1)S(1)} all-to-all(bf16[12,48,128]{2,1,0:T(8,128)(2,1)S(1)} %fold.1), channel_id=1, replica_groups=mesh['dp'=12,'fsdp'=64] {'dp'}, dimensions={0} | all-to-all | bytes 294912 | tf_op jit(solution)/shard_map/all_to_all | solution.py:361
  134.7 19.0 %all_to_all.22.pieces_ref = f32[64,4,128]{2,1,0:T(4,128)S(1)} all-to-all(f32[64,4,128]{2,1,0:T(4,128)S(1)} %get-tuple-element.32), channel_id=1, replica_groups=mesh['dp'=12,'fsdp'=64] {'fsdp'}, dimensions={0} | all-to-all | bytes 262144 | tf_op jit(solution)/shard_map/all_to_all | solution.py:361
  (34 shorter events, 7.5 us)
Async XLA Ops:
  0.6 0.8 copy-start.2
  1.4 0.8 copy-start.4
  3.1 21.0 %all-to-all-start = ((bf16[8,64,576]{2,1,0:T(8,128)(2,1)}), bf16[8,64,576]{2,1,0:T(8,128)(2,1)S(1)}, u32[]{:S(2)}, u32[]{:S(2)}) async-start(bf16[8,64,576]{2,1,0:T(8,128)(2,1)} %pack.1), calls=%async_computation | async-start | bytes 1310720 | tf_op jit(solution)/shard_map/all_to_all | solution.py:408
  11.5 1.6 %copy-start.6 = (bf16[256,4096]{1,0:T(8,128)(2,1)S(1)}, bf16[256,4096]{1,0:T(8,128)(2,1)}, u32[]{:S(2)}) copy-start(bf16[256,4096]{1,0:T(8,128)(2,1)} %hidden.1) | copy-start | bytes 6291460
  15.8 57.6 %collective-permute-start = (bf16[256,2048]{1,0:T(8,128)(2,1)}, bf16[256,2048]{1,0:T(8,128)(2,1)S(1)}, u32[]{:S(2)}, u32[]{:S(2)}) collective-permute-start(bf16[256,2048]{1,0:T(8,128)(2,1)} %get-tuple-element.22.hidden), channel_id=1, source_target_pairs={{0,1},{1,0},{2,3},{3,2},{4,5},{5,4},{6,7},{7,6},{8,9},{9,8},{10,11... | collective-permute-start | bytes 3145736 | tf_op jit(solution)/shard_map/ppermute | solution.py:387
  24.1 52.3 %collective-permute-start.6 = (bf16[8,64,576]{2,1,0:T(8,128)(2,1)S(1)}, bf16[8,64,576]{2,1,0:T(8,128)(2,1)}, u32[]{:S(2)}, u32[]{:S(2)}) collective-permute-start(bf16[8,64,576]{2,1,0:T(8,128)(2,1)S(1)} %all-to-all-done.block), channel_id=1, source_target_pairs={{0,6},{1,7},{2,0},{3,1},{4,2},{5,3},{6,4},{7,5},{8,14},{9,15},{10,... | collective-permute-start | bytes 1769480 | tf_op jit(solution)/shard_map/ppermute | solution.py:374
  35.9 44.7 %collective-permute-start.1 = (bf16[8,64,576]{2,1,0:T(8,128)(2,1)S(1)}, bf16[8,64,576]{2,1,0:T(8,128)(2,1)S(1)}, u32[]{:S(2)}, u32[]{:S(2)}) collective-permute-start(bf16[8,64,576]{2,1,0:T(8,128)(2,1)S(1)} %all-to-all-done.block), channel_id=1, source_target_pairs={{0,2},{1,3},{2,4},{3,5},{4,6},{5,7},{6,0},{7,1},{8,10},{9,11},{10,... | collective-permute-start | bytes 1769480 | tf_op jit(solution)/shard_map/ppermute | solution.py:374
  37.9 19.3 %collective-permute-start.2 = (bf16[2,64,576]{2,1,0:T(8,128)(2,1)S(1)}, bf16[2,64,576]{2,1,0:T(8,128)(2,1)S(1)}, u32[]{:S(2)}, u32[]{:S(2)}) collective-permute-start(bf16[2,64,576]{2,1,0:T(8,128)(2,1)S(1)} %constant_dynamic-slice_fusion), channel_id=1, source_target_pairs={{0,4},{1,5},{2,6},{3,7},{4,0},{5,1},{6,2},{7,3},{8,12},{9,13},{10,... | collective-permute-start | bytes 442376 | tf_op jit(solution)/shard_map/ppermute | solution.py:374
  57.2 21.0 %collective-permute-start.5 = (bf16[2,64,576]{2,1,0:T(8,128)(2,1)S(1)}, bf16[2,64,576]{2,1,0:T(8,128)(2,1)S(1)}, u32[]{:S(2)}, u32[]{:S(2)}) collective-permute-start(bf16[2,64,576]{2,1,0:T(8,128)(2,1)S(1)} %collective-permute-done.2.rest_0_), channel_id=1, source_target_pairs={{72,0},{73,1},{74,2},{75,3},{76,4},{77,5},{78,6},{79,7},{80,8},{81... | collective-permute-start | bytes 442376 | tf_op jit(solution)/shard_map/ppermute | solution.py:383
  60.0 18.2 %collective-permute-start.4 = (bf16[2,64,576]{2,1,0:T(8,128)(2,1)S(1)}, bf16[2,64,576]{2,1,0:T(8,128)(2,1)S(1)}, u32[]{:S(2)}, u32[]{:S(2)}) collective-permute-start(bf16[2,64,576]{2,1,0:T(8,128)(2,1)S(1)} %collective-permute-done.2.rest_0_), channel_id=1, source_target_pairs={{64,0},{65,1},{66,2},{67,3},{68,4},{69,5},{70,6},{71,7},{72,8},{73... | collective-permute-start | bytes 442376 | tf_op jit(solution)/shard_map/ppermute | solution.py:383
  73.4 6.1 %collective-permute-start.3 = (bf16[2,64,576]{2,1,0:T(8,128)(2,1)S(1)}, bf16[2,64,576]{2,1,0:T(8,128)(2,1)S(1)}, u32[]{:S(2)}, u32[]{:S(2)}) collective-permute-start(bf16[2,64,576]{2,1,0:T(8,128)(2,1)S(1)} %collective-permute-done.2.rest_0_), channel_id=1, source_target_pairs={{8,0},{9,1},{10,2},{11,3},{12,4},{13,5},{14,6},{15,7},{16,8},{17,9... | collective-permute-start | bytes 442376 | tf_op jit(solution)/shard_map/ppermute | solution.py:383
  82.6 10.3 %copy-start = (f32[64,512]{1,0:T(8,128)S(1)}, f32[64,512]{1,0:T(8,128)}, u32[]{:S(2)}) copy-start(f32[64,512]{1,0:T(8,128)} %up_ref.3) | copy-start | bytes 393220
  82.6 10.3 %copy-start.7 = (bf16[256,2048]{1,0:T(8,128)(2,1)S(1)}, bf16[256,2048]{1,0:T(8,128)(2,1)}, u32[]{:S(2)}) copy-start(bf16[256,2048]{1,0:T(8,128)(2,1)} %target.1) | copy-start | bytes 3145732
  82.6 10.2 %collective-permute-start.7 = (f32[256,640]{1,0:T(8,128)}, f32[256,640]{1,0:T(8,128)S(1)}, u32[]{:S(2)}, u32[]{:S(2)}) collective-permute-start(f32[256,640]{1,0:T(8,128)} %get-tuple-element.24), channel_id=1, source_target_pairs={{0,1},{1,0},{2,3},{3,2},{4,5},{5,4},{6,7},{7,6},{8,9},{9,8},{10,11... | collective-permute-start | bytes 1966088 | tf_op jit(solution)/shard_map/ppermute | solution.py:387
  92.9 1.6 %copy-start.8 = (bf16[4,1024,256]{2,1,0:T(8,128)(2,1)S(1)}, bf16[4,1024,256]{2,1,0:T(8,128)(2,1)}, u32[]{:S(2)}) copy-start(bf16[4,1024,256]{2,1,0:T(8,128)(2,1)} %get-tuple-element.25.probs) | copy-start | bytes 6291460
  94.5 1.6 %copy-start.9 = (bf16[4,256,1024]{2,1,0:T(8,128)(2,1)S(1)}, bf16[4,256,1024]{2,1,0:T(8,128)(2,1)}, u32[]{:S(2)}) copy-start(bf16[4,256,1024]{2,1,0:T(8,128)(2,1)} %get-tuple-element.26.probs_t) | copy-start | bytes 6291460
  99.7 4.0 %collective-permute-start.8 = (f32[32,40,128]{2,1,0:T(8,128)S(1)}, f32[32,40,128]{2,1,0:T(8,128)S(1)}, u32[]{:S(2)}, u32[]{:S(2)}) collective-permute-start(f32[32,40,128]{2,1,0:T(8,128)S(1)} %get-tuple-element.30), channel_id=1, source_target_pairs={{0,1},{1,0},{2,3},{3,2},{4,5},{5,4},{6,7},{7,6},{8,9},{9,8},{10,11... | collective-permute-start | bytes 1966088 | tf_op jit(solution)/shard_map/ppermute | solution.py:387
  101.6 32.3 %copy-start.3 = (f32[64,64]{1,0:T(8,128)S(1)}, f32[64,64]{1,0:T(8,128)}, u32[]{:S(2)}) copy-start(f32[64,64]{1,0:T(8,128)} %down_ref.3) | copy-start | bytes 49156
  101.6 32.3 %copy-start.5 = (f32[64,64]{1,0:T(8,128)S(1)}, f32[64,64]{1,0:T(8,128)}, u32[]{:S(2)}) copy-start(f32[64,64]{1,0:T(8,128)} %average_ref.2) | copy-start | bytes 49156
  102.6 51.2 %copy-start.1 = (f32[64,512]{1,0:T(8,128)S(1)}, f32[64,512]{1,0:T(8,128)}, u32[]{:S(2)}) copy-start(f32[64,512]{1,0:T(8,128)} %average_ref.3) | copy-start | bytes 393220

commit v6 on v5

--- a/solution.py
+++ b/solution.py
@@ -1,4 +1,3 @@
-import functools
 import math
 
 import jax
@@ -87,14 +86,19 @@
     return pl.pallas_call(
         pack_kernel,
         out_shape=jax.ShapeDtypeStruct((copies, RANK, WIDTH), jnp.bfloat16),
-        compiler_params=SMALL,
+        compiler_params=pltpu.CompilerParams(vmem_limit_bytes=67_000_000),
         name="pack",
     )(value_rows, down_rows)
 
 
-def split_kernel(facts_ref, hidden, keep, send):
+def places():
+    place, plane = lax.axis_index("fsdp"), lax.axis_index("dp")
+    return place & 1, (place >> 1) & 3, (plane & 1) * 2 + ((place >> 3) & 1)
+
+
+def split_kernel(hidden, keep, send):
     first = lax.broadcasted_iota(jnp.int32, (TOK, HEAD_DIM), 1) < RANK
-    mine = facts_ref[1] == 0
+    mine = places()[0] == 0
     for x in range(4):
         for y in range(0, 8, 2):
             a = hidden[:, y * 512 + x * 128 : y * 512 + (x + 1) * 128].astype(jnp.float32)
@@ -106,67 +110,67 @@
             send[:, to] = jnp.where(mine, odd, even).astype(jnp.bfloat16)
 
 
-def split_hidden(facts, hidden):
+def split_hidden(hidden):
     vmem = pl.BlockSpec(memory_space=pltpu.VMEM)
     shape = jax.ShapeDtypeStruct((TOK, MODEL // 2), jnp.bfloat16)
     return pl.pallas_call(
         split_kernel,
-        in_specs=[pl.BlockSpec(memory_space=pltpu.SMEM), vmem],
+        in_specs=[vmem],
         out_specs=[vmem, vmem],
         out_shape=[shape, shape],
         compiler_params=pltpu.CompilerParams(vmem_limit_bytes=12 * 2**20),
         cost_estimate=pl.CostEstimate(flops=2**30, bytes_accessed=2**22, transcendentals=0),
         name="split",
-    )(facts, hidden)
-
-
-def partial_kernel(which, facts_ref, mine, theirs, *rest):
-    *blocks, before, out = rest
-    column = lax.rem(facts_ref[2] + (4 - which), 4) * 512
+    )(hidden)
+
+
+def block_product(tokens, block, which):
+    _, x, own_quarter = places()
+    column = ((x + (4 - which)) & 3) * 512
+    if len(block) == 1:
+        return nn(tokens[:, pl.ds(pl.multiple_of(column, 512), 512)], block[0][...].reshape(512, WIDTH))
+    total = None
+    for j in (0, 2):
+        left, right = [], []
+        for k in (j, j + 1):
+            quarter = own_quarter ^ k
+            left.append(tokens[:, pl.ds(pl.multiple_of(column + quarter * 128, 128), 128)])
+            right.append(block[k][...].reshape(128, WIDTH))
+        part = nn(jnp.concatenate(left, axis=1), jnp.concatenate(right, axis=0))
+        total = part if total is None else total + part
+    return total
+
+
+def first_kernel(mine, theirs, own, out):
     for i, tokens in enumerate((mine, theirs)):
-        if len(blocks) == 1:
-            part = nn(tokens[:, pl.ds(pl.multiple_of(column, 512), 512)], blocks[0][...].reshape(512, WIDTH))
-        else:
-            part = None
-            for j in (0, 2):
-                left, right = [], []
-                for k in (j, j + 1):
-                    quarter = facts_ref[3] ^ k
-                    left.append(tokens[:, pl.ds(pl.multiple_of(column + quarter * 128, 128), 128)])
-                    right.append(blocks[k][...].reshape(128, WIDTH))
-                more = nn(jnp.concatenate(left, axis=1), jnp.concatenate(right, axis=0))
-                part = more if part is None else part + more
-        out[i] = part if before is None else part + before[i]
-
-
-def first_partial_kernel(which, facts_ref, mine, theirs, block, out):
-    partial_kernel(which, facts_ref, mine, theirs, block, None, out)
-
-
-def last_partial_kernel(which, facts_ref, mine, theirs, block, before, own, other):
-    class Outs:
-        def __setitem__(self, i, value):
-            (own, other)[i][:, :WIDTH] = value
-
-    partial_kernel(which, facts_ref, mine, theirs, block, before, Outs())
-    for out in (own, other):
+        out[i] = block_product(tokens, (own,), 0)
+
+
+def next_kernel(mine, theirs, far, before, out):
+    for i, tokens in enumerate((mine, theirs)):
+        out[i] = block_product(tokens, (far,), 3) + before[i]
+
+
+def last_kernel(mine, theirs, q0, q1, q2, q3, near, before, own, other):
+    for i, (tokens, out) in enumerate(((mine, own), (theirs, other))):
+        far = block_product(tokens, (q0, q1, q2, q3), 2)
+        out[:, :WIDTH] = (before[i] + far) + block_product(tokens, (near,), 1)
         out[:, WIDTH:] = jnp.zeros((TOK, PADDED - WIDTH), jnp.float32)
 
 
-def partial_values(facts, mine, theirs, blocks, which, before=None, last=False):
+def partial_values(body, *given):
     vmem = pl.BlockSpec(memory_space=pltpu.VMEM)
-    given = tuple(blocks) + (() if before is None else (before,))
-    body = last_partial_kernel if last else first_partial_kernel if before is None else partial_kernel
-    shape = jax.ShapeDtypeStruct((TOK, PADDED), jnp.float32)
-    return pl.pallas_call(
-        functools.partial(body, which),
-        in_specs=[pl.BlockSpec(memory_space=pltpu.SMEM)] + [vmem] * (2 + len(given)),
+    shape = jax.ShapeDtypeStruct
+    last = body is last_kernel
+    return pl.pallas_call(
+        body,
+        in_specs=[vmem] * len(given),
         out_specs=[vmem, vmem] if last else vmem,
-        out_shape=[shape, shape] if last else jax.ShapeDtypeStruct((2, TOK, WIDTH), jnp.float32),
+        out_shape=[shape((TOK, PADDED), jnp.float32)] * 2 if last else shape((2, TOK, WIDTH), jnp.float32),
         compiler_params=pltpu.CompilerParams(vmem_limit_bytes=12 * 2**20),
         cost_estimate=pl.CostEstimate(flops=2**29, bytes_accessed=2**21, transcendentals=0),
         name="partial",
-    )(facts, mine, theirs, *given)
+    )(*given)
 
 
 def store_pieces(out_ref, latent_grad_t, hidden, up_term, facts, core):
@@ -187,10 +191,10 @@
 
 
 def grads_kernel(
-    facts_ref, hidden, before, swapped, probs, probs_t, target, up_ref,
+    length_ref, hidden, before, swapped, probs, probs_t, target, up_ref,
     out_ref, latent_grad_ref, up_term_ref, sums_ref, cot, value_grad,
 ):
-    length = facts_ref[0]
+    length = length_ref[0]
     up = up_ref[...].astype(jnp.bfloat16)
     total = before[...] + swapped[...]
     latent = total[:, KV_WIDTH:WIDTH].astype(jnp.bfloat16)
@@ -205,8 +209,8 @@
             aim = target[:, h * HEAD_DIM : (h + 1) * HEAD_DIM].astype(jnp.float32)
             differ = jnp.where(live, output[g * TOK : (g + 1) * TOK, :] - aim, 0.0)
             squares = squares + differ * differ
-            cot[g * TOK : (g + 1) * TOK, :] = differ.astype(jnp.bfloat16)
-        value_grad[:, k * HEAD_DIM : (k + 1) * HEAD_DIM] = nn(probs_t[k], cot[...]).astype(jnp.bfloat16)
+            cot[k, g * TOK : (g + 1) * TOK, :] = differ.astype(jnp.bfloat16)
+        value_grad[:, k * HEAD_DIM : (k + 1) * HEAD_DIM] = nn(probs_t[k], cot[k]).astype(jnp.bfloat16)
 
     grad = value_grad[...]
     latent_grad_t = nt(up, grad).astype(jnp.bfloat16)
@@ -221,13 +225,13 @@
     latent_grad_ref[...] = latent_grad_t
     up_term_ref[...] = up_term
     sums_ref[...] = sums
-    store_pieces(out_ref, latent_grad_t, hidden, up_term, sums, 1 - facts_ref[1])
+    store_pieces(out_ref, latent_grad_t, hidden, up_term, sums, 1 - places()[0])
 
 
 PIECES = jax.ShapeDtypeStruct((MODEL // RANK // 2, PIECE_ROWS, HEAD_DIM), jnp.float32)
 
 
-def gradients(facts, hidden, before, swapped, probs, probs_t, target, up_map):
+def gradients(lengths, hidden, before, swapped, probs, probs_t, target, up_map):
     vmem = pl.BlockSpec(memory_space=pltpu.VMEM)
     shape = jax.ShapeDtypeStruct
     return pl.pallas_call(
@@ -241,30 +245,30 @@
             shape((8, HEAD_DIM), jnp.float32),
         ],
         scratch_shapes=[
-            pltpu.VMEM((GROUP * TOK, HEAD_DIM), jnp.bfloat16),
+            pltpu.VMEM((KEY_VALUE_HEADS, GROUP * TOK, HEAD_DIM), jnp.bfloat16),
             pltpu.VMEM((TOK, KV_WIDTH), jnp.bfloat16),
         ],
         compiler_params=pltpu.CompilerParams(vmem_limit_bytes=24 * 2**20),
         cost_estimate=pl.CostEstimate(flops=2**32, bytes_accessed=10 * 2**20, transcendentals=0),
         name="grads",
-    )(facts, hidden, before, swapped, probs, probs_t, target, up_map)
-
-
-def keep_kernel(facts_ref, hidden, latent_grad_ref, up_term_ref, sums_ref, out_ref):
-    store_pieces(out_ref, latent_grad_ref[...], hidden, up_term_ref[...], sums_ref[...], facts_ref[1])
-
-
-def kept_pieces(facts, hidden, latent_grad_t, up_term, sums):
+    )(lengths, hidden, before, swapped, probs, probs_t, target, up_map)
+
+
+def keep_kernel(hidden, latent_grad_ref, up_term_ref, sums_ref, out_ref):
+    store_pieces(out_ref, latent_grad_ref[...], hidden, up_term_ref[...], sums_ref[...], places()[0])
+
+
+def kept_pieces(hidden, latent_grad_t, up_term, sums):
     vmem = pl.BlockSpec(memory_space=pltpu.VMEM)
     return pl.pallas_call(
         keep_kernel,
-        in_specs=[pl.BlockSpec(memory_space=pltpu.SMEM)] + [vmem] * 4,
+        in_specs=[vmem] * 4,
         out_specs=vmem,
         out_shape=PIECES,
         compiler_params=pltpu.CompilerParams(vmem_limit_bytes=8 * 2**20),
         cost_estimate=pl.CostEstimate(flops=2**28, bytes_accessed=2**21, transcendentals=0),
         name="keep",
-    )(facts, hidden, latent_grad_t, up_term, sums)
+    )(hidden, latent_grad_t, up_term, sums)
 
 
 def halved(wide):
@@ -400,13 +404,10 @@
     average_up_map,
 ):
     owners, replicas = lax.axis_size("fsdp"), lax.axis_size("dp")
-    place = lax.axis_index("fsdp").astype(jnp.int32)
-    plane = lax.axis_index("dp").astype(jnp.int32)
-    quarter = (plane & 1) * 2 + ((place >> 3) & 1)
-    facts = jnp.stack([lengths[0], place & 1, (place >> 1) & 3, quarter])
+    quarter = places()[2]
     shards = packed_shard(value_weight_frozen, adapter_down_map, owners // 8)
     own = lax.all_to_all(shards, "fsdp", 0, 0, tiled=True, axis_index_groups=along_y(owners))
-    mine, send = split_hidden(facts, hidden)
+    mine, send = split_hidden(hidden)
     theirs = from_other_core(send, owners)
     probs, probs_t = attention_probs(lengths, queries, keys)
     part = along_x(lax.dynamic_slice_in_dim(own, quarter * 2, 2, axis=0), owners, 2)
@@ -415,16 +416,17 @@
     beside = from_neighbour(part, owners, replicas, 1, 0)
     behind = from_neighbour(part, owners, replicas, 0, 1)
     corner = from_neighbour(part, owners, replicas, 1, 1)
-    total = None
-    for shift, given in ((0, (own,)), (3, (far,)), (2, (part, beside, behind, corner))):
-        total = partial_values(facts, mine, theirs, given, shift, total)
-    total, other = partial_values(facts, mine, theirs, (near,), 1, total, last=True)
+    total = partial_values(first_kernel, mine, theirs, own)
+    total = partial_values(next_kernel, mine, theirs, far, total)
+    total, other = partial_values(
+        last_kernel, mine, theirs, part, beside, behind, corner, near, total
+    )
     swapped = from_other_core(other, owners)
     pieces, latent_grad_t, up_term, sums = gradients(
-        facts, send, total, swapped, probs, probs_t, target, adapter_up_map
+        lengths, send, total, swapped, probs, probs_t, target, adapter_up_map
     )
     came = from_other_core(pieces, owners)
-    kept = kept_pieces(facts, mine, latent_grad_t, up_term, sums)
+    kept = kept_pieces(mine, latent_grad_t, up_term, sums)
     arrived = lax.all_to_all(
         merged(kept, came), "fsdp", 0, 0, tiled=True, axis_index_groups=same_core(owners)
     )

time: 155 us -> 154 us (level)
  waiting for transfers between devices: 18 us -> 20.3 us
  Pallas kernels: 20.9 us -> 18.9 us
  local copies, waits for them, and re-layouts: 6.41 us -> 4.82 us
    pallas_call x6 -> x5, Pallas kernels: 9.55 us -> 6.66 us  [the longest x3 4.1 us: partial_values(): pl.pallas_call(body, in_specs=[vmem] * len(given), out_specs=[vmem, vmem]...]
    unnamed x20 -> x16, local copies, waits for them, and re-layouts: 6.39 us -> 4.79 us
  transfers between devices with their start and end apart: 10 -> 10, of which waited for: 3 -> 4; matrix products, arithmetic and copies ran while one was open for 0% -> 0% of each run, Pallas kernels for 8% -> 7%
where the time goes in v6:
time: 154 us; the launch traced here: 153 us
  starting transfers between devices  58.4 us (38%)
  blocking collectives  49.1 us (32%)
  waiting for transfers between devices  20.3 us (13%)
  Pallas kernels  18.9 us (12%)
  local copies, waits for them, and re-layouts  4.82 us (3%)
    all_to_all x2, blocking collectives, exchange(): return lax.all_to_all(pieces, axis, 0, 0, tiled=True)  32.1 us
    ppermute x3, starting transfers between devices, from_neighbour(): return lax.ppermute(part, ('dp', 'fsdp'), moved)  18.1 us
    ppermute x3, starting transfers between devices, along_x(): return lax.ppermute(block, 'fsdp', moved)  17.4 us
    all_to_all x1, blocking collectives, per_device(): lax.all_to_all(merged(kept, came), 'fsdp', 0, 0, tiled=True, axis_index_g...  17 us
    ppermute x3, waiting for transfers between devices, along_x(): return lax.ppermute(block, 'fsdp', moved)  15.6 us
    ppermute x3, starting transfers between devices, from_other_core(): return lax.ppermute(block, 'fsdp', [(i, i ^ 1) for i in range(owners)])  15.2 us
    all_to_all x1, starting transfers between devices, per_device(): lax.all_to_all(shards, 'fsdp', 0, 0, tiled=True, axis_index_groups=along_...  7.64 us
    pallas_call x1, Pallas kernels, attention_probs(): pl.pallas_call(probs_kernel, grid=(KEY_VALUE_HEADS,), in_specs=[pl.BlockS...  5.2 us
  transfers between devices with their start and end apart: 10, of which 4 were waited for; matrix products, arithmetic and copies ran while one was open for 0% of the time, Pallas kernels for 7%

profile of v6, /device:TPU:1, one launch (start us, length us, event | category | flops | bytes accessed | tf_op | source)
XLA Modules:
  0.0 153.1 jit_solution(10238332478474864707)
XLA Ops:
  0.6 1.8 %pack.1 = bf16[8,64,576]{2,1,0:T(8,128)(2,1)} custom-call(bf16[64,512]{1,0:T(8,128)(2,1)} %value_ref.1, f32[64,64]{1,0:T(8,128)} %down_ref.3), custom_call_target="tpu_custom_call" | custom-call | tf_op jit(solution)/shard_map/pack/pallas_call | solution.py:86
  2.4 7.6 %all-to-all-start = ((bf16[8,64,576]{2,1,0:T(8,128)(2,1)}), bf16[8,64,576]{2,1,0:T(8,128)(2,1)S(1)}, u32[]{:S(2)}, u32[]{:S(2)}) async-start(bf16[8,64,576]{2,1,0:T(8,128)(2,1)} %pack.1), calls=%async_computation | async-start | bytes 1310720 | tf_op jit(solution)/shard_map/all_to_all | solution.py:409
  10.0 1.6 %copy-done.4 = bf16[256,4096]{1,0:T(8,128)(2,1)S(1)} copy-done((bf16[256,4096]{1,0:T(8,128)(2,1)S(1)}, bf16[256,4096]{1,0:T(8,128)(2,1)}, u32[]{:S(2)}) %copy-start.4) | copy-done | bytes 2097176
  11.6 2.2 %split.1 = (bf16[256,2048]{1,0:T(8,128)(2,1)S(1)}, bf16[256,2048]{1,0:T(8,128)(2,1)}) custom-call(bf16[256,4096]{1,0:T(8,128)(2,1)S(1)} %copy-done.4), custom_call_target="tpu_custom_call" | custom-call | flops 1073741824 | bytes 4194304 | tf_op jit(solution)/shard_map/split/pallas_call | solution.py:116
  13.8 8.3 %collective-permute-start = (bf16[256,2048]{1,0:T(8,128)(2,1)}, bf16[256,2048]{1,0:T(8,128)(2,1)S(1)}, u32[]{:S(2)}, u32[]{:S(2)}) collective-permute-start(bf16[256,2048]{1,0:T(8,128)(2,1)} %get-tuple-element.22.hidden), channel_id=1, source_target_pairs={{0,1},{1,0},{2,3},{3,2},{4,5},{5,4},{6,7},{7,6},{8,9},{9,8},{10,11... | collective-permute-start | bytes 3145736 | tf_op jit(solution)/shard_map/ppermute | solution.py:391
  23.3 11.9 %collective-permute-start.6 = (bf16[8,64,576]{2,1,0:T(8,128)(2,1)S(1)}, bf16[8,64,576]{2,1,0:T(8,128)(2,1)}, u32[]{:S(2)}, u32[]{:S(2)}) collective-permute-start(bf16[8,64,576]{2,1,0:T(8,128)(2,1)S(1)} %all-to-all-done.own), channel_id=1, source_target_pairs={{0,6},{1,7},{2,0},{3,1},{4,2},{5,3},{6,4},{7,5},{8,14},{9,15},{10,... | collective-permute-start | bytes 1769480 | tf_op jit(solution)/shard_map/ppermute | solution.py:378
  35.2 1.9 %collective-permute-start.5 = (bf16[8,64,576]{2,1,0:T(8,128)(2,1)S(1)}, bf16[8,64,576]{2,1,0:T(8,128)(2,1)S(1)}, u32[]{:S(2)}, u32[]{:S(2)}) collective-permute-start(bf16[8,64,576]{2,1,0:T(8,128)(2,1)S(1)} %all-to-all-done.own), channel_id=1, source_target_pairs={{0,2},{1,3},{2,4},{3,5},{4,6},{5,7},{6,0},{7,1},{8,10},{9,11},{10,... | collective-permute-start | bytes 1769480 | tf_op jit(solution)/shard_map/ppermute | solution.py:378
  37.1 3.6 %collective-permute-start.1 = (bf16[2,64,576]{2,1,0:T(8,128)(2,1)S(1)}, bf16[2,64,576]{2,1,0:T(8,128)(2,1)S(1)}, u32[]{:S(2)}, u32[]{:S(2)}) collective-permute-start(bf16[2,64,576]{2,1,0:T(8,128)(2,1)S(1)} %constant_dynamic-slice_fusion), channel_id=1, source_target_pairs={{0,4},{1,5},{2,6},{3,7},{4,0},{5,1},{6,2},{7,3},{8,12},{9,13},{10,... | collective-permute-start | bytes 442376 | tf_op jit(solution)/shard_map/ppermute | solution.py:378
  40.8 15.6 %collective-permute-done.1.q0 = bf16[2,64,576]{2,1,0:T(8,128)(2,1)S(1)} collective-permute-done((bf16[2,64,576]{2,1,0:T(8,128)(2,1)S(1)}, bf16[2,64,576]{2,1,0:T(8,128)(2,1)S(1)}, u32[]{:S(2)}, u32[]{:S(2)}) %collective-permute-start.1) | collective-permute-done | bytes 147488 | tf_op jit(solution)/shard_map/ppermute | solution.py:378
  56.4 2.8 %collective-permute-start.4 = (bf16[2,64,576]{2,1,0:T(8,128)(2,1)S(1)}, bf16[2,64,576]{2,1,0:T(8,128)(2,1)S(1)}, u32[]{:S(2)}, u32[]{:S(2)}) collective-permute-start(bf16[2,64,576]{2,1,0:T(8,128)(2,1)S(1)} %collective-permute-done.1.q0), channel_id=1, source_target_pairs={{72,0},{73,1},{74,2},{75,3},{76,4},{77,5},{78,6},{79,7},{80,8},{81... | collective-permute-start | bytes 442376 | tf_op jit(solution)/shard_map/ppermute | solution.py:387
  59.3 13.4 %collective-permute-start.3 = (bf16[2,64,576]{2,1,0:T(8,128)(2,1)S(1)}, bf16[2,64,576]{2,1,0:T(8,128)(2,1)S(1)}, u32[]{:S(2)}, u32[]{:S(2)}) collective-permute-start(bf16[2,64,576]{2,1,0:T(8,128)(2,1)S(1)} %collective-permute-done.1.q0), channel_id=1, source_target_pairs={{64,0},{65,1},{66,2},{67,3},{68,4},{69,5},{70,6},{71,7},{72,8},{73... | collective-permute-start | bytes 442376 | tf_op jit(solution)/shard_map/ppermute | solution.py:387
  72.7 1.9 %collective-permute-start.2 = (bf16[2,64,576]{2,1,0:T(8,128)(2,1)S(1)}, bf16[2,64,576]{2,1,0:T(8,128)(2,1)S(1)}, u32[]{:S(2)}, u32[]{:S(2)}) collective-permute-start(bf16[2,64,576]{2,1,0:T(8,128)(2,1)S(1)} %collective-permute-done.1.q0), channel_id=1, source_target_pairs={{8,0},{9,1},{10,2},{11,3},{12,4},{13,5},{14,6},{15,7},{16,8},{17,9... | collective-permute-start | bytes 442376 | tf_op jit(solution)/shard_map/ppermute | solution.py:387
  75.2 1.7 %partial.4.before = f32[2,256,576]{2,1,0:T(8,128)S(1)} custom-call(bf16[256,2048]{1,0:T(8,128)(2,1)S(1)} %get-tuple-element.21.mine.hidden, bf16[256,2048]{1,0:T(8,128)(2,1)S(1)} %collective-permute-done.theirs, bf16[8,64,576]{2,1,0:T(8,128)(2,1)} %collective-permute-done.6.far, f32[2,256,576]{2,1,0:T(8,128)S(1)} %partial.3.before), custom_call_target="tpu_custom_call" | custom-call | flops 536870912 | bytes 2097152 | tf_op jit(solution)/shard_map/partial/pallas_call | solution.py:165
  76.9 1.9 %collective-permute-done.2.q1 = bf16[2,64,576]{2,1,0:T(8,128)(2,1)S(1)} collective-permute-done((bf16[2,64,576]{2,1,0:T(8,128)(2,1)S(1)}, bf16[2,64,576]{2,1,0:T(8,128)(2,1)S(1)}, u32[]{:S(2)}, u32[]{:S(2)}) %collective-permute-start.2) | collective-permute-done | bytes 147488 | tf_op jit(solution)/shard_map/ppermute | solution.py:387
  78.7 1.9 %partial.5 = (f32[256,640]{1,0:T(8,128)S(1)}, f32[256,640]{1,0:T(8,128)}) custom-call(bf16[256,2048]{1,0:T(8,128)(2,1)S(1)} %get-tuple-element.21.mine.hidden, bf16[256,2048]{1,0:T(8,128)(2,1)S(1)} %collective-permute-done.theirs, bf16[2,64,576]{2,1,0:T(8,128)(2,1)S(1)} %collective-permute-done.1.q0, bf16[2,64,576]{2,1,0:T(8,128)(2,1)S(1)} %collective-permute-done.2.q1, ...), custom_call_target="tpu_custom_call" | custom-call | flops 536870912 | bytes 2097152 | tf_op jit(solution)/shard_map/partial/pallas_call | solution.py:165
  80.6 5.0 %collective-permute-start.7 = (f32[256,640]{1,0:T(8,128)}, f32[256,640]{1,0:T(8,128)S(1)}, u32[]{:S(2)}, u32[]{:S(2)}) collective-permute-start(f32[256,640]{1,0:T(8,128)} %get-tuple-element.24), channel_id=1, source_target_pairs={{0,1},{1,0},{2,3},{3,2},{4,5},{5,4},{6,7},{7,6},{8,9},{9,8},{10,11... | collective-permute-start | bytes 1966088 | tf_op jit(solution)/shard_map/ppermute | solution.py:391
  86.3 5.2 %probs.1 = (bf16[4,1024,256]{2,1,0:T(8,128)(2,1)}, bf16[4,256,1024]{2,1,0:T(8,128)(2,1)}) custom-call(s32[1]{0:T(128)S(6)} %copy.15.length_ref, bf16[256,2048]{1,0:T(8,128)(2,1)} %q_ref.1, bf16[256,512]{1,0:T(8,128)(2,1)} %k_ref.1), custom_call_target="tpu_custom_call" | custom-call | flops 2147483648 | bytes 6291456 | tf_op jit(solution)/shard_map/probs/pallas_call | solution.py:56
  93.1 1.6 %copy-done.7 = bf16[4,256,1024]{2,1,0:T(8,128)(2,1)S(1)} copy-done((bf16[4,256,1024]{2,1,0:T(8,128)(2,1)S(1)}, bf16[4,256,1024]{2,1,0:T(8,128)(2,1)}, u32[]{:S(2)}) %copy-start.7) | copy-done | bytes 2097176
  94.7 3.6 %grads.1 = (f32[32,40,128]{2,1,0:T(8,128)S(1)}, bf16[64,256]{1,0:T(8,128)(2,1)S(1)}, f32[64,512]{1,0:T(8,128)S(1)}, f32[8,128]{1,0:T(8,128)S(1)}) custom-call(s32[1]{0:T(128)S(6)} %copy.15.length_ref, bf16[256,2048]{1,0:T(8,128)(2,1)} %get-tuple-element.22.hidden, f32[256,640]{1,0:T(8,128)S(1)} %get-tuple-element.23.before, ...), custom_call_target="tpu_custom_call" | custom-call | flops 4294967296 | bytes 10485760 | tf_op jit(solution)/shard_map/grads/pallas_call | solution.py:237
  98.2 1.9 %collective-permute-start.8 = (f32[32,40,128]{2,1,0:T(8,128)S(1)}, f32[32,40,128]{2,1,0:T(8,128)S(1)}, u32[]{:S(2)}, u32[]{:S(2)}) collective-permute-start(f32[32,40,128]{2,1,0:T(8,128)S(1)} %get-tuple-element.30), channel_id=1, source_target_pairs={{0,1},{1,0},{2,3},{3,2},{4,5},{5,4},{6,7},{7,6},{8,9},{9,8},{10,11... | collective-permute-start | bytes 1966088 | tf_op jit(solution)/shard_map/ppermute | solution.py:391
  100.6 1.6 %collective-permute-done.8.came = f32[32,40,128]{2,1,0:T(8,128)S(1)} collective-permute-done((f32[32,40,128]{2,1,0:T(8,128)S(1)}, f32[32,40,128]{2,1,0:T(8,128)S(1)}, u32[]{:S(2)}, u32[]{:S(2)}) %collective-permute-start.8) | collective-permute-done | bytes 655392 | tf_op jit(solution)/shard_map/ppermute | solution.py:391
  102.3 17.0 %all_to_all.20.pieces_ref = bf16[32,40,128]{2,1,0:T(8,128)(2,1)S(1)} all-to-all(bf16[32,40,128]{2,1,0:T(8,128)(2,1)S(1)} %merge.1), channel_id=1, replica_groups={{0,2,4,6,8,10,12,14,16,18,20,22,24,26,28,30,32,34,36,38,40,42,44,46,48,..., dimensions={0} | all-to-all | bytes 655360 | tf_op jit(solution)/shard_map/all_to_all | solution.py:430
  119.4 13.0 %all_to_all.21.pieces_ref = bf16[12,48,128]{2,1,0:T(8,128)(2,1)S(1)} all-to-all(bf16[12,48,128]{2,1,0:T(8,128)(2,1)S(1)} %fold.1), channel_id=1, replica_groups=mesh['dp'=12,'fsdp'=64] {'dp'}, dimensions={0} | all-to-all | bytes 294912 | tf_op jit(solution)/shard_map/all_to_all | solution.py:365
  133.3 19.0 %all_to_all.22.pieces_ref = f32[64,4,128]{2,1,0:T(4,128)S(1)} all-to-all(f32[64,4,128]{2,1,0:T(4,128)S(1)} %get-tuple-element.32), channel_id=1, replica_groups=mesh['dp'=12,'fsdp'=64] {'fsdp'}, dimensions={0} | all-to-all | bytes 262144 | tf_op jit(solution)/shard_map/all_to_all | solution.py:365
  (28 shorter events, 5.6 us)
Async XLA Ops:
  2.4 20.9 %all-to-all-start = ((bf16[8,64,576]{2,1,0:T(8,128)(2,1)}), bf16[8,64,576]{2,1,0:T(8,128)(2,1)S(1)}, u32[]{:S(2)}, u32[]{:S(2)}) async-start(bf16[8,64,576]{2,1,0:T(8,128)(2,1)} %pack.1), calls=%async_computation | async-start | bytes 1310720 | tf_op jit(solution)/shard_map/all_to_all | solution.py:409
  10.0 1.6 %copy-start.4 = (bf16[256,4096]{1,0:T(8,128)(2,1)S(1)}, bf16[256,4096]{1,0:T(8,128)(2,1)}, u32[]{:S(2)}) copy-start(bf16[256,4096]{1,0:T(8,128)(2,1)} %hidden.1) | copy-start | bytes 6291460
  13.8 58.9 %collective-permute-start = (bf16[256,2048]{1,0:T(8,128)(2,1)}, bf16[256,2048]{1,0:T(8,128)(2,1)S(1)}, u32[]{:S(2)}, u32[]{:S(2)}) collective-permute-start(bf16[256,2048]{1,0:T(8,128)(2,1)} %get-tuple-element.22.hidden), channel_id=1, source_target_pairs={{0,1},{1,0},{2,3},{3,2},{4,5},{5,4},{6,7},{7,6},{8,9},{9,8},{10,11... | collective-permute-start | bytes 3145736 | tf_op jit(solution)/shard_map/ppermute | solution.py:391
  23.3 51.9 %collective-permute-start.6 = (bf16[8,64,576]{2,1,0:T(8,128)(2,1)S(1)}, bf16[8,64,576]{2,1,0:T(8,128)(2,1)}, u32[]{:S(2)}, u32[]{:S(2)}) collective-permute-start(bf16[8,64,576]{2,1,0:T(8,128)(2,1)S(1)} %all-to-all-done.own), channel_id=1, source_target_pairs={{0,6},{1,7},{2,0},{3,1},{4,2},{5,3},{6,4},{7,5},{8,14},{9,15},{10,... | collective-permute-start | bytes 1769480 | tf_op jit(solution)/shard_map/ppermute | solution.py:378
  35.2 43.5 %collective-permute-start.5 = (bf16[8,64,576]{2,1,0:T(8,128)(2,1)S(1)}, bf16[8,64,576]{2,1,0:T(8,128)(2,1)S(1)}, u32[]{:S(2)}, u32[]{:S(2)}) collective-permute-start(bf16[8,64,576]{2,1,0:T(8,128)(2,1)S(1)} %all-to-all-done.own), channel_id=1, source_target_pairs={{0,2},{1,3},{2,4},{3,5},{4,6},{5,7},{6,0},{7,1},{8,10},{9,11},{10,... | collective-permute-start | bytes 1769480 | tf_op jit(solution)/shard_map/ppermute | solution.py:378
  37.1 19.3 %collective-permute-start.1 = (bf16[2,64,576]{2,1,0:T(8,128)(2,1)S(1)}, bf16[2,64,576]{2,1,0:T(8,128)(2,1)S(1)}, u32[]{:S(2)}, u32[]{:S(2)}) collective-permute-start(bf16[2,64,576]{2,1,0:T(8,128)(2,1)S(1)} %constant_dynamic-slice_fusion), channel_id=1, source_target_pairs={{0,4},{1,5},{2,6},{3,7},{4,0},{5,1},{6,2},{7,3},{8,12},{9,13},{10,... | collective-permute-start | bytes 442376 | tf_op jit(solution)/shard_map/ppermute | solution.py:378
  56.4 20.4 %collective-permute-start.4 = (bf16[2,64,576]{2,1,0:T(8,128)(2,1)S(1)}, bf16[2,64,576]{2,1,0:T(8,128)(2,1)S(1)}, u32[]{:S(2)}, u32[]{:S(2)}) collective-permute-start(bf16[2,64,576]{2,1,0:T(8,128)(2,1)S(1)} %collective-permute-done.1.q0), channel_id=1, source_target_pairs={{72,0},{73,1},{74,2},{75,3},{76,4},{77,5},{78,6},{79,7},{80,8},{81... | collective-permute-start | bytes 442376 | tf_op jit(solution)/shard_map/ppermute | solution.py:387
  59.3 17.6 %collective-permute-start.3 = (bf16[2,64,576]{2,1,0:T(8,128)(2,1)S(1)}, bf16[2,64,576]{2,1,0:T(8,128)(2,1)S(1)}, u32[]{:S(2)}, u32[]{:S(2)}) collective-permute-start(bf16[2,64,576]{2,1,0:T(8,128)(2,1)S(1)} %collective-permute-done.1.q0), channel_id=1, source_target_pairs={{64,0},{65,1},{66,2},{67,3},{68,4},{69,5},{70,6},{71,7},{72,8},{73... | collective-permute-start | bytes 442376 | tf_op jit(solution)/shard_map/ppermute | solution.py:387
  72.7 6.1 %collective-permute-start.2 = (bf16[2,64,576]{2,1,0:T(8,128)(2,1)S(1)}, bf16[2,64,576]{2,1,0:T(8,128)(2,1)S(1)}, u32[]{:S(2)}, u32[]{:S(2)}) collective-permute-start(bf16[2,64,576]{2,1,0:T(8,128)(2,1)S(1)} %collective-permute-done.1.q0), channel_id=1, source_target_pairs={{8,0},{9,1},{10,2},{11,3},{12,4},{13,5},{14,6},{15,7},{16,8},{17,9... | collective-permute-start | bytes 442376 | tf_op jit(solution)/shard_map/ppermute | solution.py:387
  80.6 10.9 %collective-permute-start.7 = (f32[256,640]{1,0:T(8,128)}, f32[256,640]{1,0:T(8,128)S(1)}, u32[]{:S(2)}, u32[]{:S(2)}) collective-permute-start(f32[256,640]{1,0:T(8,128)} %get-tuple-element.24), channel_id=1, source_target_pairs={{0,1},{1,0},{2,3},{3,2},{4,5},{5,4},{6,7},{7,6},{8,9},{9,8},{10,11... | collective-permute-start | bytes 1966088 | tf_op jit(solution)/shard_map/ppermute | solution.py:391
  86.2 5.2 %copy-start = (f32[64,512]{1,0:T(8,128)S(1)}, f32[64,512]{1,0:T(8,128)}, u32[]{:S(2)}) copy-start(f32[64,512]{1,0:T(8,128)} %up_ref.3) | copy-start | bytes 393220
  86.3 5.2 %copy-start.5 = (bf16[256,2048]{1,0:T(8,128)(2,1)S(1)}, bf16[256,2048]{1,0:T(8,128)(2,1)}, u32[]{:S(2)}) copy-start(bf16[256,2048]{1,0:T(8,128)(2,1)} %target.1) | copy-start | bytes 3145732
  91.5 1.6 %copy-start.6 = (bf16[4,1024,256]{2,1,0:T(8,128)(2,1)S(1)}, bf16[4,1024,256]{2,1,0:T(8,128)(2,1)}, u32[]{:S(2)}) copy-start(bf16[4,1024,256]{2,1,0:T(8,128)(2,1)} %get-tuple-element.25.probs) | copy-start | bytes 6291460
  93.1 1.6 %copy-start.7 = (bf16[4,256,1024]{2,1,0:T(8,128)(2,1)S(1)}, bf16[4,256,1024]{2,1,0:T(8,128)(2,1)}, u32[]{:S(2)}) copy-start(bf16[4,256,1024]{2,1,0:T(8,128)(2,1)} %get-tuple-element.26.probs_t) | copy-start | bytes 6291460
  98.2 4.0 %collective-permute-start.8 = (f32[32,40,128]{2,1,0:T(8,128)S(1)}, f32[32,40,128]{2,1,0:T(8,128)S(1)}, u32[]{:S(2)}, u32[]{:S(2)}) collective-permute-start(f32[32,40,128]{2,1,0:T(8,128)S(1)} %get-tuple-element.30), channel_id=1, source_target_pairs={{0,1},{1,0},{2,3},{3,2},{4,5},{5,4},{6,7},{7,6},{8,9},{9,8},{10,11... | collective-permute-start | bytes 1966088 | tf_op jit(solution)/shard_map/ppermute | solution.py:391
  100.2 32.3 %copy-start.2 = (f32[64,64]{1,0:T(8,128)S(1)}, f32[64,64]{1,0:T(8,128)}, u32[]{:S(2)}) copy-start(f32[64,64]{1,0:T(8,128)} %down_ref.3) | copy-start | bytes 49156
  100.2 32.3 %copy-start.3 = (f32[64,64]{1,0:T(8,128)S(1)}, f32[64,64]{1,0:T(8,128)}, u32[]{:S(2)}) copy-start(f32[64,64]{1,0:T(8,128)} %average_ref.2) | copy-start | bytes 49156
  100.6 51.7 %copy-start.1 = (f32[64,512]{1,0:T(8,128)S(1)}, f32[64,512]{1,0:T(8,128)}, u32[]{:S(2)}) copy-start(f32[64,512]{1,0:T(8,128)} %average_ref.3) | copy-start | bytes 393220

commit v7 on v6

--- a/solution.py
+++ b/solution.py
@@ -202,14 +202,15 @@
 
     live = lax.broadcasted_iota(jnp.int32, (TOK, HEAD_DIM), 0) < length
     squares = jnp.zeros((TOK, HEAD_DIM), jnp.float32)
+    outputs = [nn(probs[k], values[:, k * HEAD_DIM : (k + 1) * HEAD_DIM]) for k in range(KEY_VALUE_HEADS)]
     for k in range(KEY_VALUE_HEADS):
-        output = nn(probs[k], values[:, k * HEAD_DIM : (k + 1) * HEAD_DIM])
         for g in range(GROUP):
             h = k * GROUP + g
             aim = target[:, h * HEAD_DIM : (h + 1) * HEAD_DIM].astype(jnp.float32)
-            differ = jnp.where(live, output[g * TOK : (g + 1) * TOK, :] - aim, 0.0)
+            differ = jnp.where(live, outputs[k][g * TOK : (g + 1) * TOK, :] - aim, 0.0)
             squares = squares + differ * differ
             cot[k, g * TOK : (g + 1) * TOK, :] = differ.astype(jnp.bfloat16)
+    for k in range(KEY_VALUE_HEADS):
         value_grad[:, k * HEAD_DIM : (k + 1) * HEAD_DIM] = nn(probs_t[k], cot[k]).astype(jnp.bfloat16)
 
     grad = value_grad[...]
@@ -324,7 +325,7 @@
     grad = jnp.transpose(rows) * factor
     grad_ref[...] = grad
     next_ref[...] = average_decay * average_ref[...] + (1.0 - average_decay) * (down_ref[...] - learning_rate * grad)
-    piece = tail[:4, :] * factor
+    piece = (tail[:4, :] * factor).astype(jnp.bfloat16)
     for d in range(up_ref.shape[0]):
         up_ref[d] = piece
 
@@ -336,7 +337,7 @@
         out_shape=[
             shape((RANK, RANK), jnp.float32),
             shape((RANK, RANK), jnp.float32),
-            shape((copies, 4, HEAD_DIM), jnp.float32),
+            shape((copies, 4, HEAD_DIM), jnp.bfloat16),
             shape((1, 1), jnp.float32),
         ],
         compiler_params=SMALL,
@@ -348,7 +349,7 @@
     for j in range(MODEL // RANK):
         q, b = divmod(j // 2, 4)
         top = 8 * q + 4 * (j % 2)
-        grad_ref[top : top + 4, b * 128 : (b + 1) * 128] = pieces_ref[j]
+        grad_ref[top : top + 4, b * 128 : (b + 1) * 128] = pieces_ref[j].astype(jnp.float32)
     next_ref[...] = average_decay * average_ref[...] + (1.0 - average_decay) * (
         up_ref[...] - learning_rate * grad_ref[...]
     )

time: 154 us -> 153 us (level)
  no operation moved by 1% of the time
where the time goes in v7:
time: 153 us; the launch traced here: 152 us
  starting transfers between devices  58.4 us (38%)
  blocking collectives  48.1 us (31%)
  waiting for transfers between devices  20.3 us (13%)
  Pallas kernels  18.5 us (12%)
  local copies, waits for them, and re-layouts  4.82 us (3%)
    all_to_all x2, blocking collectives, exchange(): return lax.all_to_all(pieces, axis, 0, 0, tiled=True)  31.1 us
    ppermute x3, starting transfers between devices, from_neighbour(): return lax.ppermute(part, ('dp', 'fsdp'), moved)  18.1 us
    ppermute x3, starting transfers between devices, along_x(): return lax.ppermute(block, 'fsdp', moved)  17.4 us
    all_to_all x1, blocking collectives, per_device(): lax.all_to_all(merged(kept, came), 'fsdp', 0, 0, tiled=True, axis_index_g...  17 us
    ppermute x3, waiting for transfers between devices, along_x(): return lax.ppermute(block, 'fsdp', moved)  15.6 us
    ppermute x3, starting transfers between devices, from_other_core(): return lax.ppermute(block, 'fsdp', [(i, i ^ 1) for i in range(owners)])  15.2 us
    all_to_all x1, starting transfers between devices, per_device(): lax.all_to_all(shards, 'fsdp', 0, 0, tiled=True, axis_index_groups=along_...  7.64 us
    pallas_call x1, Pallas kernels, attention_probs(): pl.pallas_call(probs_kernel, grid=(KEY_VALUE_HEADS,), in_specs=[pl.BlockS...  5.2 us
  transfers between devices with their start and end apart: 10, of which 4 were waited for; matrix products, arithmetic and copies ran while one was open for 0% of the time, Pallas kernels for 7%

profile of v7, /device:TPU:1, one launch (start us, length us, event | category | flops | bytes accessed | tf_op | source)
XLA Modules:
  0.0 151.7 jit_solution(14891468643657226046)
XLA Ops:
  0.6 1.8 %pack.1 = bf16[8,64,576]{2,1,0:T(8,128)(2,1)} custom-call(bf16[64,512]{1,0:T(8,128)(2,1)} %value_ref.1, f32[64,64]{1,0:T(8,128)} %down_ref.3), custom_call_target="tpu_custom_call" | custom-call | tf_op jit(solution)/shard_map/pack/pallas_call | solution.py:86
  2.4 7.6 %all-to-all-start = ((bf16[8,64,576]{2,1,0:T(8,128)(2,1)}), bf16[8,64,576]{2,1,0:T(8,128)(2,1)S(1)}, u32[]{:S(2)}, u32[]{:S(2)}) async-start(bf16[8,64,576]{2,1,0:T(8,128)(2,1)} %pack.1), calls=%async_computation | async-start | bytes 1310720 | tf_op jit(solution)/shard_map/all_to_all | solution.py:410
  10.0 1.6 %copy-done.4 = bf16[256,4096]{1,0:T(8,128)(2,1)S(1)} copy-done((bf16[256,4096]{1,0:T(8,128)(2,1)S(1)}, bf16[256,4096]{1,0:T(8,128)(2,1)}, u32[]{:S(2)}) %copy-start.4) | copy-done | bytes 2097176
  11.6 2.2 %split.1 = (bf16[256,2048]{1,0:T(8,128)(2,1)S(1)}, bf16[256,2048]{1,0:T(8,128)(2,1)}) custom-call(bf16[256,4096]{1,0:T(8,128)(2,1)S(1)} %copy-done.4), custom_call_target="tpu_custom_call" | custom-call | flops 1073741824 | bytes 4194304 | tf_op jit(solution)/shard_map/split/pallas_call | solution.py:116
  13.8 8.3 %collective-permute-start = (bf16[256,2048]{1,0:T(8,128)(2,1)}, bf16[256,2048]{1,0:T(8,128)(2,1)S(1)}, u32[]{:S(2)}, u32[]{:S(2)}) collective-permute-start(bf16[256,2048]{1,0:T(8,128)(2,1)} %get-tuple-element.22.hidden), channel_id=1, source_target_pairs={{0,1},{1,0},{2,3},{3,2},{4,5},{5,4},{6,7},{7,6},{8,9},{9,8},{10,11... | collective-permute-start | bytes 3145736 | tf_op jit(solution)/shard_map/ppermute | solution.py:392
  23.3 11.9 %collective-permute-start.6 = (bf16[8,64,576]{2,1,0:T(8,128)(2,1)S(1)}, bf16[8,64,576]{2,1,0:T(8,128)(2,1)}, u32[]{:S(2)}, u32[]{:S(2)}) collective-permute-start(bf16[8,64,576]{2,1,0:T(8,128)(2,1)S(1)} %all-to-all-done.own), channel_id=1, source_target_pairs={{0,6},{1,7},{2,0},{3,1},{4,2},{5,3},{6,4},{7,5},{8,14},{9,15},{10,... | collective-permute-start | bytes 1769480 | tf_op jit(solution)/shard_map/ppermute | solution.py:379
  35.2 1.9 %collective-permute-start.5 = (bf16[8,64,576]{2,1,0:T(8,128)(2,1)S(1)}, bf16[8,64,576]{2,1,0:T(8,128)(2,1)S(1)}, u32[]{:S(2)}, u32[]{:S(2)}) collective-permute-start(bf16[8,64,576]{2,1,0:T(8,128)(2,1)S(1)} %all-to-all-done.own), channel_id=1, source_target_pairs={{0,2},{1,3},{2,4},{3,5},{4,6},{5,7},{6,0},{7,1},{8,10},{9,11},{10,... | collective-permute-start | bytes 1769480 | tf_op jit(solution)/shard_map/ppermute | solution.py:379
  37.1 3.6 %collective-permute-start.1 = (bf16[2,64,576]{2,1,0:T(8,128)(2,1)S(1)}, bf16[2,64,576]{2,1,0:T(8,128)(2,1)S(1)}, u32[]{:S(2)}, u32[]{:S(2)}) collective-permute-start(bf16[2,64,576]{2,1,0:T(8,128)(2,1)S(1)} %constant_dynamic-slice_fusion), channel_id=1, source_target_pairs={{0,4},{1,5},{2,6},{3,7},{4,0},{5,1},{6,2},{7,3},{8,12},{9,13},{10,... | collective-permute-start | bytes 442376 | tf_op jit(solution)/shard_map/ppermute | solution.py:379
  40.8 15.6 %collective-permute-done.1.q0 = bf16[2,64,576]{2,1,0:T(8,128)(2,1)S(1)} collective-permute-done((bf16[2,64,576]{2,1,0:T(8,128)(2,1)S(1)}, bf16[2,64,576]{2,1,0:T(8,128)(2,1)S(1)}, u32[]{:S(2)}, u32[]{:S(2)}) %collective-permute-start.1) | collective-permute-done | bytes 147488 | tf_op jit(solution)/shard_map/ppermute | solution.py:379
  56.4 2.8 %collective-permute-start.4 = (bf16[2,64,576]{2,1,0:T(8,128)(2,1)S(1)}, bf16[2,64,576]{2,1,0:T(8,128)(2,1)S(1)}, u32[]{:S(2)}, u32[]{:S(2)}) collective-permute-start(bf16[2,64,576]{2,1,0:T(8,128)(2,1)S(1)} %collective-permute-done.1.q0), channel_id=1, source_target_pairs={{72,0},{73,1},{74,2},{75,3},{76,4},{77,5},{78,6},{79,7},{80,8},{81... | collective-permute-start | bytes 442376 | tf_op jit(solution)/shard_map/ppermute | solution.py:388
  59.3 13.4 %collective-permute-start.3 = (bf16[2,64,576]{2,1,0:T(8,128)(2,1)S(1)}, bf16[2,64,576]{2,1,0:T(8,128)(2,1)S(1)}, u32[]{:S(2)}, u32[]{:S(2)}) collective-permute-start(bf16[2,64,576]{2,1,0:T(8,128)(2,1)S(1)} %collective-permute-done.1.q0), channel_id=1, source_target_pairs={{64,0},{65,1},{66,2},{67,3},{68,4},{69,5},{70,6},{71,7},{72,8},{73... | collective-permute-start | bytes 442376 | tf_op jit(solution)/shard_map/ppermute | solution.py:388
  72.7 1.9 %collective-permute-start.2 = (bf16[2,64,576]{2,1,0:T(8,128)(2,1)S(1)}, bf16[2,64,576]{2,1,0:T(8,128)(2,1)S(1)}, u32[]{:S(2)}, u32[]{:S(2)}) collective-permute-start(bf16[2,64,576]{2,1,0:T(8,128)(2,1)S(1)} %collective-permute-done.1.q0), channel_id=1, source_target_pairs={{8,0},{9,1},{10,2},{11,3},{12,4},{13,5},{14,6},{15,7},{16,8},{17,9... | collective-permute-start | bytes 442376 | tf_op jit(solution)/shard_map/ppermute | solution.py:388
  75.2 1.7 %partial.4.before = f32[2,256,576]{2,1,0:T(8,128)S(1)} custom-call(bf16[256,2048]{1,0:T(8,128)(2,1)S(1)} %get-tuple-element.21.mine.hidden, bf16[256,2048]{1,0:T(8,128)(2,1)S(1)} %collective-permute-done.theirs, bf16[8,64,576]{2,1,0:T(8,128)(2,1)} %collective-permute-done.6.far, f32[2,256,576]{2,1,0:T(8,128)S(1)} %partial.3.before), custom_call_target="tpu_custom_call" | custom-call | flops 536870912 | bytes 2097152 | tf_op jit(solution)/shard_map/partial/pallas_call | solution.py:165
  76.9 1.9 %collective-permute-done.2.q1 = bf16[2,64,576]{2,1,0:T(8,128)(2,1)S(1)} collective-permute-done((bf16[2,64,576]{2,1,0:T(8,128)(2,1)S(1)}, bf16[2,64,576]{2,1,0:T(8,128)(2,1)S(1)}, u32[]{:S(2)}, u32[]{:S(2)}) %collective-permute-start.2) | collective-permute-done | bytes 147488 | tf_op jit(solution)/shard_map/ppermute | solution.py:388
  78.7 1.9 %partial.5 = (f32[256,640]{1,0:T(8,128)S(1)}, f32[256,640]{1,0:T(8,128)}) custom-call(bf16[256,2048]{1,0:T(8,128)(2,1)S(1)} %get-tuple-element.21.mine.hidden, bf16[256,2048]{1,0:T(8,128)(2,1)S(1)} %collective-permute-done.theirs, bf16[2,64,576]{2,1,0:T(8,128)(2,1)S(1)} %collective-permute-done.1.q0, bf16[2,64,576]{2,1,0:T(8,128)(2,1)S(1)} %collective-permute-done.2.q1, ...), custom_call_target="tpu_custom_call" | custom-call | flops 536870912 | bytes 2097152 | tf_op jit(solution)/shard_map/partial/pallas_call | solution.py:165
  80.6 5.0 %collective-permute-start.7 = (f32[256,640]{1,0:T(8,128)}, f32[256,640]{1,0:T(8,128)S(1)}, u32[]{:S(2)}, u32[]{:S(2)}) collective-permute-start(f32[256,640]{1,0:T(8,128)} %get-tuple-element.24), channel_id=1, source_target_pairs={{0,1},{1,0},{2,3},{3,2},{4,5},{5,4},{6,7},{7,6},{8,9},{9,8},{10,11... | collective-permute-start | bytes 1966088 | tf_op jit(solution)/shard_map/ppermute | solution.py:392
  86.3 5.2 %probs.1 = (bf16[4,1024,256]{2,1,0:T(8,128)(2,1)}, bf16[4,256,1024]{2,1,0:T(8,128)(2,1)}) custom-call(s32[1]{0:T(128)S(6)} %copy.15.length_ref, bf16[256,2048]{1,0:T(8,128)(2,1)} %q_ref.1, bf16[256,512]{1,0:T(8,128)(2,1)} %k_ref.1), custom_call_target="tpu_custom_call" | custom-call | flops 2147483648 | bytes 6291456 | tf_op jit(solution)/shard_map/probs/pallas_call | solution.py:56
  93.1 1.6 %copy-done.7 = bf16[4,256,1024]{2,1,0:T(8,128)(2,1)S(1)} copy-done((bf16[4,256,1024]{2,1,0:T(8,128)(2,1)S(1)}, bf16[4,256,1024]{2,1,0:T(8,128)(2,1)}, u32[]{:S(2)}) %copy-start.7) | copy-done | bytes 2097176
  94.7 3.2 %grads.1 = (f32[32,40,128]{2,1,0:T(8,128)S(1)}, bf16[64,256]{1,0:T(8,128)(2,1)S(1)}, f32[64,512]{1,0:T(8,128)S(1)}, f32[8,128]{1,0:T(8,128)S(1)}) custom-call(s32[1]{0:T(128)S(6)} %copy.15.length_ref, bf16[256,2048]{1,0:T(8,128)(2,1)} %get-tuple-element.22.hidden, f32[256,640]{1,0:T(8,128)S(1)} %get-tuple-element.23.before, ...), custom_call_target="tpu_custom_call" | custom-call | flops 4294967296 | bytes 10485760 | tf_op jit(solution)/shard_map/grads/pallas_call | solution.py:238
  97.9 1.9 %collective-permute-start.8 = (f32[32,40,128]{2,1,0:T(8,128)S(1)}, f32[32,40,128]{2,1,0:T(8,128)S(1)}, u32[]{:S(2)}, u32[]{:S(2)}) collective-permute-start(f32[32,40,128]{2,1,0:T(8,128)S(1)} %get-tuple-element.30), channel_id=1, source_target_pairs={{0,1},{1,0},{2,3},{3,2},{4,5},{5,4},{6,7},{7,6},{8,9},{9,8},{10,11... | collective-permute-start | bytes 1966088 | tf_op jit(solution)/shard_map/ppermute | solution.py:392
  100.3 1.6 %collective-permute-done.8.came = f32[32,40,128]{2,1,0:T(8,128)S(1)} collective-permute-done((f32[32,40,128]{2,1,0:T(8,128)S(1)}, f32[32,40,128]{2,1,0:T(8,128)S(1)}, u32[]{:S(2)}, u32[]{:S(2)}) %collective-permute-start.8) | collective-permute-done | bytes 655392 | tf_op jit(solution)/shard_map/ppermute | solution.py:392
  102.0 17.0 %all_to_all.20.pieces_ref = bf16[32,40,128]{2,1,0:T(8,128)(2,1)S(1)} all-to-all(bf16[32,40,128]{2,1,0:T(8,128)(2,1)S(1)} %merge.1), channel_id=1, replica_groups={{0,2,4,6,8,10,12,14,16,18,20,22,24,26,28,30,32,34,36,38,40,42,44,46,48,..., dimensions={0} | all-to-all | bytes 655360 | tf_op jit(solution)/shard_map/all_to_all | solution.py:431
  119.1 13.0 %all_to_all.21.pieces_ref = bf16[12,48,128]{2,1,0:T(8,128)(2,1)S(1)} all-to-all(bf16[12,48,128]{2,1,0:T(8,128)(2,1)S(1)} %fold.1), channel_id=1, replica_groups=mesh['dp'=12,'fsdp'=64] {'dp'}, dimensions={0} | all-to-all | bytes 294912 | tf_op jit(solution)/shard_map/all_to_all | solution.py:366
  132.9 18.0 %all_to_all.22.pieces_ref = bf16[64,4,128]{2,1,0:T(4,128)(2,1)S(1)} all-to-all(bf16[64,4,128]{2,1,0:T(4,128)(2,1)S(1)} %get-tuple-element.32), channel_id=1, replica_groups=mesh['dp'=12,'fsdp'=64] {'fsdp'}, dimensions={0} | all-to-all | bytes 131072 | tf_op jit(solution)/shard_map/all_to_all | solution.py:366
  (28 shorter events, 5.6 us)
Async XLA Ops:
  2.4 20.9 %all-to-all-start = ((bf16[8,64,576]{2,1,0:T(8,128)(2,1)}), bf16[8,64,576]{2,1,0:T(8,128)(2,1)S(1)}, u32[]{:S(2)}, u32[]{:S(2)}) async-start(bf16[8,64,576]{2,1,0:T(8,128)(2,1)} %pack.1), calls=%async_computation | async-start | bytes 1310720 | tf_op jit(solution)/shard_map/all_to_all | solution.py:410
  10.0 1.6 %copy-start.4 = (bf16[256,4096]{1,0:T(8,128)(2,1)S(1)}, bf16[256,4096]{1,0:T(8,128)(2,1)}, u32[]{:S(2)}) copy-start(bf16[256,4096]{1,0:T(8,128)(2,1)} %hidden.1) | copy-start | bytes 6291460
  13.8 58.9 %collective-permute-start = (bf16[256,2048]{1,0:T(8,128)(2,1)}, bf16[256,2048]{1,0:T(8,128)(2,1)S(1)}, u32[]{:S(2)}, u32[]{:S(2)}) collective-permute-start(bf16[256,2048]{1,0:T(8,128)(2,1)} %get-tuple-element.22.hidden), channel_id=1, source_target_pairs={{0,1},{1,0},{2,3},{3,2},{4,5},{5,4},{6,7},{7,6},{8,9},{9,8},{10,11... | collective-permute-start | bytes 3145736 | tf_op jit(solution)/shard_map/ppermute | solution.py:392
  23.3 51.9 %collective-permute-start.6 = (bf16[8,64,576]{2,1,0:T(8,128)(2,1)S(1)}, bf16[8,64,576]{2,1,0:T(8,128)(2,1)}, u32[]{:S(2)}, u32[]{:S(2)}) collective-permute-start(bf16[8,64,576]{2,1,0:T(8,128)(2,1)S(1)} %all-to-all-done.own), channel_id=1, source_target_pairs={{0,6},{1,7},{2,0},{3,1},{4,2},{5,3},{6,4},{7,5},{8,14},{9,15},{10,... | collective-permute-start | bytes 1769480 | tf_op jit(solution)/shard_map/ppermute | solution.py:379
  35.2 43.5 %collective-permute-start.5 = (bf16[8,64,576]{2,1,0:T(8,128)(2,1)S(1)}, bf16[8,64,576]{2,1,0:T(8,128)(2,1)S(1)}, u32[]{:S(2)}, u32[]{:S(2)}) collective-permute-start(bf16[8,64,576]{2,1,0:T(8,128)(2,1)S(1)} %all-to-all-done.own), channel_id=1, source_target_pairs={{0,2},{1,3},{2,4},{3,5},{4,6},{5,7},{6,0},{7,1},{8,10},{9,11},{10,... | collective-permute-start | bytes 1769480 | tf_op jit(solution)/shard_map/ppermute | solution.py:379
  37.1 19.3 %collective-permute-start.1 = (bf16[2,64,576]{2,1,0:T(8,128)(2,1)S(1)}, bf16[2,64,576]{2,1,0:T(8,128)(2,1)S(1)}, u32[]{:S(2)}, u32[]{:S(2)}) collective-permute-start(bf16[2,64,576]{2,1,0:T(8,128)(2,1)S(1)} %constant_dynamic-slice_fusion), channel_id=1, source_target_pairs={{0,4},{1,5},{2,6},{3,7},{4,0},{5,1},{6,2},{7,3},{8,12},{9,13},{10,... | collective-permute-start | bytes 442376 | tf_op jit(solution)/shard_map/ppermute | solution.py:379
  56.4 20.4 %collective-permute-start.4 = (bf16[2,64,576]{2,1,0:T(8,128)(2,1)S(1)}, bf16[2,64,576]{2,1,0:T(8,128)(2,1)S(1)}, u32[]{:S(2)}, u32[]{:S(2)}) collective-permute-start(bf16[2,64,576]{2,1,0:T(8,128)(2,1)S(1)} %collective-permute-done.1.q0), channel_id=1, source_target_pairs={{72,0},{73,1},{74,2},{75,3},{76,4},{77,5},{78,6},{79,7},{80,8},{81... | collective-permute-start | bytes 442376 | tf_op jit(solution)/shard_map/ppermute | solution.py:388
  59.3 17.6 %collective-permute-start.3 = (bf16[2,64,576]{2,1,0:T(8,128)(2,1)S(1)}, bf16[2,64,576]{2,1,0:T(8,128)(2,1)S(1)}, u32[]{:S(2)}, u32[]{:S(2)}) collective-permute-start(bf16[2,64,576]{2,1,0:T(8,128)(2,1)S(1)} %collective-permute-done.1.q0), channel_id=1, source_target_pairs={{64,0},{65,1},{66,2},{67,3},{68,4},{69,5},{70,6},{71,7},{72,8},{73... | collective-permute-start | bytes 442376 | tf_op jit(solution)/shard_map/ppermute | solution.py:388
  72.7 6.1 %collective-permute-start.2 = (bf16[2,64,576]{2,1,0:T(8,128)(2,1)S(1)}, bf16[2,64,576]{2,1,0:T(8,128)(2,1)S(1)}, u32[]{:S(2)}, u32[]{:S(2)}) collective-permute-start(bf16[2,64,576]{2,1,0:T(8,128)(2,1)S(1)} %collective-permute-done.1.q0), channel_id=1, source_target_pairs={{8,0},{9,1},{10,2},{11,3},{12,4},{13,5},{14,6},{15,7},{16,8},{17,9... | collective-permute-start | bytes 442376 | tf_op jit(solution)/shard_map/ppermute | solution.py:388
  80.6 10.9 %collective-permute-start.7 = (f32[256,640]{1,0:T(8,128)}, f32[256,640]{1,0:T(8,128)S(1)}, u32[]{:S(2)}, u32[]{:S(2)}) collective-permute-start(f32[256,640]{1,0:T(8,128)} %get-tuple-element.24), channel_id=1, source_target_pairs={{0,1},{1,0},{2,3},{3,2},{4,5},{5,4},{6,7},{7,6},{8,9},{9,8},{10,11... | collective-permute-start | bytes 1966088 | tf_op jit(solution)/shard_map/ppermute | solution.py:392
  86.2 5.2 %copy-start = (f32[64,512]{1,0:T(8,128)S(1)}, f32[64,512]{1,0:T(8,128)}, u32[]{:S(2)}) copy-start(f32[64,512]{1,0:T(8,128)} %up_ref.3) | copy-start | bytes 393220
  86.3 5.2 %copy-start.5 = (bf16[256,2048]{1,0:T(8,128)(2,1)S(1)}, bf16[256,2048]{1,0:T(8,128)(2,1)}, u32[]{:S(2)}) copy-start(bf16[256,2048]{1,0:T(8,128)(2,1)} %target.1) | copy-start | bytes 3145732
  91.5 1.6 %copy-start.6 = (bf16[4,1024,256]{2,1,0:T(8,128)(2,1)S(1)}, bf16[4,1024,256]{2,1,0:T(8,128)(2,1)}, u32[]{:S(2)}) copy-start(bf16[4,1024,256]{2,1,0:T(8,128)(2,1)} %get-tuple-element.25.probs) | copy-start | bytes 6291460
  93.1 1.6 %copy-start.7 = (bf16[4,256,1024]{2,1,0:T(8,128)(2,1)S(1)}, bf16[4,256,1024]{2,1,0:T(8,128)(2,1)}, u32[]{:S(2)}) copy-start(bf16[4,256,1024]{2,1,0:T(8,128)(2,1)} %get-tuple-element.26.probs_t) | copy-start | bytes 6291460
  97.9 4.0 %collective-permute-start.8 = (f32[32,40,128]{2,1,0:T(8,128)S(1)}, f32[32,40,128]{2,1,0:T(8,128)S(1)}, u32[]{:S(2)}, u32[]{:S(2)}) collective-permute-start(f32[32,40,128]{2,1,0:T(8,128)S(1)} %get-tuple-element.30), channel_id=1, source_target_pairs={{0,1},{1,0},{2,3},{3,2},{4,5},{5,4},{6,7},{7,6},{8,9},{9,8},{10,11... | collective-permute-start | bytes 1966088 | tf_op jit(solution)/shard_map/ppermute | solution.py:392
  99.8 32.3 %copy-start.2 = (f32[64,64]{1,0:T(8,128)S(1)}, f32[64,64]{1,0:T(8,128)}, u32[]{:S(2)}) copy-start(f32[64,64]{1,0:T(8,128)} %down_ref.3) | copy-start | bytes 49156
  99.8 32.3 %copy-start.3 = (f32[64,64]{1,0:T(8,128)S(1)}, f32[64,64]{1,0:T(8,128)}, u32[]{:S(2)}) copy-start(f32[64,64]{1,0:T(8,128)} %average_ref.2) | copy-start | bytes 49156
  100.2 50.7 %copy-start.1 = (f32[64,512]{1,0:T(8,128)S(1)}, f32[64,512]{1,0:T(8,128)}, u32[]{:S(2)}) copy-start(f32[64,512]{1,0:T(8,128)} %average_ref.3) | copy-start | bytes 393220

commit v8 on v7

--- a/solution.py
+++ b/solution.py
@@ -272,18 +272,16 @@
     )(hidden, latent_grad_t, up_term, sums)
 
 
-def halved(wide):
-    high = wide.astype(jnp.bfloat16)
-    return high, (wide - high.astype(jnp.float32)).astype(jnp.bfloat16)
+def rounded(rows):
+    row = lax.broadcasted_iota(jnp.int32, (8, HEAD_DIM), 0)
+    rest = rows - rows.astype(jnp.bfloat16).astype(jnp.float32)
+    return jnp.where(row == 5, pltpu.roll(rest, 1, 0), rows).astype(jnp.bfloat16)
 
 
 def merge_kernel(kept, came, out_ref):
-    row = lax.broadcasted_iota(jnp.int32, (8, HEAD_DIM), 0)
     for r in range(out_ref.shape[0]):
         out_ref[r, :32, :] = (kept[r, :32, :] + came[r, :32, :]).astype(jnp.bfloat16)
-        rows = kept[r, 32:, :] + came[r, 32:, :]
-        rest = rows - rows.astype(jnp.bfloat16).astype(jnp.float32)
-        out_ref[r, 32:, :] = jnp.where(row == 5, pltpu.roll(rest, 1, 0), rows).astype(jnp.bfloat16)
+        out_ref[r, 32:, :] = rounded(kept[r, 32:, :] + came[r, 32:, :])
 
 
 def merged(kept, came):
@@ -300,8 +298,7 @@
     row = lax.broadcasted_iota(jnp.int32, (8, HEAD_DIM), 0)
     tail = total[32:, :]
     tail = jnp.where(row == 4, tail + pltpu.roll(tail, 7, 0), tail)
-    high, low = halved(tail)
-    rows = jnp.concatenate([total[:32, :].astype(jnp.bfloat16), jnp.concatenate([high, low], axis=0)], axis=0)
+    rows = jnp.concatenate([total[:32, :].astype(jnp.bfloat16), rounded(tail)], axis=0)
     for d in range(out_ref.shape[0]):
         out_ref[d] = rows
 
@@ -309,7 +306,7 @@
 def fold(pieces, copies):
     return pl.pallas_call(
         fold_kernel,
-        out_shape=jax.ShapeDtypeStruct((copies, PIECE_ROWS + 8, HEAD_DIM), jnp.bfloat16),
+        out_shape=jax.ShapeDtypeStruct((copies, PIECE_ROWS, HEAD_DIM), jnp.bfloat16),
         compiler_params=SMALL,
         name="fold",
     )(pieces)
@@ -317,15 +314,15 @@
 
 def owner_kernel(pieces_ref, down_ref, average_ref, grad_ref, next_ref, up_ref, loss_ref):
     total = jnp.sum(pieces_ref[...].astype(jnp.float32), axis=0)
-    tail = total[32:40, :] + total[40:48, :]
-    count = tail[4:5, 1:2]
-    loss_ref[...] = tail[4:5, 0:1] / (2.0 * count)
+    sums = total[36:37, :] + total[37:38, :]
+    count = sums[:, 1:2]
+    loss_ref[...] = sums[:, 0:1] / (2.0 * count)
     factor = adapter_scale / count
     rows = jnp.concatenate([total[:32, :RANK], total[:32, RANK:]], axis=0)
     grad = jnp.transpose(rows) * factor
     grad_ref[...] = grad
     next_ref[...] = average_decay * average_ref[...] + (1.0 - average_decay) * (down_ref[...] - learning_rate * grad)
-    piece = (tail[:4, :] * factor).astype(jnp.bfloat16)
+    piece = (total[32:36, :] * factor).astype(jnp.bfloat16)
     for d in range(up_ref.shape[0]):
         up_ref[d] = piece
 

time: 153 us -> 152 us (level)
  no operation moved by 1% of the time
where the time goes in v8:
time: 152 us; the launch traced here: 151 us
  starting transfers between devices  58.4 us (38%)
  blocking collectives  47.7 us (31%)
  waiting for transfers between devices  20.3 us (13%)
  Pallas kernels  18.5 us (12%)
  local copies, waits for them, and re-layouts  4.82 us (3%)
    all_to_all x2, blocking collectives, exchange(): return lax.all_to_all(pieces, axis, 0, 0, tiled=True)  30.7 us
    ppermute x3, starting transfers between devices, from_neighbour(): return lax.ppermute(part, ('dp', 'fsdp'), moved)  18.1 us
    ppermute x3, starting transfers between devices, along_x(): return lax.ppermute(block, 'fsdp', moved)  17.4 us
    all_to_all x1, blocking collectives, per_device(): lax.all_to_all(merged(kept, came), 'fsdp', 0, 0, tiled=True, axis_index_g...  17 us
    ppermute x3, waiting for transfers between devices, along_x(): return lax.ppermute(block, 'fsdp', moved)  15.6 us
    ppermute x3, starting transfers between devices, from_other_core(): return lax.ppermute(block, 'fsdp', [(i, i ^ 1) for i in range(owners)])  15.2 us
    all_to_all x1, starting transfers between devices, per_device(): lax.all_to_all(shards, 'fsdp', 0, 0, tiled=True, axis_index_groups=along_...  7.64 us
    pallas_call x1, Pallas kernels, attention_probs(): pl.pallas_call(probs_kernel, grid=(KEY_VALUE_HEADS,), in_specs=[pl.BlockS...  5.2 us
  transfers between devices with their start and end apart: 10, of which 4 were waited for; matrix products, arithmetic and copies ran while one was open for 0% of the time, Pallas kernels for 7%

profile of v8, /device:TPU:1, one launch (start us, length us, event | category | flops | bytes accessed | tf_op | source)
XLA Modules:
  0.0 151.3 jit_solution(5063985516381844874)
XLA Ops:
  0.6 1.8 %pack.1 = bf16[8,64,576]{2,1,0:T(8,128)(2,1)} custom-call(bf16[64,512]{1,0:T(8,128)(2,1)} %value_ref.1, f32[64,64]{1,0:T(8,128)} %down_ref.3), custom_call_target="tpu_custom_call" | custom-call | tf_op jit(solution)/shard_map/pack/pallas_call | solution.py:86
  2.4 7.6 %all-to-all-start = ((bf16[8,64,576]{2,1,0:T(8,128)(2,1)}), bf16[8,64,576]{2,1,0:T(8,128)(2,1)S(1)}, u32[]{:S(2)}, u32[]{:S(2)}) async-start(bf16[8,64,576]{2,1,0:T(8,128)(2,1)} %pack.1), calls=%async_computation | async-start | bytes 1310720 | tf_op jit(solution)/shard_map/all_to_all | solution.py:407
  10.0 1.6 %copy-done.4 = bf16[256,4096]{1,0:T(8,128)(2,1)S(1)} copy-done((bf16[256,4096]{1,0:T(8,128)(2,1)S(1)}, bf16[256,4096]{1,0:T(8,128)(2,1)}, u32[]{:S(2)}) %copy-start.4) | copy-done | bytes 2097176
  11.6 2.2 %split.1 = (bf16[256,2048]{1,0:T(8,128)(2,1)S(1)}, bf16[256,2048]{1,0:T(8,128)(2,1)}) custom-call(bf16[256,4096]{1,0:T(8,128)(2,1)S(1)} %copy-done.4), custom_call_target="tpu_custom_call" | custom-call | flops 1073741824 | bytes 4194304 | tf_op jit(solution)/shard_map/split/pallas_call | solution.py:116
  13.8 8.3 %collective-permute-start = (bf16[256,2048]{1,0:T(8,128)(2,1)}, bf16[256,2048]{1,0:T(8,128)(2,1)S(1)}, u32[]{:S(2)}, u32[]{:S(2)}) collective-permute-start(bf16[256,2048]{1,0:T(8,128)(2,1)} %get-tuple-element.22.hidden), channel_id=1, source_target_pairs={{0,1},{1,0},{2,3},{3,2},{4,5},{5,4},{6,7},{7,6},{8,9},{9,8},{10,11... | collective-permute-start | bytes 3145736 | tf_op jit(solution)/shard_map/ppermute | solution.py:389
  23.3 11.9 %collective-permute-start.6 = (bf16[8,64,576]{2,1,0:T(8,128)(2,1)S(1)}, bf16[8,64,576]{2,1,0:T(8,128)(2,1)}, u32[]{:S(2)}, u32[]{:S(2)}) collective-permute-start(bf16[8,64,576]{2,1,0:T(8,128)(2,1)S(1)} %all-to-all-done.own), channel_id=1, source_target_pairs={{0,6},{1,7},{2,0},{3,1},{4,2},{5,3},{6,4},{7,5},{8,14},{9,15},{10,... | collective-permute-start | bytes 1769480 | tf_op jit(solution)/shard_map/ppermute | solution.py:376
  35.2 1.9 %collective-permute-start.5 = (bf16[8,64,576]{2,1,0:T(8,128)(2,1)S(1)}, bf16[8,64,576]{2,1,0:T(8,128)(2,1)S(1)}, u32[]{:S(2)}, u32[]{:S(2)}) collective-permute-start(bf16[8,64,576]{2,1,0:T(8,128)(2,1)S(1)} %all-to-all-done.own), channel_id=1, source_target_pairs={{0,2},{1,3},{2,4},{3,5},{4,6},{5,7},{6,0},{7,1},{8,10},{9,11},{10,... | collective-permute-start | bytes 1769480 | tf_op jit(solution)/shard_map/ppermute | solution.py:376
  37.1 3.6 %collective-permute-start.1 = (bf16[2,64,576]{2,1,0:T(8,128)(2,1)S(1)}, bf16[2,64,576]{2,1,0:T(8,128)(2,1)S(1)}, u32[]{:S(2)}, u32[]{:S(2)}) collective-permute-start(bf16[2,64,576]{2,1,0:T(8,128)(2,1)S(1)} %constant_dynamic-slice_fusion), channel_id=1, source_target_pairs={{0,4},{1,5},{2,6},{3,7},{4,0},{5,1},{6,2},{7,3},{8,12},{9,13},{10,... | collective-permute-start | bytes 442376 | tf_op jit(solution)/shard_map/ppermute | solution.py:376
  40.8 15.6 %collective-permute-done.1.q0 = bf16[2,64,576]{2,1,0:T(8,128)(2,1)S(1)} collective-permute-done((bf16[2,64,576]{2,1,0:T(8,128)(2,1)S(1)}, bf16[2,64,576]{2,1,0:T(8,128)(2,1)S(1)}, u32[]{:S(2)}, u32[]{:S(2)}) %collective-permute-start.1) | collective-permute-done | bytes 147488 | tf_op jit(solution)/shard_map/ppermute | solution.py:376
  56.4 2.8 %collective-permute-start.4 = (bf16[2,64,576]{2,1,0:T(8,128)(2,1)S(1)}, bf16[2,64,576]{2,1,0:T(8,128)(2,1)S(1)}, u32[]{:S(2)}, u32[]{:S(2)}) collective-permute-start(bf16[2,64,576]{2,1,0:T(8,128)(2,1)S(1)} %collective-permute-done.1.q0), channel_id=1, source_target_pairs={{72,0},{73,1},{74,2},{75,3},{76,4},{77,5},{78,6},{79,7},{80,8},{81... | collective-permute-start | bytes 442376 | tf_op jit(solution)/shard_map/ppermute | solution.py:385
  59.3 13.4 %collective-permute-start.3 = (bf16[2,64,576]{2,1,0:T(8,128)(2,1)S(1)}, bf16[2,64,576]{2,1,0:T(8,128)(2,1)S(1)}, u32[]{:S(2)}, u32[]{:S(2)}) collective-permute-start(bf16[2,64,576]{2,1,0:T(8,128)(2,1)S(1)} %collective-permute-done.1.q0), channel_id=1, source_target_pairs={{64,0},{65,1},{66,2},{67,3},{68,4},{69,5},{70,6},{71,7},{72,8},{73... | collective-permute-start | bytes 442376 | tf_op jit(solution)/shard_map/ppermute | solution.py:385
  72.7 1.9 %collective-permute-start.2 = (bf16[2,64,576]{2,1,0:T(8,128)(2,1)S(1)}, bf16[2,64,576]{2,1,0:T(8,128)(2,1)S(1)}, u32[]{:S(2)}, u32[]{:S(2)}) collective-permute-start(bf16[2,64,576]{2,1,0:T(8,128)(2,1)S(1)} %collective-permute-done.1.q0), channel_id=1, source_target_pairs={{8,0},{9,1},{10,2},{11,3},{12,4},{13,5},{14,6},{15,7},{16,8},{17,9... | collective-permute-start | bytes 442376 | tf_op jit(solution)/shard_map/ppermute | solution.py:385
  75.2 1.7 %partial.4.before = f32[2,256,576]{2,1,0:T(8,128)S(1)} custom-call(bf16[256,2048]{1,0:T(8,128)(2,1)S(1)} %get-tuple-element.21.mine.hidden, bf16[256,2048]{1,0:T(8,128)(2,1)S(1)} %collective-permute-done.theirs, bf16[8,64,576]{2,1,0:T(8,128)(2,1)} %collective-permute-done.6.far, f32[2,256,576]{2,1,0:T(8,128)S(1)} %partial.3.before), custom_call_target="tpu_custom_call" | custom-call | flops 536870912 | bytes 2097152 | tf_op jit(solution)/shard_map/partial/pallas_call | solution.py:165
  76.9 1.9 %collective-permute-done.2.q1 = bf16[2,64,576]{2,1,0:T(8,128)(2,1)S(1)} collective-permute-done((bf16[2,64,576]{2,1,0:T(8,128)(2,1)S(1)}, bf16[2,64,576]{2,1,0:T(8,128)(2,1)S(1)}, u32[]{:S(2)}, u32[]{:S(2)}) %collective-permute-start.2) | collective-permute-done | bytes 147488 | tf_op jit(solution)/shard_map/ppermute | solution.py:385
  78.7 1.9 %partial.5 = (f32[256,640]{1,0:T(8,128)S(1)}, f32[256,640]{1,0:T(8,128)}) custom-call(bf16[256,2048]{1,0:T(8,128)(2,1)S(1)} %get-tuple-element.21.mine.hidden, bf16[256,2048]{1,0:T(8,128)(2,1)S(1)} %collective-permute-done.theirs, bf16[2,64,576]{2,1,0:T(8,128)(2,1)S(1)} %collective-permute-done.1.q0, bf16[2,64,576]{2,1,0:T(8,128)(2,1)S(1)} %collective-permute-done.2.q1, ...), custom_call_target="tpu_custom_call" | custom-call | flops 536870912 | bytes 2097152 | tf_op jit(solution)/shard_map/partial/pallas_call | solution.py:165
  80.6 5.0 %collective-permute-start.7 = (f32[256,640]{1,0:T(8,128)}, f32[256,640]{1,0:T(8,128)S(1)}, u32[]{:S(2)}, u32[]{:S(2)}) collective-permute-start(f32[256,640]{1,0:T(8,128)} %get-tuple-element.24), channel_id=1, source_target_pairs={{0,1},{1,0},{2,3},{3,2},{4,5},{5,4},{6,7},{7,6},{8,9},{9,8},{10,11... | collective-permute-start | bytes 1966088 | tf_op jit(solution)/shard_map/ppermute | solution.py:389
  86.3 5.2 %probs.1 = (bf16[4,1024,256]{2,1,0:T(8,128)(2,1)}, bf16[4,256,1024]{2,1,0:T(8,128)(2,1)}) custom-call(s32[1]{0:T(128)S(6)} %copy.15.length_ref, bf16[256,2048]{1,0:T(8,128)(2,1)} %q_ref.1, bf16[256,512]{1,0:T(8,128)(2,1)} %k_ref.1), custom_call_target="tpu_custom_call" | custom-call | flops 2147483648 | bytes 6291456 | tf_op jit(solution)/shard_map/probs/pallas_call | solution.py:56
  93.1 1.6 %copy-done.7 = bf16[4,256,1024]{2,1,0:T(8,128)(2,1)S(1)} copy-done((bf16[4,256,1024]{2,1,0:T(8,128)(2,1)S(1)}, bf16[4,256,1024]{2,1,0:T(8,128)(2,1)}, u32[]{:S(2)}) %copy-start.7) | copy-done | bytes 2097176
  94.7 3.2 %grads.1 = (f32[32,40,128]{2,1,0:T(8,128)S(1)}, bf16[64,256]{1,0:T(8,128)(2,1)S(1)}, f32[64,512]{1,0:T(8,128)S(1)}, f32[8,128]{1,0:T(8,128)S(1)}) custom-call(s32[1]{0:T(128)S(6)} %copy.15.length_ref, bf16[256,2048]{1,0:T(8,128)(2,1)} %get-tuple-element.22.hidden, f32[256,640]{1,0:T(8,128)S(1)} %get-tuple-element.23.before, ...), custom_call_target="tpu_custom_call" | custom-call | flops 4294967296 | bytes 10485760 | tf_op jit(solution)/shard_map/grads/pallas_call | solution.py:238
  97.9 1.9 %collective-permute-start.8 = (f32[32,40,128]{2,1,0:T(8,128)S(1)}, f32[32,40,128]{2,1,0:T(8,128)S(1)}, u32[]{:S(2)}, u32[]{:S(2)}) collective-permute-start(f32[32,40,128]{2,1,0:T(8,128)S(1)} %get-tuple-element.30), channel_id=1, source_target_pairs={{0,1},{1,0},{2,3},{3,2},{4,5},{5,4},{6,7},{7,6},{8,9},{9,8},{10,11... | collective-permute-start | bytes 1966088 | tf_op jit(solution)/shard_map/ppermute | solution.py:389
  100.3 1.6 %collective-permute-done.8.came = f32[32,40,128]{2,1,0:T(8,128)S(1)} collective-permute-done((f32[32,40,128]{2,1,0:T(8,128)S(1)}, f32[32,40,128]{2,1,0:T(8,128)S(1)}, u32[]{:S(2)}, u32[]{:S(2)}) %collective-permute-start.8) | collective-permute-done | bytes 655392 | tf_op jit(solution)/shard_map/ppermute | solution.py:389
  102.0 17.0 %all_to_all.20.pieces_ref = bf16[32,40,128]{2,1,0:T(8,128)(2,1)S(1)} all-to-all(bf16[32,40,128]{2,1,0:T(8,128)(2,1)S(1)} %merge.1), channel_id=1, replica_groups={{0,2,4,6,8,10,12,14,16,18,20,22,24,26,28,30,32,34,36,38,40,42,44,46,48,..., dimensions={0} | all-to-all | bytes 655360 | tf_op jit(solution)/shard_map/all_to_all | solution.py:428
  119.1 13.0 %all_to_all.21.pieces_ref = bf16[12,40,128]{2,1,0:T(8,128)(2,1)S(1)} all-to-all(bf16[12,40,128]{2,1,0:T(8,128)(2,1)S(1)} %fold.1), channel_id=1, replica_groups=mesh['dp'=12,'fsdp'=64] {'dp'}, dimensions={0} | all-to-all | bytes 245760 | tf_op jit(solution)/shard_map/all_to_all | solution.py:363
  132.9 17.7 %all_to_all.22.pieces_ref = bf16[64,4,128]{2,1,0:T(4,128)(2,1)S(1)} all-to-all(bf16[64,4,128]{2,1,0:T(4,128)(2,1)S(1)} %get-tuple-element.32), channel_id=1, replica_groups=mesh['dp'=12,'fsdp'=64] {'fsdp'}, dimensions={0} | all-to-all | bytes 131072 | tf_op jit(solution)/shard_map/all_to_all | solution.py:363
  (28 shorter events, 5.6 us)
Async XLA Ops:
  2.4 20.9 %all-to-all-start = ((bf16[8,64,576]{2,1,0:T(8,128)(2,1)}), bf16[8,64,576]{2,1,0:T(8,128)(2,1)S(1)}, u32[]{:S(2)}, u32[]{:S(2)}) async-start(bf16[8,64,576]{2,1,0:T(8,128)(2,1)} %pack.1), calls=%async_computation | async-start | bytes 1310720 | tf_op jit(solution)/shard_map/all_to_all | solution.py:407
  10.0 1.6 %copy-start.4 = (bf16[256,4096]{1,0:T(8,128)(2,1)S(1)}, bf16[256,4096]{1,0:T(8,128)(2,1)}, u32[]{:S(2)}) copy-start(bf16[256,4096]{1,0:T(8,128)(2,1)} %hidden.1) | copy-start | bytes 6291460
  13.8 58.9 %collective-permute-start = (bf16[256,2048]{1,0:T(8,128)(2,1)}, bf16[256,2048]{1,0:T(8,128)(2,1)S(1)}, u32[]{:S(2)}, u32[]{:S(2)}) collective-permute-start(bf16[256,2048]{1,0:T(8,128)(2,1)} %get-tuple-element.22.hidden), channel_id=1, source_target_pairs={{0,1},{1,0},{2,3},{3,2},{4,5},{5,4},{6,7},{7,6},{8,9},{9,8},{10,11... | collective-permute-start | bytes 3145736 | tf_op jit(solution)/shard_map/ppermute | solution.py:389
  23.3 51.9 %collective-permute-start.6 = (bf16[8,64,576]{2,1,0:T(8,128)(2,1)S(1)}, bf16[8,64,576]{2,1,0:T(8,128)(2,1)}, u32[]{:S(2)}, u32[]{:S(2)}) collective-permute-start(bf16[8,64,576]{2,1,0:T(8,128)(2,1)S(1)} %all-to-all-done.own), channel_id=1, source_target_pairs={{0,6},{1,7},{2,0},{3,1},{4,2},{5,3},{6,4},{7,5},{8,14},{9,15},{10,... | collective-permute-start | bytes 1769480 | tf_op jit(solution)/shard_map/ppermute | solution.py:376
  35.2 43.5 %collective-permute-start.5 = (bf16[8,64,576]{2,1,0:T(8,128)(2,1)S(1)}, bf16[8,64,576]{2,1,0:T(8,128)(2,1)S(1)}, u32[]{:S(2)}, u32[]{:S(2)}) collective-permute-start(bf16[8,64,576]{2,1,0:T(8,128)(2,1)S(1)} %all-to-all-done.own), channel_id=1, source_target_pairs={{0,2},{1,3},{2,4},{3,5},{4,6},{5,7},{6,0},{7,1},{8,10},{9,11},{10,... | collective-permute-start | bytes 1769480 | tf_op jit(solution)/shard_map/ppermute | solution.py:376
  37.1 19.3 %collective-permute-start.1 = (bf16[2,64,576]{2,1,0:T(8,128)(2,1)S(1)}, bf16[2,64,576]{2,1,0:T(8,128)(2,1)S(1)}, u32[]{:S(2)}, u32[]{:S(2)}) collective-permute-start(bf16[2,64,576]{2,1,0:T(8,128)(2,1)S(1)} %constant_dynamic-slice_fusion), channel_id=1, source_target_pairs={{0,4},{1,5},{2,6},{3,7},{4,0},{5,1},{6,2},{7,3},{8,12},{9,13},{10,... | collective-permute-start | bytes 442376 | tf_op jit(solution)/shard_map/ppermute | solution.py:376
  56.4 20.4 %collective-permute-start.4 = (bf16[2,64,576]{2,1,0:T(8,128)(2,1)S(1)}, bf16[2,64,576]{2,1,0:T(8,128)(2,1)S(1)}, u32[]{:S(2)}, u32[]{:S(2)}) collective-permute-start(bf16[2,64,576]{2,1,0:T(8,128)(2,1)S(1)} %collective-permute-done.1.q0), channel_id=1, source_target_pairs={{72,0},{73,1},{74,2},{75,3},{76,4},{77,5},{78,6},{79,7},{80,8},{81... | collective-permute-start | bytes 442376 | tf_op jit(solution)/shard_map/ppermute | solution.py:385
  59.3 17.6 %collective-permute-start.3 = (bf16[2,64,576]{2,1,0:T(8,128)(2,1)S(1)}, bf16[2,64,576]{2,1,0:T(8,128)(2,1)S(1)}, u32[]{:S(2)}, u32[]{:S(2)}) collective-permute-start(bf16[2,64,576]{2,1,0:T(8,128)(2,1)S(1)} %collective-permute-done.1.q0), channel_id=1, source_target_pairs={{64,0},{65,1},{66,2},{67,3},{68,4},{69,5},{70,6},{71,7},{72,8},{73... | collective-permute-start | bytes 442376 | tf_op jit(solution)/shard_map/ppermute | solution.py:385
  72.7 6.1 %collective-permute-start.2 = (bf16[2,64,576]{2,1,0:T(8,128)(2,1)S(1)}, bf16[2,64,576]{2,1,0:T(8,128)(2,1)S(1)}, u32[]{:S(2)}, u32[]{:S(2)}) collective-permute-start(bf16[2,64,576]{2,1,0:T(8,128)(2,1)S(1)} %collective-permute-done.1.q0), channel_id=1, source_target_pairs={{8,0},{9,1},{10,2},{11,3},{12,4},{13,5},{14,6},{15,7},{16,8},{17,9... | collective-permute-start | bytes 442376 | tf_op jit(solution)/shard_map/ppermute | solution.py:385
  80.6 10.9 %collective-permute-start.7 = (f32[256,640]{1,0:T(8,128)}, f32[256,640]{1,0:T(8,128)S(1)}, u32[]{:S(2)}, u32[]{:S(2)}) collective-permute-start(f32[256,640]{1,0:T(8,128)} %get-tuple-element.24), channel_id=1, source_target_pairs={{0,1},{1,0},{2,3},{3,2},{4,5},{5,4},{6,7},{7,6},{8,9},{9,8},{10,11... | collective-permute-start | bytes 1966088 | tf_op jit(solution)/shard_map/ppermute | solution.py:389
  86.2 5.2 %copy-start = (f32[64,512]{1,0:T(8,128)S(1)}, f32[64,512]{1,0:T(8,128)}, u32[]{:S(2)}) copy-start(f32[64,512]{1,0:T(8,128)} %up_ref.3) | copy-start | bytes 393220
  86.3 5.2 %copy-start.5 = (bf16[256,2048]{1,0:T(8,128)(2,1)S(1)}, bf16[256,2048]{1,0:T(8,128)(2,1)}, u32[]{:S(2)}) copy-start(bf16[256,2048]{1,0:T(8,128)(2,1)} %target.1) | copy-start | bytes 3145732
  91.5 1.6 %copy-start.6 = (bf16[4,1024,256]{2,1,0:T(8,128)(2,1)S(1)}, bf16[4,1024,256]{2,1,0:T(8,128)(2,1)}, u32[]{:S(2)}) copy-start(bf16[4,1024,256]{2,1,0:T(8,128)(2,1)} %get-tuple-element.25.probs) | copy-start | bytes 6291460
  93.1 1.6 %copy-start.7 = (bf16[4,256,1024]{2,1,0:T(8,128)(2,1)S(1)}, bf16[4,256,1024]{2,1,0:T(8,128)(2,1)}, u32[]{:S(2)}) copy-start(bf16[4,256,1024]{2,1,0:T(8,128)(2,1)} %get-tuple-element.26.probs_t) | copy-start | bytes 6291460
  97.9 4.0 %collective-permute-start.8 = (f32[32,40,128]{2,1,0:T(8,128)S(1)}, f32[32,40,128]{2,1,0:T(8,128)S(1)}, u32[]{:S(2)}, u32[]{:S(2)}) collective-permute-start(f32[32,40,128]{2,1,0:T(8,128)S(1)} %get-tuple-element.30), channel_id=1, source_target_pairs={{0,1},{1,0},{2,3},{3,2},{4,5},{5,4},{6,7},{7,6},{8,9},{9,8},{10,11... | collective-permute-start | bytes 1966088 | tf_op jit(solution)/shard_map/ppermute | solution.py:389
  99.8 32.3 %copy-start.2 = (f32[64,64]{1,0:T(8,128)S(1)}, f32[64,64]{1,0:T(8,128)}, u32[]{:S(2)}) copy-start(f32[64,64]{1,0:T(8,128)} %down_ref.3) | copy-start | bytes 49156
  99.8 32.3 %copy-start.3 = (f32[64,64]{1,0:T(8,128)S(1)}, f32[64,64]{1,0:T(8,128)}, u32[]{:S(2)}) copy-start(f32[64,64]{1,0:T(8,128)} %average_ref.2) | copy-start | bytes 49156
  100.2 50.4 %copy-start.1 = (f32[64,512]{1,0:T(8,128)S(1)}, f32[64,512]{1,0:T(8,128)}, u32[]{:S(2)}) copy-start(f32[64,512]{1,0:T(8,128)} %average_ref.3) | copy-start | bytes 393220

commit v9 on v8

--- a/solution.py
+++ b/solution.py
@@ -151,10 +151,14 @@
         out[i] = block_product(tokens, (far,), 3) + before[i]
 
 
-def last_kernel(mine, theirs, q0, q1, q2, q3, near, before, own, other):
+def quarters_kernel(mine, theirs, q0, q1, q2, q3, before, out):
+    for i, tokens in enumerate((mine, theirs)):
+        out[i] = before[i] + block_product(tokens, (q0, q1, q2, q3), 2)
+
+
+def last_kernel(mine, theirs, near, before, own, other):
     for i, (tokens, out) in enumerate(((mine, own), (theirs, other))):
-        far = block_product(tokens, (q0, q1, q2, q3), 2)
-        out[:, :WIDTH] = (before[i] + far) + block_product(tokens, (near,), 1)
+        out[:, :WIDTH] = before[i] + block_product(tokens, (near,), 1)
         out[:, WIDTH:] = jnp.zeros((TOK, PADDED - WIDTH), jnp.float32)
 
 
@@ -416,9 +420,8 @@
     corner = from_neighbour(part, owners, replicas, 1, 1)
     total = partial_values(first_kernel, mine, theirs, own)
     total = partial_values(next_kernel, mine, theirs, far, total)
-    total, other = partial_values(
-        last_kernel, mine, theirs, part, beside, behind, corner, near, total
-    )
+    total = partial_values(quarters_kernel, mine, theirs, part, beside, behind, corner, total)
+    total, other = partial_values(last_kernel, mine, theirs, near, total)
     swapped = from_other_core(other, owners)
     pieces, latent_grad_t, up_term, sums = gradients(
         lengths, send, total, swapped, probs, probs_t, target, adapter_up_map

time: 152 us -> 152 us (level)
    pallas_call x3 -> x4, Pallas kernels: 4.1 us -> 4.27 us  [partial_values(): pl.pallas_call(body, in_specs=[vmem] * len(given), out_specs=[vmem, vmem]...]
where the time goes in v9:
time: 152 us
  starting transfers between devices  58.4 us (38%)
  blocking collectives  47.8 us (31%)
  waiting for transfers between devices  20.3 us (13%)
  Pallas kernels  18.7 us (12%)
  local copies, waits for them, and re-layouts  4.82 us (3%)
    all_to_all x2, blocking collectives, exchange(): return lax.all_to_all(pieces, axis, 0, 0, tiled=True)  30.7 us
    ppermute x3, starting transfers between devices, from_neighbour(): return lax.ppermute(part, ('dp', 'fsdp'), moved)  18.1 us
    ppermute x3, starting transfers between devices, along_x(): return lax.ppermute(block, 'fsdp', moved)  17.4 us
    all_to_all x1, blocking collectives, per_device(): lax.all_to_all(merged(kept, came), 'fsdp', 0, 0, tiled=True, axis_index_g...  17 us
    ppermute x3, waiting for transfers between devices, along_x(): return lax.ppermute(block, 'fsdp', moved)  15.6 us
    ppermute x3, starting transfers between devices, from_other_core(): return lax.ppermute(block, 'fsdp', [(i, i ^ 1) for i in range(owners)])  15.2 us
    all_to_all x1, starting transfers between devices, per_device(): lax.all_to_all(shards, 'fsdp', 0, 0, tiled=True, axis_index_groups=along_...  7.64 us
    pallas_call x1, Pallas kernels, attention_probs(): pl.pallas_call(probs_kernel, grid=(KEY_VALUE_HEADS,), in_specs=[pl.BlockS...  5.2 us
  transfers between devices with their start and end apart: 10, of which 4 were waited for; matrix products, arithmetic and copies ran while one was open for 0% of the time, Pallas kernels for 7%

profile of v9, /device:TPU:1, one launch (start us, length us, event | category | flops | bytes accessed | tf_op | source)
XLA Modules:
  0.0 151.5 jit_solution(5456666844156664633)
XLA Ops:
  0.6 1.8 %pack.1 = bf16[8,64,576]{2,1,0:T(8,128)(2,1)} custom-call(bf16[64,512]{1,0:T(8,128)(2,1)} %value_ref.1, f32[64,64]{1,0:T(8,128)} %down_ref.3), custom_call_target="tpu_custom_call" | custom-call | tf_op jit(solution)/shard_map/pack/pallas_call | solution.py:86
  2.4 7.6 %all-to-all-start = ((bf16[8,64,576]{2,1,0:T(8,128)(2,1)}), bf16[8,64,576]{2,1,0:T(8,128)(2,1)S(1)}, u32[]{:S(2)}, u32[]{:S(2)}) async-start(bf16[8,64,576]{2,1,0:T(8,128)(2,1)} %pack.1), calls=%async_computation | async-start | bytes 1310720 | tf_op jit(solution)/shard_map/all_to_all | solution.py:411
  10.0 1.6 %copy-done.4 = bf16[256,4096]{1,0:T(8,128)(2,1)S(1)} copy-done((bf16[256,4096]{1,0:T(8,128)(2,1)S(1)}, bf16[256,4096]{1,0:T(8,128)(2,1)}, u32[]{:S(2)}) %copy-start.4) | copy-done | bytes 2097176
  11.6 2.2 %split.1 = (bf16[256,2048]{1,0:T(8,128)(2,1)S(1)}, bf16[256,2048]{1,0:T(8,128)(2,1)}) custom-call(bf16[256,4096]{1,0:T(8,128)(2,1)S(1)} %copy-done.4), custom_call_target="tpu_custom_call" | custom-call | flops 1073741824 | bytes 4194304 | tf_op jit(solution)/shard_map/split/pallas_call | solution.py:116
  13.8 8.3 %collective-permute-start = (bf16[256,2048]{1,0:T(8,128)(2,1)}, bf16[256,2048]{1,0:T(8,128)(2,1)S(1)}, u32[]{:S(2)}, u32[]{:S(2)}) collective-permute-start(bf16[256,2048]{1,0:T(8,128)(2,1)} %get-tuple-element.22.hidden), channel_id=1, source_target_pairs={{0,1},{1,0},{2,3},{3,2},{4,5},{5,4},{6,7},{7,6},{8,9},{9,8},{10,11... | collective-permute-start | bytes 3145736 | tf_op jit(solution)/shard_map/ppermute | solution.py:393
  23.3 11.9 %collective-permute-start.6 = (bf16[8,64,576]{2,1,0:T(8,128)(2,1)S(1)}, bf16[8,64,576]{2,1,0:T(8,128)(2,1)}, u32[]{:S(2)}, u32[]{:S(2)}) collective-permute-start(bf16[8,64,576]{2,1,0:T(8,128)(2,1)S(1)} %all-to-all-done.own), channel_id=1, source_target_pairs={{0,6},{1,7},{2,0},{3,1},{4,2},{5,3},{6,4},{7,5},{8,14},{9,15},{10,... | collective-permute-start | bytes 1769480 | tf_op jit(solution)/shard_map/ppermute | solution.py:380
  35.2 1.9 %collective-permute-start.1 = (bf16[8,64,576]{2,1,0:T(8,128)(2,1)S(1)}, bf16[8,64,576]{2,1,0:T(8,128)(2,1)S(1)}, u32[]{:S(2)}, u32[]{:S(2)}) collective-permute-start(bf16[8,64,576]{2,1,0:T(8,128)(2,1)S(1)} %all-to-all-done.own), channel_id=1, source_target_pairs={{0,2},{1,3},{2,4},{3,5},{4,6},{5,7},{6,0},{7,1},{8,10},{9,11},{10,... | collective-permute-start | bytes 1769480 | tf_op jit(solution)/shard_map/ppermute | solution.py:380
  37.1 3.6 %collective-permute-start.2 = (bf16[2,64,576]{2,1,0:T(8,128)(2,1)S(1)}, bf16[2,64,576]{2,1,0:T(8,128)(2,1)S(1)}, u32[]{:S(2)}, u32[]{:S(2)}) collective-permute-start(bf16[2,64,576]{2,1,0:T(8,128)(2,1)S(1)} %constant_dynamic-slice_fusion), channel_id=1, source_target_pairs={{0,4},{1,5},{2,6},{3,7},{4,0},{5,1},{6,2},{7,3},{8,12},{9,13},{10,... | collective-permute-start | bytes 442376 | tf_op jit(solution)/shard_map/ppermute | solution.py:380
  40.8 15.6 %collective-permute-done.2.q0 = bf16[2,64,576]{2,1,0:T(8,128)(2,1)S(1)} collective-permute-done((bf16[2,64,576]{2,1,0:T(8,128)(2,1)S(1)}, bf16[2,64,576]{2,1,0:T(8,128)(2,1)S(1)}, u32[]{:S(2)}, u32[]{:S(2)}) %collective-permute-start.2) | collective-permute-done | bytes 147488 | tf_op jit(solution)/shard_map/ppermute | solution.py:380
  56.4 2.8 %collective-permute-start.5 = (bf16[2,64,576]{2,1,0:T(8,128)(2,1)S(1)}, bf16[2,64,576]{2,1,0:T(8,128)(2,1)S(1)}, u32[]{:S(2)}, u32[]{:S(2)}) collective-permute-start(bf16[2,64,576]{2,1,0:T(8,128)(2,1)S(1)} %collective-permute-done.2.q0), channel_id=1, source_target_pairs={{72,0},{73,1},{74,2},{75,3},{76,4},{77,5},{78,6},{79,7},{80,8},{81... | collective-permute-start | bytes 442376 | tf_op jit(solution)/shard_map/ppermute | solution.py:389
  59.3 13.4 %collective-permute-start.4 = (bf16[2,64,576]{2,1,0:T(8,128)(2,1)S(1)}, bf16[2,64,576]{2,1,0:T(8,128)(2,1)S(1)}, u32[]{:S(2)}, u32[]{:S(2)}) collective-permute-start(bf16[2,64,576]{2,1,0:T(8,128)(2,1)S(1)} %collective-permute-done.2.q0), channel_id=1, source_target_pairs={{64,0},{65,1},{66,2},{67,3},{68,4},{69,5},{70,6},{71,7},{72,8},{73... | collective-permute-start | bytes 442376 | tf_op jit(solution)/shard_map/ppermute | solution.py:389
  72.7 1.9 %collective-permute-start.3 = (bf16[2,64,576]{2,1,0:T(8,128)(2,1)S(1)}, bf16[2,64,576]{2,1,0:T(8,128)(2,1)S(1)}, u32[]{:S(2)}, u32[]{:S(2)}) collective-permute-start(bf16[2,64,576]{2,1,0:T(8,128)(2,1)S(1)} %collective-permute-done.2.q0), channel_id=1, source_target_pairs={{8,0},{9,1},{10,2},{11,3},{12,4},{13,5},{14,6},{15,7},{16,8},{17,9... | collective-permute-start | bytes 442376 | tf_op jit(solution)/shard_map/ppermute | solution.py:389
  75.2 1.7 %partial.5.before = f32[2,256,576]{2,1,0:T(8,128)S(1)} custom-call(bf16[256,2048]{1,0:T(8,128)(2,1)S(1)} %get-tuple-element.21.mine.hidden, bf16[256,2048]{1,0:T(8,128)(2,1)S(1)} %collective-permute-done.theirs, bf16[8,64,576]{2,1,0:T(8,128)(2,1)} %collective-permute-done.6.far, f32[2,256,576]{2,1,0:T(8,128)S(1)} %partial.4.before), custom_call_target="tpu_custom_call" | custom-call | flops 536870912 | bytes 2097152 | tf_op jit(solution)/shard_map/partial/pallas_call | solution.py:169
  76.9 1.9 %collective-permute-done.3.q1 = bf16[2,64,576]{2,1,0:T(8,128)(2,1)S(1)} collective-permute-done((bf16[2,64,576]{2,1,0:T(8,128)(2,1)S(1)}, bf16[2,64,576]{2,1,0:T(8,128)(2,1)S(1)}, u32[]{:S(2)}, u32[]{:S(2)}) %collective-permute-start.3) | collective-permute-done | bytes 147488 | tf_op jit(solution)/shard_map/ppermute | solution.py:389
  80.8 5.0 %collective-permute-start.7 = (f32[256,640]{1,0:T(8,128)}, f32[256,640]{1,0:T(8,128)S(1)}, u32[]{:S(2)}, u32[]{:S(2)}) collective-permute-start(f32[256,640]{1,0:T(8,128)} %get-tuple-element.24), channel_id=1, source_target_pairs={{0,1},{1,0},{2,3},{3,2},{4,5},{5,4},{6,7},{7,6},{8,9},{9,8},{10,11... | collective-permute-start | bytes 1966088 | tf_op jit(solution)/shard_map/ppermute | solution.py:393
  86.5 5.2 %probs.1 = (bf16[4,1024,256]{2,1,0:T(8,128)(2,1)}, bf16[4,256,1024]{2,1,0:T(8,128)(2,1)}) custom-call(s32[1]{0:T(128)S(6)} %copy.15.length_ref, bf16[256,2048]{1,0:T(8,128)(2,1)} %q_ref.1, bf16[256,512]{1,0:T(8,128)(2,1)} %k_ref.1), custom_call_target="tpu_custom_call" | custom-call | flops 2147483648 | bytes 6291456 | tf_op jit(solution)/shard_map/probs/pallas_call | solution.py:56
  91.7 1.6 %copy-done.6 = bf16[4,1024,256]{2,1,0:T(8,128)(2,1)S(1)} copy-done((bf16[4,1024,256]{2,1,0:T(8,128)(2,1)S(1)}, bf16[4,1024,256]{2,1,0:T(8,128)(2,1)}, u32[]{:S(2)}) %copy-start.6) | copy-done | bytes 2097176
  93.3 1.6 %copy-done.7 = bf16[4,256,1024]{2,1,0:T(8,128)(2,1)S(1)} copy-done((bf16[4,256,1024]{2,1,0:T(8,128)(2,1)S(1)}, bf16[4,256,1024]{2,1,0:T(8,128)(2,1)}, u32[]{:S(2)}) %copy-start.7) | copy-done | bytes 2097176
  94.9 3.2 %grads.1 = (f32[32,40,128]{2,1,0:T(8,128)S(1)}, bf16[64,256]{1,0:T(8,128)(2,1)S(1)}, f32[64,512]{1,0:T(8,128)S(1)}, f32[8,128]{1,0:T(8,128)S(1)}) custom-call(s32[1]{0:T(128)S(6)} %copy.15.length_ref, bf16[256,2048]{1,0:T(8,128)(2,1)} %get-tuple-element.22.hidden, f32[256,640]{1,0:T(8,128)S(1)} %get-tuple-element.23.before, ...), custom_call_target="tpu_custom_call" | custom-call | flops 4294967296 | bytes 10485760 | tf_op jit(solution)/shard_map/grads/pallas_call | solution.py:242
  98.1 1.9 %collective-permute-start.8 = (f32[32,40,128]{2,1,0:T(8,128)S(1)}, f32[32,40,128]{2,1,0:T(8,128)S(1)}, u32[]{:S(2)}, u32[]{:S(2)}) collective-permute-start(f32[32,40,128]{2,1,0:T(8,128)S(1)} %get-tuple-element.30), channel_id=1, source_target_pairs={{0,1},{1,0},{2,3},{3,2},{4,5},{5,4},{6,7},{7,6},{8,9},{9,8},{10,11... | collective-permute-start | bytes 1966088 | tf_op jit(solution)/shard_map/ppermute | solution.py:393
  100.4 1.6 %collective-permute-done.8.came = f32[32,40,128]{2,1,0:T(8,128)S(1)} collective-permute-done((f32[32,40,128]{2,1,0:T(8,128)S(1)}, f32[32,40,128]{2,1,0:T(8,128)S(1)}, u32[]{:S(2)}, u32[]{:S(2)}) %collective-permute-start.8) | collective-permute-done | bytes 655392 | tf_op jit(solution)/shard_map/ppermute | solution.py:393
  102.2 17.0 %all_to_all.20.pieces_ref = bf16[32,40,128]{2,1,0:T(8,128)(2,1)S(1)} all-to-all(bf16[32,40,128]{2,1,0:T(8,128)(2,1)S(1)} %merge.1), channel_id=1, replica_groups={{0,2,4,6,8,10,12,14,16,18,20,22,24,26,28,30,32,34,36,38,40,42,44,46,48,..., dimensions={0} | all-to-all | bytes 655360 | tf_op jit(solution)/shard_map/all_to_all | solution.py:431
  119.3 13.0 %all_to_all.21.pieces_ref = bf16[12,40,128]{2,1,0:T(8,128)(2,1)S(1)} all-to-all(bf16[12,40,128]{2,1,0:T(8,128)(2,1)S(1)} %fold.1), channel_id=1, replica_groups=mesh['dp'=12,'fsdp'=64] {'dp'}, dimensions={0} | all-to-all | bytes 245760 | tf_op jit(solution)/shard_map/all_to_all | solution.py:367
  133.1 17.7 %all_to_all.22.pieces_ref = bf16[64,4,128]{2,1,0:T(4,128)(2,1)S(1)} all-to-all(bf16[64,4,128]{2,1,0:T(4,128)(2,1)S(1)} %get-tuple-element.32), channel_id=1, replica_groups=mesh['dp'=12,'fsdp'=64] {'fsdp'}, dimensions={0} | all-to-all | bytes 131072 | tf_op jit(solution)/shard_map/all_to_all | solution.py:367
  (29 shorter events, 6.0 us)
Async XLA Ops:
  2.4 20.9 %all-to-all-start = ((bf16[8,64,576]{2,1,0:T(8,128)(2,1)}), bf16[8,64,576]{2,1,0:T(8,128)(2,1)S(1)}, u32[]{:S(2)}, u32[]{:S(2)}) async-start(bf16[8,64,576]{2,1,0:T(8,128)(2,1)} %pack.1), calls=%async_computation | async-start | bytes 1310720 | tf_op jit(solution)/shard_map/all_to_all | solution.py:411
  10.0 1.6 %copy-start.4 = (bf16[256,4096]{1,0:T(8,128)(2,1)S(1)}, bf16[256,4096]{1,0:T(8,128)(2,1)}, u32[]{:S(2)}) copy-start(bf16[256,4096]{1,0:T(8,128)(2,1)} %hidden.1) | copy-start | bytes 6291460
  13.8 58.9 %collective-permute-start = (bf16[256,2048]{1,0:T(8,128)(2,1)}, bf16[256,2048]{1,0:T(8,128)(2,1)S(1)}, u32[]{:S(2)}, u32[]{:S(2)}) collective-permute-start(bf16[256,2048]{1,0:T(8,128)(2,1)} %get-tuple-element.22.hidden), channel_id=1, source_target_pairs={{0,1},{1,0},{2,3},{3,2},{4,5},{5,4},{6,7},{7,6},{8,9},{9,8},{10,11... | collective-permute-start | bytes 3145736 | tf_op jit(solution)/shard_map/ppermute | solution.py:393
  23.3 51.9 %collective-permute-start.6 = (bf16[8,64,576]{2,1,0:T(8,128)(2,1)S(1)}, bf16[8,64,576]{2,1,0:T(8,128)(2,1)}, u32[]{:S(2)}, u32[]{:S(2)}) collective-permute-start(bf16[8,64,576]{2,1,0:T(8,128)(2,1)S(1)} %all-to-all-done.own), channel_id=1, source_target_pairs={{0,6},{1,7},{2,0},{3,1},{4,2},{5,3},{6,4},{7,5},{8,14},{9,15},{10,... | collective-permute-start | bytes 1769480 | tf_op jit(solution)/shard_map/ppermute | solution.py:380
  35.2 44.1 %collective-permute-start.1 = (bf16[8,64,576]{2,1,0:T(8,128)(2,1)S(1)}, bf16[8,64,576]{2,1,0:T(8,128)(2,1)S(1)}, u32[]{:S(2)}, u32[]{:S(2)}) collective-permute-start(bf16[8,64,576]{2,1,0:T(8,128)(2,1)S(1)} %all-to-all-done.own), channel_id=1, source_target_pairs={{0,2},{1,3},{2,4},{3,5},{4,6},{5,7},{6,0},{7,1},{8,10},{9,11},{10,... | collective-permute-start | bytes 1769480 | tf_op jit(solution)/shard_map/ppermute | solution.py:380
  37.1 19.3 %collective-permute-start.2 = (bf16[2,64,576]{2,1,0:T(8,128)(2,1)S(1)}, bf16[2,64,576]{2,1,0:T(8,128)(2,1)S(1)}, u32[]{:S(2)}, u32[]{:S(2)}) collective-permute-start(bf16[2,64,576]{2,1,0:T(8,128)(2,1)S(1)} %constant_dynamic-slice_fusion), channel_id=1, source_target_pairs={{0,4},{1,5},{2,6},{3,7},{4,0},{5,1},{6,2},{7,3},{8,12},{9,13},{10,... | collective-permute-start | bytes 442376 | tf_op jit(solution)/shard_map/ppermute | solution.py:380
  56.4 20.4 %collective-permute-start.5 = (bf16[2,64,576]{2,1,0:T(8,128)(2,1)S(1)}, bf16[2,64,576]{2,1,0:T(8,128)(2,1)S(1)}, u32[]{:S(2)}, u32[]{:S(2)}) collective-permute-start(bf16[2,64,576]{2,1,0:T(8,128)(2,1)S(1)} %collective-permute-done.2.q0), channel_id=1, source_target_pairs={{72,0},{73,1},{74,2},{75,3},{76,4},{77,5},{78,6},{79,7},{80,8},{81... | collective-permute-start | bytes 442376 | tf_op jit(solution)/shard_map/ppermute | solution.py:389
  59.3 17.6 %collective-permute-start.4 = (bf16[2,64,576]{2,1,0:T(8,128)(2,1)S(1)}, bf16[2,64,576]{2,1,0:T(8,128)(2,1)S(1)}, u32[]{:S(2)}, u32[]{:S(2)}) collective-permute-start(bf16[2,64,576]{2,1,0:T(8,128)(2,1)S(1)} %collective-permute-done.2.q0), channel_id=1, source_target_pairs={{64,0},{65,1},{66,2},{67,3},{68,4},{69,5},{70,6},{71,7},{72,8},{73... | collective-permute-start | bytes 442376 | tf_op jit(solution)/shard_map/ppermute | solution.py:389
  72.7 6.1 %collective-permute-start.3 = (bf16[2,64,576]{2,1,0:T(8,128)(2,1)S(1)}, bf16[2,64,576]{2,1,0:T(8,128)(2,1)S(1)}, u32[]{:S(2)}, u32[]{:S(2)}) collective-permute-start(bf16[2,64,576]{2,1,0:T(8,128)(2,1)S(1)} %collective-permute-done.2.q0), channel_id=1, source_target_pairs={{8,0},{9,1},{10,2},{11,3},{12,4},{13,5},{14,6},{15,7},{16,8},{17,9... | collective-permute-start | bytes 442376 | tf_op jit(solution)/shard_map/ppermute | solution.py:389
  80.8 10.9 %collective-permute-start.7 = (f32[256,640]{1,0:T(8,128)}, f32[256,640]{1,0:T(8,128)S(1)}, u32[]{:S(2)}, u32[]{:S(2)}) collective-permute-start(f32[256,640]{1,0:T(8,128)} %get-tuple-element.24), channel_id=1, source_target_pairs={{0,1},{1,0},{2,3},{3,2},{4,5},{5,4},{6,7},{7,6},{8,9},{9,8},{10,11... | collective-permute-start | bytes 1966088 | tf_op jit(solution)/shard_map/ppermute | solution.py:393
  86.4 5.2 %copy-start = (f32[64,512]{1,0:T(8,128)S(1)}, f32[64,512]{1,0:T(8,128)}, u32[]{:S(2)}) copy-start(f32[64,512]{1,0:T(8,128)} %up_ref.3) | copy-start | bytes 393220
  86.4 5.2 %copy-start.5 = (bf16[256,2048]{1,0:T(8,128)(2,1)S(1)}, bf16[256,2048]{1,0:T(8,128)(2,1)}, u32[]{:S(2)}) copy-start(bf16[256,2048]{1,0:T(8,128)(2,1)} %target.1) | copy-start | bytes 3145732
  91.7 1.6 %copy-start.6 = (bf16[4,1024,256]{2,1,0:T(8,128)(2,1)S(1)}, bf16[4,1024,256]{2,1,0:T(8,128)(2,1)}, u32[]{:S(2)}) copy-start(bf16[4,1024,256]{2,1,0:T(8,128)(2,1)} %get-tuple-element.25.probs) | copy-start | bytes 6291460
  93.3 1.6 %copy-start.7 = (bf16[4,256,1024]{2,1,0:T(8,128)(2,1)S(1)}, bf16[4,256,1024]{2,1,0:T(8,128)(2,1)}, u32[]{:S(2)}) copy-start(bf16[4,256,1024]{2,1,0:T(8,128)(2,1)} %get-tuple-element.26.probs_t) | copy-start | bytes 6291460
  98.1 4.0 %collective-permute-start.8 = (f32[32,40,128]{2,1,0:T(8,128)S(1)}, f32[32,40,128]{2,1,0:T(8,128)S(1)}, u32[]{:S(2)}, u32[]{:S(2)}) collective-permute-start(f32[32,40,128]{2,1,0:T(8,128)S(1)} %get-tuple-element.30), channel_id=1, source_target_pairs={{0,1},{1,0},{2,3},{3,2},{4,5},{5,4},{6,7},{7,6},{8,9},{9,8},{10,11... | collective-permute-start | bytes 1966088 | tf_op jit(solution)/shard_map/ppermute | solution.py:393
  100.0 32.3 %copy-start.2 = (f32[64,64]{1,0:T(8,128)S(1)}, f32[64,64]{1,0:T(8,128)}, u32[]{:S(2)}) copy-start(f32[64,64]{1,0:T(8,128)} %down_ref.3) | copy-start | bytes 49156
  100.0 32.3 %copy-start.3 = (f32[64,64]{1,0:T(8,128)S(1)}, f32[64,64]{1,0:T(8,128)}, u32[]{:S(2)}) copy-start(f32[64,64]{1,0:T(8,128)} %average_ref.2) | copy-start | bytes 49156
  100.4 50.4 %copy-start.1 = (f32[64,512]{1,0:T(8,128)S(1)}, f32[64,512]{1,0:T(8,128)}, u32[]{:S(2)}) copy-start(f32[64,512]{1,0:T(8,128)} %average_ref.3) | copy-start | bytes 393220
